TPU v7x, 8 devices: a whole 2x2x1 slice. The times are simulated.
8 devices in a mesh: dp: 1 (over z), ei: 2 (over y), eo: 4 (over x, core).
Axes of the slice: x: 2, y: 2, z: 1, core: 2. Of those that a mesh axis runs over, the one named last changes fastest.
Arguments:
- x_tokens: bfloat16 [512, 1024], P(('dp', 'ei', 'eo'))
- expert_idx: int32 [512, 8], P(('dp', 'ei', 'eo'))
- gate_vals: float32 [512, 8], P(('dp', 'ei', 'eo'))
- dy_tokens: bfloat16 [512, 1024], P(('dp', 'ei', 'eo'))
- w_gate: bfloat16 [32, 1024, 512], P(('ei', 'eo'))
- w_up: bfloat16 [32, 1024, 512], P(('ei', 'eo'))
- w_down: bfloat16 [32, 512, 1024], P(('ei', 'eo'))
- x_attn: bfloat16 [8, 64, 1024], P(('dp', 'ei', 'eo'))
- w_query: bfloat16 [1024, 16, 64], P(None, ('ei', 'eo'))
- w_key: bfloat16 [1024, 8, 64], P(None, ('ei', 'eo'))
- w_value: bfloat16 [1024, 8, 64], P(None, ('ei', 'eo'))
- w_out: bfloat16 [16, 64, 1024], P(('ei', 'eo'))
Outputs:
- output 1: bfloat16 [512, 1024], P(('dp', 'ei', 'eo'))
- output 2: bfloat16 [512, 1024], P(('dp', 'ei', 'eo'))
- output 3: float32 [512, 8], P(('dp', 'ei', 'eo'))
- output 4: float32 [32, 1024, 512], P(('dp', 'ei', 'eo'))
- output 5: float32 [32, 1024, 512], P(('dp', 'ei', 'eo'))
- output 6: float32 [32, 512, 1024], P(('dp', 'ei', 'eo'))
- output 7: bfloat16 [8, 64, 1024], P(('dp', 'ei', 'eo'))
All inputs are finite; a program needn't handle non-finite values.
Results may differ from a plain program's by a relative error of at most 0.0135428.
Values are sent between devices in bfloat16 or wider.
A program may use at most 1 GiB of HBM per device.

v0:
```python
import jax
import jax.numpy as jnp
from jax import lax
from jax.sharding import PartitionSpec as P

CAP_MULT = 4
GROUP_AXES = ('ei', 'eo')
TOKEN_AXES = ('dp', 'ei', 'eo')


def slot_plan(flat_exp, num_exp, cap_rows):
    num_asg = flat_exp.shape[0]
    onehot = (flat_exp[:, None] == jnp.arange(num_exp, dtype=jnp.int32)[None, :]).astype(jnp.int32)
    ranks = jnp.sum((jnp.cumsum(onehot, axis=0) - 1) * onehot, axis=1)
    dest_slot = flat_exp * cap_rows + ranks
    slot_owner = jnp.full((num_exp * cap_rows,), num_asg, jnp.int32).at[dest_slot].set(jnp.arange(num_asg, dtype=jnp.int32))
    return dest_slot, slot_owner


def expert_forward(x_slots, w_gate, w_up, w_down):
    pre_gate = jnp.einsum('secd,edf->secf', x_slots, w_gate, preferred_element_type=jnp.float32)
    pre_up = jnp.einsum('secd,edf->secf', x_slots, w_up, preferred_element_type=jnp.float32)
    sigmoid_g = jax.nn.sigmoid(pre_gate)
    act_gate = pre_gate * sigmoid_g
    hidden = (act_gate * pre_up).astype(jnp.bfloat16)
    out_slots = jnp.einsum('secf,efd->secd', hidden, w_down, preferred_element_type=jnp.float32).astype(jnp.bfloat16)
    return out_slots, (pre_gate, pre_up, sigmoid_g, act_gate, hidden)


def expert_backward(x_slots, d_out, saved, w_gate, w_up, w_down):
    pre_gate, pre_up, sigmoid_g, act_gate, hidden = saved
    d_hidden = jnp.einsum('secd,efd->secf', d_out, w_down, preferred_element_type=jnp.float32).astype(jnp.bfloat16).astype(jnp.float32)
    d_pre_gate = (d_hidden * pre_up * sigmoid_g * (1.0 + pre_gate * (1.0 - sigmoid_g))).astype(jnp.bfloat16)
    d_pre_up = (d_hidden * act_gate).astype(jnp.bfloat16)
    dw_gate = jnp.einsum('secd,secf->edf', x_slots, d_pre_gate, preferred_element_type=jnp.float32)
    dw_up = jnp.einsum('secd,secf->edf', x_slots, d_pre_up, preferred_element_type=jnp.float32)
    dw_down = jnp.einsum('secf,secd->efd', hidden, d_out, preferred_element_type=jnp.float32)
    d_x = jnp.einsum('secf,edf->secd', d_pre_gate, w_gate, preferred_element_type=jnp.float32) + jnp.einsum('secf,edf->secd', d_pre_up, w_up, preferred_element_type=jnp.float32)
    return d_x.astype(jnp.bfloat16), dw_gate, dw_up, dw_down


def attention_partial(x_all, w_query, w_key, w_value, w_out):
    num_seq, seq_len = x_all.shape[0], x_all.shape[1]
    heads, head_dim = w_query.shape[1], w_query.shape[2]
    kv_heads = w_key.shape[1]
    query = jnp.einsum('nld,dhe->nlhe', x_all, w_query, preferred_element_type=jnp.float32).astype(jnp.bfloat16)
    query = query.reshape(num_seq, seq_len, kv_heads, heads // kv_heads, head_dim)
    keys_h = jnp.einsum('nld,dke->nlke', x_all, w_key, preferred_element_type=jnp.float32).astype(jnp.bfloat16)
    vals_h = jnp.einsum('nld,dke->nlke', x_all, w_value, preferred_element_type=jnp.float32).astype(jnp.bfloat16)
    scores = jnp.einsum('nqkge,nske->nkgqs', query, keys_h, preferred_element_type=jnp.float32) * head_dim ** -0.5
    causal = jnp.arange(seq_len)[:, None] >= jnp.arange(seq_len)[None, :]
    probs = jax.nn.softmax(jnp.where(causal, scores, -1e30), axis=-1).astype(jnp.bfloat16)
    context = jnp.einsum('nkgqs,nske->nqkge', probs, vals_h, preferred_element_type=jnp.float32).astype(jnp.bfloat16)
    context = context.reshape(num_seq, seq_len, heads, head_dim)
    return jnp.einsum('nqhe,hed->nqd', context, w_out, preferred_element_type=jnp.float32)


def solution(mesh):
    ei_size = mesh.shape['ei']
    eo_size = mesh.shape['eo']
    num_dev = ei_size * eo_size

    def to_experts(rows, exp_loc, cap_rows):
        d_model = rows.shape[-1]
        buffer = rows.reshape(ei_size, eo_size, exp_loc, cap_rows, d_model)
        buffer = lax.all_to_all(buffer, 'eo', 1, 1, tiled=True)
        buffer = lax.all_to_all(buffer, 'ei', 0, 0, tiled=True)
        return buffer.reshape(num_dev, exp_loc, cap_rows, d_model)

    def from_experts(slots):
        exp_loc, cap_rows, d_model = slots.shape[1], slots.shape[2], slots.shape[3]
        buffer = slots.reshape(ei_size, eo_size, exp_loc, cap_rows, d_model)
        buffer = lax.all_to_all(buffer, 'ei', 0, 0, tiled=True)
        buffer = lax.all_to_all(buffer, 'eo', 1, 1, tiled=True)
        return buffer.reshape(num_dev * exp_loc * cap_rows, d_model)

    def local_step(x_tokens, expert_idx, gate_vals, dy_tokens, w_gate, w_up, w_down, x_attn, w_query, w_key, w_value, w_out):
        tok_rows, top_k = expert_idx.shape
        exp_loc, d_model = w_gate.shape[0], w_gate.shape[1]
        num_exp = exp_loc * num_dev
        cap_rows = min(tok_rows, CAP_MULT * tok_rows * top_k // num_exp)
        num_asg = tok_rows * top_k
        dest_slot, slot_owner = slot_plan(expert_idx.reshape(num_asg), num_exp, cap_rows)
        zero_row = jnp.zeros((1, d_model), jnp.bfloat16)
        src_tok = jnp.where(slot_owner < num_asg, slot_owner // top_k, tok_rows)
        x_slots = to_experts(jnp.take(jnp.concatenate([x_tokens, zero_row]), src_tok, axis=0), exp_loc, cap_rows)
        out_slots, saved = expert_forward(x_slots, w_gate, w_up, w_down)
        out_rows = jnp.take(from_experts(out_slots), dest_slot, axis=0).reshape(tok_rows, top_k, d_model)
        y_tokens = jnp.sum(gate_vals[:, :, None] * out_rows, axis=1).astype(jnp.bfloat16)
        d_gates = jnp.einsum('td,tkd->tk', dy_tokens, out_rows, preferred_element_type=jnp.float32)
        d_rows = (gate_vals[:, :, None] * dy_tokens[:, None, :]).astype(jnp.bfloat16).reshape(num_asg, d_model)
        d_out = to_experts(jnp.take(jnp.concatenate([d_rows, zero_row]), slot_owner, axis=0), exp_loc, cap_rows)
        dx_slots, dw_gate, dw_up, dw_down = expert_backward(x_slots, d_out, saved, w_gate, w_up, w_down)
        dx_rows = jnp.take(from_experts(dx_slots), dest_slot, axis=0).reshape(tok_rows, top_k, d_model)
        dx_tokens = jnp.sum(dx_rows, axis=1, dtype=jnp.float32).astype(jnp.bfloat16)
        x_all = lax.all_gather(x_attn, GROUP_AXES, axis=0, tiled=True)
        attn_part = attention_partial(x_all, w_query, w_key, w_value, w_out)
        attn_out = lax.psum_scatter(attn_part, GROUP_AXES, scatter_dimension=0, tiled=True).astype(jnp.bfloat16)
        return y_tokens, dx_tokens, d_gates, dw_gate, dw_up, dw_down, attn_out

    spec_rows = P(TOKEN_AXES, None)
    spec_seqs = P(TOKEN_AXES, None, None)
    spec_experts = P(GROUP_AXES, None, None)
    spec_heads = P(None, GROUP_AXES, None)
    return jax.shard_map(local_step, mesh=mesh,
                         in_specs=(spec_rows, spec_rows, spec_rows, spec_rows, spec_experts, spec_experts, spec_experts, spec_seqs, spec_heads, spec_heads, spec_heads, spec_experts),
                         out_specs=(spec_rows, spec_rows, spec_rows, spec_seqs, spec_seqs, spec_seqs, spec_seqs),
                         check_vma=False)
```

profile of v0, /device:TPU:0, one launch (start us, length us, event | category | flops | bytes accessed | tf_op | source)
XLA Modules:
  0.0 508.8 jit_solution(119992442538366412)
XLA Ops:
  10.6 2.5 scatter_custom_fusion
  14.2 9.6 %gather_fusion = bf16[2048,1024]{1,0:T(8,128)(2,1)} fusion(bf16[65,1024]{1,0:T(8,128)(2,1)S(1)} %concatenate.6, s32[2048]{0:T(1024)S(1)} %get-tuple-element.15), kind=kCustom, calls=%fused_computation.2 | custom fusion | bytes 8396800 | tf_op jit(solution)/shard_map/jit(_take)/gather | solution.py:86
  23.8 3.9 copy_select_fusion.1
  27.6 5.0 all-to-all-start
  33.2 9.6 %gather_fusion.1 = bf16[2048,1024]{1,0:T(8,128)(2,1)} fusion(bf16[513,1024]{1,0:T(8,128)(2,1)S(1)} %concatenate.7, s32[2048]{0:T(1024)S(1)} %get-tuple-element.14), kind=kCustom, calls=%fused_computation.3 | custom fusion | bytes 8396800 | tf_op jit(solution)/shard_map/jit(_take)/gather | solution.py:92
  42.8 3.9 copy_select_fusion
  46.7 34.9 %all-to-all-done = bf16[2,4,4,64,1024]{4,3,0,2,1:T(8,128)(2,1)} async-done(((bf16[2,4,4,64,1024]{4,3,0,2,1:T(8,128)(2,1)}), bf16[2,4,4,64,1024]{4,3,0,2,1:T(8,128)(2,1)}, u32[]{:S(2)}, u32[]{:S(2)}) %all-to-all-start) | async-done | bytes 4194336 | tf_op jit(solution)/shard_map/all_to_all | solution.py:66
  81.6 4.8 all-to-all-start.4
  86.4 4.9 copy.47
  91.3 43.0 %all-to-all-done.4 = bf16[2,4,4,64,1024]{4,3,0,2,1:T(8,128)(2,1)} async-done(((bf16[2,4,4,64,1024]{4,3,0,2,1:T(8,128)(2,1)}), bf16[2,4,4,64,1024]{4,3,0,2,1:T(8,128)(2,1)}, u32[]{:S(2)}, u32[]{:S(2)}) %all-to-all-start.4) | async-done | bytes 4194336 | tf_op jit(solution)/shard_map/all_to_all | solution.py:66
  134.3 5.6 %all-to-all-start.1 = ((bf16[2,4,4,64,1024]{4,3,1,2,0:T(8,128)(2,1)}), bf16[2,4,4,64,1024]{4,3,1,2,0:T(8,128)(2,1)}, u32[]{:S(2)}, u32[]{:S(2)}) async-start(bf16[2,4,4,64,1024]{4,3,1,2,0:T(8,128)(2,1)} %copy.47), calls=%async_computation.1 | async-start | bytes 8388608 | tf_op jit(solution)/shard_map/all_to_all | solution.py:67
  139.9 4.9 copy.55
  144.8 42.8 %all-to-all-done.1 = bf16[2,4,4,64,1024]{4,3,1,2,0:T(8,128)(2,1)} async-done(((bf16[2,4,4,64,1024]{4,3,1,2,0:T(8,128)(2,1)}), bf16[2,4,4,64,1024]{4,3,1,2,0:T(8,128)(2,1)}, u32[]{:S(2)}, u32[]{:S(2)}) %all-to-all-start.1) | async-done | bytes 4194336 | tf_op jit(solution)/shard_map/all_to_all | solution.py:67
  187.6 5.8 %all-to-all-start.5 = ((bf16[2,4,4,64,1024]{4,3,1,2,0:T(8,128)(2,1)}), bf16[2,4,4,64,1024]{4,3,1,2,0:T(8,128)(2,1)}, u32[]{:S(2)}, u32[]{:S(2)}) async-start(bf16[2,4,4,64,1024]{4,3,1,2,0:T(8,128)(2,1)} %copy.55), calls=%async_computation.5 | async-start | bytes 8388608 | tf_op jit(solution)/shard_map/all_to_all | solution.py:67
  193.4 2.8 copy.48
  196.9 4.3 fusion.6
  201.2 4.3 fusion.2
  205.6 34.4 %all-to-all-done.5 = bf16[2,4,4,64,1024]{4,3,1,2,0:T(8,128)(2,1)} async-done(((bf16[2,4,4,64,1024]{4,3,1,2,0:T(8,128)(2,1)}), bf16[2,4,4,64,1024]{4,3,1,2,0:T(8,128)(2,1)}, u32[]{:S(2)}, u32[]{:S(2)}) %all-to-all-start.5) | async-done | bytes 4194336 | tf_op jit(solution)/shard_map/all_to_all | solution.py:67
  240.0 2.9 copy.56
  243.4 2.8 copy-done.16
  246.2 7.3 %fusion.10 = (bf16[8,4,64,512]{3,2,0,1:T(8,128)(2,1)}, bf16[8,4,64,512]{3,2,0,1:T(8,128)(2,1)}, bf16[4,8,64,512]{3,2,1,0:T(8,128)(2,1)}) fusion(f32[4,8,64,512]{3,2,1,0:T(8,128)} %fusion.2, f32[4,8,64,512]{3,2,1,0:T(8,128)S(1)} %copy-done.16, bf16[8,4,64,1024]{3,2,0,1:T(8,128)(2,1)S(1)} %bitcast.198, bf16[4,512,1024]{2,1,0:T(8,128)(2,1)S(1)} %copy-done.14), kind=kOutput, calls=%fused_computation.18 | convolution fusion | flops 2163212288 | bytes 23068672 | tf_op jit(solution)/shard_map/secd,efd->secf/dot_general | solution.py:32
  253.5 6.6 %fusion = f32[4,8,64,1024]{3,2,1,0:T(8,128)S(1)} fusion(bf16[4,1024,512]{2,1,0:T(8,128)(2,1)} %param.19, bf16[4,8,64,512]{3,2,1,0:T(8,128)(2,1)} %get-tuple-element.16, f32[4,8,64,512]{3,2,1,0:T(8,128)} %fusion.6), kind=kOutput, calls=%fused_computation.6 | convolution fusion | flops 2154823680 | bytes 18874368 | tf_op jit(solution)/shard_map/secf,edf->secd/dot_general | solution.py:38
  260.1 4.1 add_convert_fusion
  264.2 2.5 copy.57
  266.6 5.8 %all-to-all-start.6 = ((bf16[2,4,4,64,1024]{4,3,1,2,0:T(8,128)(2,1)}), bf16[2,4,4,64,1024]{4,3,1,2,0:T(8,128)(2,1)}, u32[]{:S(2)}, u32[]{:S(2)}) async-start(bf16[2,4,4,64,1024]{4,3,1,2,0:T(8,128)(2,1)} %copy.57), calls=%async_computation.6 | async-start | bytes 8388608 | tf_op jit(solution)/shard_map/all_to_all | solution.py:73
  273.2 4.5 fusion.21
  277.7 2.5 copy.49
  280.2 42.4 %all-to-all-done.6 = bf16[2,4,4,64,1024]{4,3,1,2,0:T(8,128)(2,1)} async-done(((bf16[2,4,4,64,1024]{4,3,1,2,0:T(8,128)(2,1)}), bf16[2,4,4,64,1024]{4,3,1,2,0:T(8,128)(2,1)}, u32[]{:S(2)}, u32[]{:S(2)}) %all-to-all-start.6) | async-done | bytes 4194336 | tf_op jit(solution)/shard_map/all_to_all | solution.py:73
  322.6 5.6 %all-to-all-start.2 = ((bf16[2,4,4,64,1024]{4,3,1,2,0:T(8,128)(2,1)}), bf16[2,4,4,64,1024]{4,3,1,2,0:T(8,128)(2,1)}, u32[]{:S(2)}, u32[]{:S(2)}) async-start(bf16[2,4,4,64,1024]{4,3,1,2,0:T(8,128)(2,1)} %copy.49), calls=%async_computation.2 | async-start | bytes 8388608 | tf_op jit(solution)/shard_map/all_to_all | solution.py:73
  328.3 1.7 fusion.34
  330.1 2.3 fusion.62
  332.9 2.0 convolution_bitcast_fusion.3
  335.0 4.9 copy.58
  339.9 41.9 %all-to-all-done.2 = bf16[2,4,4,64,1024]{4,3,1,2,0:T(8,128)(2,1)} async-done(((bf16[2,4,4,64,1024]{4,3,1,2,0:T(8,128)(2,1)}), bf16[2,4,4,64,1024]{4,3,1,2,0:T(8,128)(2,1)}, u32[]{:S(2)}, u32[]{:S(2)}) %all-to-all-start.2) | async-done | bytes 4194336 | tf_op jit(solution)/shard_map/all_to_all | solution.py:73
  381.8 4.9 all-to-all-start.7
  386.8 1.6 convert_element_type.100
  388.4 4.8 copy.50
  393.3 41.4 %all-to-all-done.7 = bf16[2,4,4,64,1024]{4,3,0,2,1:T(8,128)(2,1)} async-done(((bf16[2,4,4,64,1024]{4,3,0,2,1:T(8,128)(2,1)}), bf16[2,4,4,64,1024]{4,3,0,2,1:T(8,128)(2,1)}, u32[]{:S(2)}, u32[]{:S(2)}) %all-to-all-start.7) | async-done | bytes 4194336 | tf_op jit(solution)/shard_map/all_to_all | solution.py:74
  434.6 4.9 all-to-all-start.3
  439.6 8.1 %convolution_bitcast_fusion.2 = f32[4,1024,512]{2,1,0:T(8,128)} fusion(bf16[8,4,64,1024]{3,2,0,1:T(8,128)(2,1)} %bitcast.196, bf16[8,4,64,512]{3,2,0,1:T(8,128)(2,1)S(1)} %copy-done.8), kind=kOutput, calls=%fused_computation.37 | convolution fusion | flops 2147483648 | bytes 14680064 | tf_op jit(solution)/shard_map/secd,secf->edf/dot_general | solution.py:35
  447.7 5.9 %convolution_bitcast_fusion = f32[4,512,1024]{2,1,0:T(8,128)} fusion(bf16[8,4,64,512]{3,2,0,1:T(8,128)(2,1)S(1)} %copy-done.19, bf16[8,4,64,1024]{3,2,0,1:T(8,128)(2,1)S(1)} %bitcast.199), kind=kOutput, calls=%fused_computation.35 | convolution fusion | flops 2147483648 | bytes 14680064 | tf_op jit(solution)/shard_map/secf,secd->efd/dot_general | solution.py:37
  453.7 5.9 %convolution_bitcast_fusion.1 = f32[4,1024,512]{2,1,0:T(8,128)} fusion(bf16[8,4,64,1024]{3,2,0,1:T(8,128)(2,1)S(1)} %bitcast.197, bf16[4,8,64,512]{3,2,1,0:T(8,128)(2,1)S(1)} %copy-done.20, f32[4,8,64,512]{3,2,1,0:T(8,128)S(1)} %copy-done.17), kind=kOutput, calls=%fused_computation.36 | convolution fusion | flops 2154823680 | bytes 18874368 | tf_op jit(solution)/shard_map/secd,secf->edf/dot_general | solution.py:36
  459.6 4.9 copy.59
  464.4 5.5 %gather_fusion.3 = bf16[512,1024]{1,0:T(8,128)(2,1)S(1)} fusion(bf16[2048,1024]{1,0:T(8,128)(2,1)} %bitcast.190, s32[1024]{0:T(1024)S(1)} %pad_clamp_fusion), kind=kCustom, calls=%fused_computation.1.clone | custom fusion | bytes 2099200 | tf_op jit(solution)/shard_map/jit(_take)/gather | solution.py:94
  469.9 17.5 %all-to-all-done.3 = bf16[2,4,4,64,1024]{4,3,0,2,1:T(8,128)(2,1)} async-done(((bf16[2,4,4,64,1024]{4,3,0,2,1:T(8,128)(2,1)}), bf16[2,4,4,64,1024]{4,3,0,2,1:T(8,128)(2,1)}, u32[]{:S(2)}, u32[]{:S(2)}) %all-to-all-start.3) | async-done | bytes 4194336 | tf_op jit(solution)/shard_map/all_to_all | solution.py:74
  487.4 4.9 copy.51
  492.3 5.5 %gather_fusion.2 = bf16[512,1024]{1,0:T(8,128)(2,1)S(1)} fusion(bf16[2048,1024]{1,0:T(8,128)(2,1)} %bitcast.189, s32[1024]{0:T(1024)S(1)} %pad_clamp_fusion), kind=kCustom, calls=%fused_computation.clone | custom fusion | bytes 2099200 | tf_op jit(solution)/shard_map/jit(_take)/gather | solution.py:88
  499.0 1.5 multiply_reduce_fusion
  (81 shorter events, 10.4 us)
Async XLA Ops:
  7.2 325.8 %copy-start = (bf16[2,64,1024]{2,1,0:T(8,128)(2,1)S(1)}, bf16[2,64,1024]{2,1,0:T(8,128)(2,1)}, u32[]{:S(2)}) copy-start(bf16[2,64,1024]{2,1,0:T(8,128)(2,1)} %param.25) | copy-start | bytes 786436
  27.6 5.0 copy-start.12
  27.6 5.2 %copy-start.11 = (bf16[64,1024]{1,0:T(8,128)(2,1)S(1)}, bf16[64,1024]{1,0:T(8,128)(2,1)}, u32[]{:S(2)}) copy-start(bf16[64,1024]{1,0:T(8,128)(2,1)} %param.17) | copy-start | bytes 393220
  27.6 53.9 %all-to-all-start = ((bf16[2,4,4,64,1024]{4,3,0,2,1:T(8,128)(2,1)}), bf16[2,4,4,64,1024]{4,3,0,2,1:T(8,128)(2,1)}, u32[]{:S(2)}, u32[]{:S(2)}) async-start(bf16[2,4,4,64,1024]{4,3,0,2,1:T(8,128)(2,1)} %copy_select_fusion.1), calls=%async_computation | async-start | bytes 8388608 | tf_op jit(solution)/shard_map/all_to_all | solution.py:66
  81.6 52.7 %all-to-all-start.4 = ((bf16[2,4,4,64,1024]{4,3,0,2,1:T(8,128)(2,1)}), bf16[2,4,4,64,1024]{4,3,0,2,1:T(8,128)(2,1)}, u32[]{:S(2)}, u32[]{:S(2)}) async-start(bf16[2,4,4,64,1024]{4,3,0,2,1:T(8,128)(2,1)} %copy_select_fusion), calls=%async_computation.4 | async-start | bytes 8388608 | tf_op jit(solution)/shard_map/all_to_all | solution.py:66
  134.3 53.3 %all-to-all-start.1 = ((bf16[2,4,4,64,1024]{4,3,1,2,0:T(8,128)(2,1)}), bf16[2,4,4,64,1024]{4,3,1,2,0:T(8,128)(2,1)}, u32[]{:S(2)}, u32[]{:S(2)}) async-start(bf16[2,4,4,64,1024]{4,3,1,2,0:T(8,128)(2,1)} %copy.47), calls=%async_computation.1 | async-start | bytes 8388608 | tf_op jit(solution)/shard_map/all_to_all | solution.py:67
  187.6 52.3 %all-to-all-start.5 = ((bf16[2,4,4,64,1024]{4,3,1,2,0:T(8,128)(2,1)}), bf16[2,4,4,64,1024]{4,3,1,2,0:T(8,128)(2,1)}, u32[]{:S(2)}, u32[]{:S(2)}) async-start(bf16[2,4,4,64,1024]{4,3,1,2,0:T(8,128)(2,1)} %copy.55), calls=%async_computation.5 | async-start | bytes 8388608 | tf_op jit(solution)/shard_map/all_to_all | solution.py:67
  193.4 3.5 copy-start.6
  196.3 5.0 copy-start.2
  196.9 4.4 copy-start.13
  239.9 3.4 copy-start.14
  240.0 6.2 %copy-start.16 = (f32[4,8,64,512]{3,2,1,0:T(8,128)S(1)}, f32[4,8,64,512]{3,2,1,0:T(8,128)}, u32[]{:S(2)}) copy-start(f32[4,8,64,512]{3,2,1,0:T(8,128)} %fusion.6) | copy-start | bytes 12582916
  242.8 10.6 %copy-start.4 = (bf16[2,4,4,64,1024]{4,3,1,0,2:T(8,128)(2,1)}, bf16[2,4,4,64,1024]{4,3,1,0,2:T(8,128)(2,1)S(1)}, u32[]{:S(2)}) copy-start(bf16[2,4,4,64,1024]{4,3,1,0,2:T(8,128)(2,1)S(1)} %copy.56) | copy-start | bytes 12582916
  253.5 6.6 %copy-start.7 = (bf16[4,1024,512]{2,1,0:T(8,128)(2,1)S(1)}, bf16[4,1024,512]{2,1,0:T(8,128)(2,1)}, u32[]{:S(2)}) copy-start(bf16[4,1024,512]{2,1,0:T(8,128)(2,1)} %param.18) | copy-start | bytes 12582916
  266.6 6.5 %copy-start.18 = (bf16[8,4,64,512]{3,2,0,1:T(8,128)(2,1)S(1)}, bf16[8,4,64,512]{3,2,0,1:T(8,128)(2,1)}, u32[]{:S(2)}) copy-start(bf16[8,4,64,512]{3,2,0,1:T(8,128)(2,1)} %get-tuple-element.11) | copy-start | bytes 6291460
  266.6 55.9 %all-to-all-start.6 = ((bf16[2,4,4,64,1024]{4,3,1,2,0:T(8,128)(2,1)}), bf16[2,4,4,64,1024]{4,3,1,2,0:T(8,128)(2,1)}, u32[]{:S(2)}, u32[]{:S(2)}) async-start(bf16[2,4,4,64,1024]{4,3,1,2,0:T(8,128)(2,1)} %copy.57), calls=%async_computation.6 | async-start | bytes 8388608 | tf_op jit(solution)/shard_map/all_to_all | solution.py:73
  272.4 55.9 %all-gather.2.cloned.1.call-start = ((), (), s32[]{:S(2)}) async-start(), calls=%async_computation.9 | async-start | bytes 1179648 | tf_op jit(solution)/shard_map/all_gather | solution.py:96
  280.2 48.1 %copy-start.9 = (bf16[1024,1,64]{0,2,1:T(8,128)(2,1)S(1)}, bf16[1024,1,64]{0,2,1:T(8,128)(2,1)}, u32[]{:S(2)}) copy-start(bf16[1024,1,64]{0,2,1:T(8,128)(2,1)} %param.23) | copy-start | bytes 393220
  280.2 49.9 %copy-start.15 = (bf16[1024,2,64]{0,2,1:T(8,128)(2,1)S(1)}, bf16[1024,2,64]{0,2,1:T(8,128)(2,1)}, u32[]{:S(2)}) copy-start(bf16[1024,2,64]{0,2,1:T(8,128)(2,1)} %param.22) | copy-start | bytes 786436
  322.6 59.2 %all-to-all-start.2 = ((bf16[2,4,4,64,1024]{4,3,1,2,0:T(8,128)(2,1)}), bf16[2,4,4,64,1024]{4,3,1,2,0:T(8,128)(2,1)}, u32[]{:S(2)}, u32[]{:S(2)}) async-start(bf16[2,4,4,64,1024]{4,3,1,2,0:T(8,128)(2,1)} %copy.49), calls=%async_computation.2 | async-start | bytes 8388608 | tf_op jit(solution)/shard_map/all_to_all | solution.py:73
  328.2 4.3 copy-start.10
  328.2 58.6 %reduce-scatter.2.cloned.1.call-start = ((), (), s32[]{:S(2)}) async-start(), calls=%async_computation.10 | async-start | bytes 2359296 | tf_op jit(solution)/shard_map/reduce_scatter | solution.py:98
  328.3 4.2 copy-start.1
  381.8 52.8 %all-to-all-start.7 = ((bf16[2,4,4,64,1024]{4,3,0,2,1:T(8,128)(2,1)}), bf16[2,4,4,64,1024]{4,3,0,2,1:T(8,128)(2,1)}, u32[]{:S(2)}, u32[]{:S(2)}) async-start(bf16[2,4,4,64,1024]{4,3,0,2,1:T(8,128)(2,1)} %copy.58), calls=%async_computation.7 | async-start | bytes 8388608 | tf_op jit(solution)/shard_map/all_to_all | solution.py:74
  393.3 46.3 %copy-start.8 = (bf16[8,4,64,512]{3,2,0,1:T(8,128)(2,1)S(1)}, bf16[8,4,64,512]{3,2,0,1:T(8,128)(2,1)}, u32[]{:S(2)}) copy-start(bf16[8,4,64,512]{3,2,0,1:T(8,128)(2,1)} %get-tuple-element.10) | copy-start | bytes 6291460
  434.6 52.8 %all-to-all-start.3 = ((bf16[2,4,4,64,1024]{4,3,0,2,1:T(8,128)(2,1)}), bf16[2,4,4,64,1024]{4,3,0,2,1:T(8,128)(2,1)}, u32[]{:S(2)}, u32[]{:S(2)}) async-start(bf16[2,4,4,64,1024]{4,3,0,2,1:T(8,128)(2,1)} %copy.50), calls=%async_computation.3 | async-start | bytes 8388608 | tf_op jit(solution)/shard_map/all_to_all | solution.py:74
  439.6 8.1 %copy-start.5 = (bf16[2,4,4,64,1024]{4,3,1,0,2:T(8,128)(2,1)S(1)}, bf16[2,4,4,64,1024]{4,3,1,0,2:T(8,128)(2,1)}, u32[]{:S(2)}) copy-start(bf16[2,4,4,64,1024]{4,3,1,0,2:T(8,128)(2,1)} %copy-done.4) | copy-start | bytes 12582916
  439.6 8.1 %copy-start.19 = (bf16[8,4,64,512]{3,2,0,1:T(8,128)(2,1)S(1)}, bf16[8,4,64,512]{3,2,0,1:T(8,128)(2,1)}, u32[]{:S(2)}) copy-start(bf16[8,4,64,512]{3,2,0,1:T(8,128)(2,1)} %get-tuple-element.11) | copy-start | bytes 6291460
  447.7 5.9 %copy-start.3 = (bf16[2,4,4,64,1024]{4,3,1,0,2:T(8,128)(2,1)S(1)}, bf16[2,4,4,64,1024]{4,3,1,0,2:T(8,128)(2,1)}, u32[]{:S(2)}) copy-start(bf16[2,4,4,64,1024]{4,3,1,0,2:T(8,128)(2,1)} %copy-done.2) | copy-start | bytes 12582916
  447.7 5.9 %copy-start.17 = (f32[4,8,64,512]{3,2,1,0:T(8,128)S(1)}, f32[4,8,64,512]{3,2,1,0:T(8,128)}, u32[]{:S(2)}) copy-start(f32[4,8,64,512]{3,2,1,0:T(8,128)} %fusion.6) | copy-start | bytes 12582916
  447.7 5.9 %copy-start.20 = (bf16[4,8,64,512]{3,2,1,0:T(8,128)(2,1)S(1)}, bf16[4,8,64,512]{3,2,1,0:T(8,128)(2,1)}, u32[]{:S(2)}) copy-start(bf16[4,8,64,512]{3,2,1,0:T(8,128)(2,1)} %get-tuple-element.16) | copy-start | bytes 6291460
Sparse Core Ops, SparseCore 0:
  275.1 23.5 all-gather.1
  335.1 43.0 reduce-scatter.1
where the time goes:
time: 510 us; the launch traced here: 509 us
  waiting for transfers between devices  299 us (59%)
  local copies, waits for them, and re-layouts  80 us (16%)
  matrix products  58.5 us (11%)
  starting transfers between devices  42.8 us (8%)
  between operations  14.5 us (3%)
  other arithmetic  14.4 us (3%)
    all_to_all x2, waiting for transfers between devices, from_experts(): buffer = lax.all_to_all(buffer, 'ei', 0, 0, tiled=True)  84.3 us
    all_to_all x2, waiting for transfers between devices, to_experts(): buffer = lax.all_to_all(buffer, 'eo', 1, 1, tiled=True)  77.8 us
    all_to_all x2, waiting for transfers between devices, to_experts(): buffer = lax.all_to_all(buffer, 'ei', 0, 0, tiled=True)  77.2 us
    all_to_all x2, waiting for transfers between devices, from_experts(): buffer = lax.all_to_all(buffer, 'eo', 1, 1, tiled=True)  58.9 us
    all_to_all x2, starting transfers between devices, to_experts(): buffer = lax.all_to_all(buffer, 'ei', 0, 0, tiled=True)  11.4 us
    all_to_all x2, starting transfers between devices, from_experts(): buffer = lax.all_to_all(buffer, 'ei', 0, 0, tiled=True)  11.4 us
  transfers between devices with their start and end apart: 10, of which 8 were waited for; matrix products, arithmetic and copies ran while one was open for 18% of the time, Pallas kernels for 0%

commit v1 on v0

v1 whole, which is shorter than its diff:
```python
import functools

import jax
import jax.numpy as jnp
from jax import lax
from jax.experimental import pallas as pl
from jax.experimental.pallas import tpu as pltpu
from jax.sharding import PartitionSpec as P

MESH = pl.DeviceIdType.MESH
GROUP_AXES = ('ei', 'eo')
TOKEN_AXES = ('dp', 'ei', 'eo')
BF = jnp.bfloat16
F32 = jnp.float32

ROWS = 64
TOK = 512
D = 1024
FF = 512
HALF = 512
EXP = 4
TOPK = 8
GATHER_COPIES = 9
RS_COPIES = 8
XA, XT, DY = 0, 1, 2

NT = (((1,), (1,)), ((), ()))
TN = (((0,), (0,)), ((), ()))


def exchange_kernel(x_hbm, dy_hbm, xa_hbm, idx_ref, gate_ref, wg_hbm, wu_hbm, wd_hbm, wqkv_hbm, wo_hbm,
                    y_out, dx_out, dg_out, at_out, xall_out, dyall_out, h_out, da_out, db_out, gt_out,
                    rows, wg, wu, wd, wqkv, wo, hid, dag, dbg, act, gfac, gt, gpad, gsend, grecv,
                    dgs, dsend, drecv, dpad,
                    part, pair, s1, r1, s2, r2,
                    in_sem, w_sem, out_sem, gs_sem, gr_sem, rs_s, rs_r, ag_s, ag_r, dd_s, dd_r):
    y = lax.axis_index('ei')
    o = lax.axis_index('eo')
    z = lax.axis_index('dp')
    x = o // 2
    c = o % 2
    me = y * 4 + o
    q0 = 2 * y + x
    qx = 2 * y + (1 - x)
    qy = 2 * (1 - y) + x
    qd = 2 * (1 - y) + (1 - x)

    def dev(fx, fy, fc):
        xx = (1 - x) if fx else x
        yy = (1 - y) if fy else y
        cc = (1 - c) if fc else c
        return (z, yy, xx * 2 + cc)

    sib, xn, yn = dev(0, 0, 1), dev(1, 0, 0), dev(0, 1, 0)
    rels = [(fx, fy, fc) for fx in (0, 1) for fy in (0, 1) for fc in (0, 1) if fx or fy or fc]

    barrier = pltpu.get_barrier_semaphore()
    for rel in rels:
        pl.semaphore_signal(barrier, inc=1, device_id=dev(*rel), device_id_type=MESH)

    own = pl.ds(pl.multiple_of(me * ROWS, ROWS), ROWS)
    ins = [pltpu.make_async_copy(src, rows.at[t, own], in_sem.at[t])
           for t, src in ((XA, xa_hbm), (XT, x_hbm), (DY, dy_hbm))]
    for cp in ins:
        cp.start()
    wload = [pltpu.make_async_copy(wqkv_hbm, wqkv, w_sem.at[0]), pltpu.make_async_copy(wo_hbm, wo, w_sem.at[1])]
    for n, (src, dst) in enumerate(((wg_hbm, wg), (wu_hbm, wu), (wd_hbm, wd))):
        for e in range(EXP):
            wload.append(pltpu.make_async_copy(src.at[e], dst.at[e], w_sem.at[2 + n * EXP + e]))
    for cp in wload:
        cp.start()

    lane = lax.broadcasted_iota(jnp.int32, (ROWS, 128), 1)
    lane_exp = (lane // 8) * 4 + lane % 4
    is_gate = (lane % 8) < 4
    in_range = lane < 64
    table = jnp.zeros((ROWS, 128), F32)
    for j in range(TOPK):
        hit = (lane_exp == idx_ref[:, j:j + 1]) & in_range
        table = table + jnp.where(hit, jnp.where(is_gate, gate_ref[:, j:j + 1], 1.0), 0.0)
    gpad[...] = jnp.zeros((128, 128), F32)
    gpad[pl.ds(pl.multiple_of(c * ROWS, ROWS), ROWS), :] = table
    table_t = gpad[...].T
    for d in range(8):
        gsend[d] = table_t[d * 8:(d + 1) * 8, :]
    grecv[me] = gsend[me]
    dgs[...] = jnp.zeros((TOK, 128), F32)
    part[1] = jnp.zeros(part.shape[1:], F32)
    part[2] = jnp.zeros(part.shape[1:], F32)

    def blk(t, q, off=0, n=ROWS):
        return rows.at[t, pl.ds(pl.multiple_of(q * 128 + c * ROWS + off, 32), n)]

    def remote(src, dst, ss, rs, where):
        return pltpu.make_async_remote_copy(src, dst, ss, rs, device_id=where, device_id_type=MESH)

    hr = ROWS // 2

    def gather_copies(t):
        def cp(k, ref, where):
            return remote(ref, ref, ag_s.at[t, k], ag_r.at[t, k], where)
        return [cp(0, blk(t, q0), sib), cp(1, blk(t, q0), xn), cp(2, blk(t, q0), yn),
                cp(3, blk(t, qx, 0, hr), yn), cp(4, blk(t, qy, hr, hr), xn),
                cp(5, blk(t, qx), sib), cp(6, blk(t, qy), sib),
                cp(7, blk(t, qd, 0, hr), sib), cp(8, blk(t, qd, hr, hr), sib)]

    ag = [gather_copies(t) for t in range(3)]

    def ag_own(t):
        for k in (1, 2, 0):
            ag[t][k].start()

    def ag_forward(t):
        ag[t][1].wait_recv()
        ag[t][3].start()
        ag[t][5].start()
        ag[t][2].wait_recv()
        ag[t][4].start()
        ag[t][6].start()

    def ag_last(t):
        ag[t][3].wait_recv()
        ag[t][7].start()
        ag[t][4].wait_recv()
        ag[t][8].start()

    def ag_done(t):
        for k in (0, 5, 6, 7, 8):
            ag[t][k].wait_recv()

    def tile_copies(send, recv, ss, rs, chip_tiles):
        cps = []
        for k, (fx, fy, fc) in enumerate(rels):
            where = dev(fx, fy, fc)
            qq = 2 * where[1] + where[2] // 2
            src = send.at[qq] if chip_tiles else send.at[where[1] * 4 + where[2]]
            cps.append(remote(src, recv.at[me], ss.at[k], rs.at[k], where))
        return cps

    gate_cps = tile_copies(gsend, grecv, gs_sem, gr_sem, False)
    dg_cps = tile_copies(dsend, drecv, dd_s, dd_r, True)

    def rs_copies(n):
        def cp(k, src, dst, where):
            return remote(src, dst, rs_s.at[n, k], rs_r.at[n, k], where)
        return [cp(0, part.at[n, 1 - c, 0], pair.at[n, 0], sib), cp(1, part.at[n, 1 - c, 1], pair.at[n, 1], sib),
                cp(2, s1.at[n, 0, 0], r1.at[n, 0, 0], xn), cp(3, s1.at[n, 0, 1], r1.at[n, 0, 1], xn),
                cp(4, s1.at[n, 1, 0], r1.at[n, 1, 0], yn), cp(5, s1.at[n, 1, 1], r1.at[n, 1, 1], yn),
                cp(6, s2.at[n, 0], r2.at[n, 0], yn), cp(7, s2.at[n, 1], r2.at[n, 1], xn)]

    rsc = [rs_copies(n) for n in range(3)]
    first = (qx, qy)
    second = (qy, qx)

    def rs_pair(n):
        rsc[n][0].start()
        rsc[n][1].start()

    def rs_stage1(n):
        for h in range(2):
            rsc[n][h].wait_recv()
            s1[n, h, 0] = part[n, c, h, qd] + pair[n, h, qd]
            rsc[n][2 + 2 * h].start()
        for h in range(2):
            s1[n, h, 1] = part[n, c, h, first[h]] + pair[n, h, first[h]]
            rsc[n][3 + 2 * h].start()

    def rs_stage2(n):
        for h in range(2):
            rsc[n][2 + 2 * h].wait_recv()
            s2[n, h] = part[n, c, h, second[h]] + pair[n, h, second[h]] + r1[n, h, 0]
            rsc[n][6 + h].start()

    def rs_final(n, out_ref):
        for h in range(2):
            rsc[n][3 + 2 * h].wait_recv()
            rsc[n][6 + h].wait_recv()
            total = part[n, c, h, q0] + pair[n, h, q0] + r1[n, h, 1] + r2[n, h]
            out_ref[:, h * HALF:(h + 1) * HALF] = total.astype(BF)

    for cp in ins:
        cp.wait()
    pl.semaphore_wait(barrier, len(rels))
    for cp in gate_cps:
        cp.start()
    ag_own(XA)
    ag_own(XT)
    ag_forward(XA)
    ag_own(DY)
    ag_forward(XT)
    ag_last(XA)

    for cp in gate_cps:
        cp.wait_recv()
    for q in range(4):
        tile = grecv[2 * q] + grecv[2 * q + 1]
        gt[q * 128:(q + 1) * 128, :] = jnp.concatenate([tile, jnp.zeros((120, 128), F32)], axis=0).T

    ag_done(XA)

    wload[0].wait()
    wload[1].wait()
    causal_r = lax.broadcasted_iota(jnp.int32, (256, 128), 0) % 128
    causal_c = lax.broadcasted_iota(jnp.int32, (256, 128), 1)
    keep = (causal_r >= causal_c) & (causal_r // 64 == causal_c // 64)
    for q in range(4):
        xs = rows[XA, q * 128:(q + 1) * 128, :]
        qkv = jnp.dot(xs, wqkv[...], preferred_element_type=F32).astype(BF)
        qs = jnp.concatenate([qkv[:, 0:64], qkv[:, 64:128]], axis=0)
        sc = lax.dot_general(qs, qkv[:, 128:192], NT, preferred_element_type=F32) * (64 ** -0.5)
        sc = jnp.where(keep, sc, -1e30)
        ex = jnp.exp(sc - jnp.max(sc, axis=1, keepdims=True))
        pr = (ex / jnp.sum(ex, axis=1, keepdims=True)).astype(BF)
        ctx = jnp.dot(pr, qkv[:, 192:256], preferred_element_type=F32).astype(BF)
        ctx = jnp.concatenate([ctx[0:128], ctx[128:256]], axis=1)
        out = jnp.dot(ctx, wo[...], preferred_element_type=F32)
        for cc in range(2):
            for h in range(2):
                part[0, cc, h, q] = out[cc * 64:(cc + 1) * 64, h * HALF:(h + 1) * HALF]
    rs_pair(0)
    ag_forward(DY)
    ag_last(XT)
    ag_last(DY)
    rs_stage1(0)
    ag_done(XT)
    ag_done(DY)

    outs = [pltpu.make_async_copy(rows.at[XT], xall_out, out_sem.at[0]),
            pltpu.make_async_copy(rows.at[DY], dyall_out, out_sem.at[1]),
            pltpu.make_async_copy(gt, gt_out, out_sem.at[2])]
    for cp in outs:
        cp.start()
    for cp in wload[2:]:
        cp.wait()
    lane_t = lax.broadcasted_iota(jnp.int32, (256, 128), 1)

    def pick(tile, e):
        return jnp.sum(jnp.where(lane_t == e, tile, 0.0), axis=1, keepdims=True)

    def accumulate(n, m, val):
        for b in range(4):
            q, cc = (m * 4 + b) // 2, b % 2
            for h in range(2):
                part[n, cc, h, q] += val[b * 64:(b + 1) * 64, h * HALF:(h + 1) * HALF]

    def forward(e, carry):
        for m in range(2):
            sl = slice(m * 256, (m + 1) * 256)
            xs = rows[XT, sl, :]
            a = jnp.dot(xs, wg[e], preferred_element_type=F32)
            b = jnp.dot(xs, wu[e], preferred_element_type=F32)
            tile = gt[sl, :]
            mark = pick(tile, e + 4) > 0.5
            sg = jax.nn.sigmoid(a)
            ac = a * sg
            act[e, sl, :] = jnp.where(mark, ac, 0.0)
            gfac[e, sl, :] = jnp.where(mark, b * sg * (1.0 + a * (1.0 - sg)), 0.0)
            hh = jnp.where(mark, ac * b, 0.0).astype(BF)
            hid[e, sl, :] = hh
            ob = jnp.dot(hh, wd[e], preferred_element_type=F32).astype(BF).astype(F32)
            accumulate(1, m, pick(tile, e) * ob)
            dg = jnp.sum(rows[DY, sl, :].astype(F32) * ob, axis=1, keepdims=True)
            dgs[sl, :] += jnp.where(lane_t == e, dg, 0.0)
        pltpu.make_async_copy(hid.at[e], h_out.at[e], out_sem.at[3 + e]).start()

        @pl.when(e == 2)
        def _():
            rs_stage2(0)
        return carry

    lax.fori_loop(0, EXP, forward, 0)
    rs_pair(1)
    for q in range(4):
        dsend[q] = dgs[q * 128:(q + 1) * 128, :].T[0:8, :]
    drecv[me] = dsend[q0]
    for cp in dg_cps:
        cp.start()
    rs_stage1(1)

    def backward(e, carry):
        for m in range(2):
            sl = slice(m * 256, (m + 1) * 256)
            g = pick(gt[sl, :], e)
            do = (g * rows[DY, sl, :].astype(F32)).astype(BF)
            dh = lax.dot_general(do, wd[e], NT, preferred_element_type=F32).astype(BF).astype(F32)
            da = (dh * gfac[e, sl, :]).astype(BF)
            db = (dh * act[e, sl, :]).astype(BF)
            dag[e, sl, :] = da
            dbg[e, sl, :] = db
            dx = (lax.dot_general(da, wg[e], NT, preferred_element_type=F32)
                  + lax.dot_general(db, wu[e], NT, preferred_element_type=F32))
            accumulate(2, m, dx.astype(BF).astype(F32))
        pltpu.make_async_copy(dag.at[e], da_out.at[e], out_sem.at[3 + EXP + e]).start()
        pltpu.make_async_copy(dbg.at[e], db_out.at[e], out_sem.at[3 + 2 * EXP + e]).start()

        @pl.when(e == 1)
        def _():
            rs_stage2(1)
        return carry

    lax.fori_loop(0, EXP, backward, 0)
    rs_pair(2)
    rs_final(0, at_out)
    rs_stage1(2)
    rs_final(1, y_out)
    for cp in dg_cps:
        cp.wait_recv()
    dpad[...] = jnp.zeros((128, 128), F32)
    for d in range(8):
        dpad[d * 8:(d + 1) * 8, :] = drecv[d]
    gpad[...] = dpad[...].T
    mine = gpad[pl.ds(pl.multiple_of(c * ROWS, ROWS), ROWS), :]
    for j in range(TOPK):
        ij = idx_ref[:, j:j + 1]
        hit = lane == (ij // 4) * 8 + ij % 4
        dg_out[:, j:j + 1] = jnp.sum(jnp.where(hit, mine, 0.0), axis=1, keepdims=True)
    rs_stage2(2)
    rs_final(2, dx_out)

    for cp in outs:
        cp.wait()
    for e in range(EXP):
        pltpu.make_async_copy(hid.at[e], h_out.at[e], out_sem.at[3 + e]).wait()
        pltpu.make_async_copy(dag.at[e], da_out.at[e], out_sem.at[3 + EXP + e]).wait()
        pltpu.make_async_copy(dbg.at[e], db_out.at[e], out_sem.at[3 + 2 * EXP + e]).wait()
    for group in ag + rsc + [gate_cps, dg_cps]:
        for cp in group:
            cp.wait_send()


def exchange(x, dy, xa, idx, gates, wg, wu, wd, wqkv, wo):
    any_spec = pl.BlockSpec(memory_space=pl.ANY)
    vmem = pl.BlockSpec(memory_space=pltpu.VMEM)
    sds = jax.ShapeDtypeStruct
    dma = pltpu.SemaphoreType.DMA
    return pl.pallas_call(
        exchange_kernel,
        name='exchange',
        out_shape=[sds((ROWS, D), BF), sds((ROWS, D), BF), sds((ROWS, TOPK), F32), sds((ROWS, D), BF),
                   sds((TOK, D), BF), sds((TOK, D), BF),
                   sds((EXP, TOK, FF), BF), sds((EXP, TOK, FF), BF), sds((EXP, TOK, FF), BF), sds((TOK, 128), F32)],
        in_specs=[any_spec, any_spec, any_spec, vmem, vmem] + [any_spec] * 5,
        out_specs=[vmem] * 4 + [any_spec] * 6,
        scratch_shapes=[
            pltpu.VMEM((3, TOK, D), BF),
            pltpu.VMEM((EXP, D, FF), BF), pltpu.VMEM((EXP, D, FF), BF), pltpu.VMEM((EXP, FF, D), BF),
            pltpu.VMEM((D, 256), BF), pltpu.VMEM((128, D), BF),
            pltpu.VMEM((EXP, TOK, FF), BF), pltpu.VMEM((EXP, TOK, FF), BF), pltpu.VMEM((EXP, TOK, FF), BF),
            pltpu.VMEM((EXP, TOK, FF), F32), pltpu.VMEM((EXP, TOK, FF), F32),
            pltpu.VMEM((TOK, 128), F32), pltpu.VMEM((128, 128), F32),
            pltpu.VMEM((8, 8, 128), F32), pltpu.VMEM((8, 8, 128), F32),
            pltpu.VMEM((TOK, 128), F32), pltpu.VMEM((4, 8, 128), F32), pltpu.VMEM((8, 8, 128), F32),
            pltpu.VMEM((128, 128), F32),
            pltpu.VMEM((3, 2, 2, 4, ROWS, HALF), F32), pltpu.VMEM((3, 2, 4, ROWS, HALF), F32),
            pltpu.VMEM((3, 2, 2, ROWS, HALF), F32), pltpu.VMEM((3, 2, 2, ROWS, HALF), F32),
            pltpu.VMEM((3, 2, ROWS, HALF), F32), pltpu.VMEM((3, 2, ROWS, HALF), F32),
            dma((3,)), dma((2 + 3 * EXP,)), dma((3 + 3 * EXP,)), dma((7,)), dma((7,)),
            dma((3, RS_COPIES)), dma((3, RS_COPIES)), dma((3, GATHER_COPIES)), dma((3, GATHER_COPIES)),
            dma((7,)), dma((7,)),
        ],
        compiler_params=pltpu.CompilerParams(collective_id=0, has_side_effects=True, vmem_limit_bytes=60 * 1024 * 1024),
    )(x, dy, xa, idx, gates, wg, wu, wd, wqkv, wo)


def grads_kernel(x_ref, dy_ref, gt_ref, h_ref, da_ref, db_ref, dwg_ref, dwu_ref, dwd_ref, xt):
    e = pl.program_id(0)

    @pl.when(e == 0)
    def _():
        xt[...] = x_ref[...].T

    dwg_ref[0] = jnp.dot(xt[...], da_ref[0], preferred_element_type=F32)
    dwu_ref[0] = jnp.dot(xt[...], db_ref[0], preferred_element_type=F32)
    lane = lax.broadcasted_iota(jnp.int32, (TOK, 128), 1)
    g = jnp.sum(jnp.where(lane == e, gt_ref[...], 0.0), axis=1, keepdims=True)
    do = (g * dy_ref[...].astype(F32)).astype(BF)
    dwd_ref[0] = lax.dot_general(h_ref[0], do, TN, preferred_element_type=F32)


def weight_grads(xall, dyall, gt, h, da, db):
    sds = jax.ShapeDtypeStruct
    whole = lambda shape: pl.BlockSpec(shape, lambda e: (0, 0))
    per = lambda a, b: pl.BlockSpec((1, a, b), lambda e: (e, 0, 0))
    return pl.pallas_call(
        grads_kernel,
        name='weight_grads',
        grid=(EXP,),
        out_shape=[sds((EXP, D, FF), F32), sds((EXP, D, FF), F32), sds((EXP, FF, D), F32)],
        in_specs=[whole((TOK, D)), whole((TOK, D)), whole((TOK, 128)), per(TOK, FF), per(TOK, FF), per(TOK, FF)],
        out_specs=[per(D, FF), per(D, FF), per(FF, D)],
        scratch_shapes=[pltpu.VMEM((D, TOK), BF)],
        compiler_params=pltpu.CompilerParams(vmem_limit_bytes=48 * 1024 * 1024),
    )(xall, dyall, gt, h, da, db)


def solution(mesh):
    def local_step(x_tokens, expert_idx, gate_vals, dy_tokens, w_gate, w_up, w_down, x_attn, w_query, w_key, w_value, w_out):
        wqkv = jnp.concatenate([w_query.reshape(D, 128), w_key.reshape(D, 64), w_value.reshape(D, 64)], axis=1)
        wo = w_out.reshape(128, D)
        y_t, dx_t, dg, at, xall, dyall, h, da, db, gt = exchange(
            x_tokens, dy_tokens, x_attn.reshape(ROWS, D), expert_idx, gate_vals, w_gate, w_up, w_down, wqkv, wo)
        dwg, dwu, dwd = weight_grads(xall, dyall, gt, h, da, db)
        return y_t, dx_t, dg, dwg, dwu, dwd, at.reshape(1, ROWS, D)

    spec_rows = P(TOKEN_AXES, None)
    spec_seqs = P(TOKEN_AXES, None, None)
    spec_experts = P(GROUP_AXES, None, None)
    spec_heads = P(None, GROUP_AXES, None)
    return jax.shard_map(local_step, mesh=mesh,
                         in_specs=(spec_rows, spec_rows, spec_rows, spec_rows, spec_experts, spec_experts, spec_experts, spec_seqs, spec_heads, spec_heads, spec_heads, spec_experts),
                         out_specs=(spec_rows, spec_rows, spec_rows, spec_seqs, spec_seqs, spec_seqs, spec_seqs),
                         check_vma=False)
```

time: 510 us -> 90.1 us (0.18)
  waiting for transfers between devices: 299 us -> 0 us
  Pallas kernels: 0 us -> 73.5 us
  local copies, waits for them, and re-layouts: 80 us -> 14.4 us
  matrix products: 58.5 us -> 0 us
  starting transfers between devices: 42.8 us -> 0 us
  between operations: 14.5 us -> 0.67 us
  other arithmetic: 14.4 us -> 0.97 us
    all_to_all x8 -> x0, waiting for transfers between devices: 298 us -> none  [the longest x2 84.3 us: from_experts(): buffer = lax.all_to_all(buffer, 'ei', 0, 0, tiled=True)]
    pallas_call x0 -> x2, Pallas kernels: none -> 73.5 us  [the longest x1 62.1 us: exchange(): pl.pallas_call(exchange_kernel, name='exchange', out_shape=[sds((ROWS, D)...]
    dot_general x14 -> x0, matrix products: 58.5 us -> none  [the longest x1 8.12 us: expert_backward(): jnp.einsum('secd,secf->edf', x_slots, d_pre_gate, preferred_element_type=...]
    all_to_all x8 -> x0, starting transfers between devices: 42.5 us -> none  [the longest x2 11.4 us: to_experts(): buffer = lax.all_to_all(buffer, 'ei', 0, 0, tiled=True)]
    all_to_all x8 -> x0, local copies, waits for them, and re-layouts: 35 us -> none  [the longest x2 9.83 us: to_experts(): buffer = lax.all_to_all(buffer, 'eo', 1, 1, tiled=True)]
    gather x4 -> x0, local copies, waits for them, and re-layouts: 30.1 us -> none  [the longest x1 9.61 us: local_step(): jnp.take(jnp.concatenate([x_tokens, zero_row]), src_tok, axis=0)]
    unnamed x44 -> x22, local copies, waits for them, and re-layouts: 4.96 us -> 13.3 us
    select_n x3 -> x0, other arithmetic: 7.75 us -> none  [the longest x1 3.87 us: local_step(): jnp.take(jnp.concatenate([x_tokens, zero_row]), src_tok, axis=0)]
  transfers between devices with their start and end apart: 10 -> 0, of which waited for: 8 -> 0; matrix products, arithmetic and copies ran while one was open for 18% -> 0% of each run, Pallas kernels for 0% -> 0%
where the time goes in v1:
time: 90.1 us; the launch traced here: 89.5 us
  Pallas kernels  73.5 us (82%)
  local copies, waits for them, and re-layouts  14.4 us (16%)
  other arithmetic  0.97 us (1%)
    pallas_call x1, Pallas kernels, exchange(): pl.pallas_call(exchange_kernel, name='exchange', out_shape=[sds((ROWS, D)...  62.1 us
    unnamed x22, local copies, waits for them, and re-layouts  13.3 us
    pallas_call x1, Pallas kernels, weight_grads(): pl.pallas_call(grads_kernel, name='weight_grads', grid=(EXP,), out_shape=...  11.4 us

profile of v1, /device:TPU:0, one launch (start us, length us, event | category | flops | bytes accessed | tf_op | source)
XLA Modules:
  0.0 89.5 jit_solution(7590347201056700819)
XLA Ops:
  0.6 1.4 %copy.28.idx_ref = s32[64,8]{1,0:T(8,128)} copy(s32[64,8]{0,1:T(8,128)} %param.13) | data formatting | bytes 4096 | tf_op args[1]
  2.0 1.4 %copy.29.gate_ref = f32[64,8]{1,0:T(8,128)} copy(f32[64,8]{0,1:T(8,128)} %param.14) | data formatting | bytes 4096 | tf_op args[2]
  3.4 1.1 %copy.27 = bf16[1024,128]{1,0:T(8,128)(2,1)S(1)} copy(bf16[1024,128]{0,1:T(8,128)(2,1)} %bitcast.8) | data formatting | bytes 524288 | tf_op jit(solution)/shard_map/reshape | solution.py:398
  4.5 1.1 %copy.25 = bf16[1024,1,64]{2,0,1:T(8,128)(2,1)S(1)} copy(bf16[1024,1,64]{0,2,1:T(8,128)(2,1)} %param.21) | data formatting | bytes 262144 | tf_op args[9]
  5.6 1.1 %copy.26 = bf16[1024,1,64]{2,0,1:T(8,128)(2,1)S(1)} copy(bf16[1024,1,64]{0,2,1:T(8,128)(2,1)} %param.22) | data formatting | bytes 262144 | tf_op args[10]
  6.7 1.0 %pad_maximum_fusion.wqkv_hbm = bf16[1024,256]{1,0:T(8,128)(2,1)} fusion(bf16[1024,64]{1,0:T(8,128)(2,1)S(1)} %bitcast.7, bf16[1024,64]{1,0:T(8,128)(2,1)S(1)} %bitcast.6, bf16[1024,128]{1,0:T(8,128)(2,1)S(1)} %copy.27), kind=kLoop, calls=%fused_computation | loop fusion | flops 1572864 | bytes 1048576 | tf_op jit(solution)/shard_map/concatenate | solution.py:398
  7.7 62.1 %exchange.1 = (bf16[64,1024]{1,0:T(8,128)(2,1)}, bf16[64,1024]{1,0:T(8,128)(2,1)}, f32[64,8]{1,0:T(8,128)}, bf16[64,1024]{1,0:T(8,128)(2,1)}, bf16[512,1024]{1,0...) custom-call(bf16[64,1024]{1,0:T(8,128)(2,1)} %x_hbm.1, ...), custom_call_target="tpu_custom_call" | custom-call | tf_op jit(solution)/shard_map/exchange/pallas_call | solution.py:336
  69.8 1.4 %copy.30 = f32[64,8]{0,1:T(8,128)} copy(f32[64,8]{1,0:T(8,128)} %get-tuple-element.42) | data formatting | bytes 4096
  71.2 0.0 copy-start
  71.2 1.6 %copy-done = bf16[4,512,512]{2,1,0:T(8,128)(2,1)S(1)} copy-done((bf16[4,512,512]{2,1,0:T(8,128)(2,1)S(1)}, bf16[4,512,512]{2,1,0:T(8,128)(2,1)}, u32[]{:S(2)}) %copy-start) | copy-done | bytes 2097176
  72.8 0.0 copy-start.1
  72.8 1.2 %copy-done.1 = bf16[512,1024]{1,0:T(8,128)(2,1)S(1)} copy-done((bf16[512,1024]{1,0:T(8,128)(2,1)S(1)}, bf16[512,1024]{1,0:T(8,128)(2,1)}, u32[]{:S(2)}) %copy-start.1) | copy-done | bytes 1048600
  74.0 0.0 copy-start.2
  74.0 1.2 %copy-done.2 = bf16[512,1024]{1,0:T(8,128)(2,1)S(1)} copy-done((bf16[512,1024]{1,0:T(8,128)(2,1)S(1)}, bf16[512,1024]{1,0:T(8,128)(2,1)}, u32[]{:S(2)}) %copy-start.2) | copy-done | bytes 1048600
  75.2 0.0 copy-start.3
  75.2 0.9 %copy-done.3 = f32[512,128]{1,0:T(8,128)S(1)} copy-done((f32[512,128]{1,0:T(8,128)S(1)}, f32[512,128]{1,0:T(8,128)}, u32[]{:S(2)}) %copy-start.3) | copy-done | bytes 262168
  76.2 0.0 copy-start.6
  76.2 0.0 copy-start.5
  76.2 0.0 copy-start.4
  76.2 11.4 %weight_grads.1 = (f32[4,1024,512]{2,1,0:T(8,128)}, f32[4,1024,512]{2,1,0:T(8,128)}, f32[4,512,1024]{2,1,0:T(8,128)}) custom-call(bf16[512,1024]{1,0:T(8,128)(2,1)S(1)} %copy-done.1, bf16[512,1024]{1,0:T(8,128)(2,1)S(1)} %copy-done.2, f32[512,128]{1,0:T(8,128)S(1)} %copy-done.3, bf16[4,512,512]{2,1,0:T(8,128)(2,1)S(1)} %copy-done, ...), custom_call_target="tpu_custom_call" | custom-call | tf_op jit(solution)/shard_map/weight_grads/pallas_call | solution.py:384
  87.6 0.0 copy-done.6
  87.6 0.7 copy.34
  88.2 0.0 copy-done.5
  88.2 0.7 copy.35
  88.9 0.0 copy-done.4
  88.9 0.7 copy.36
Async XLA Ops:
  71.2 1.6 %copy-start = (bf16[4,512,512]{2,1,0:T(8,128)(2,1)S(1)}, bf16[4,512,512]{2,1,0:T(8,128)(2,1)}, u32[]{:S(2)}) copy-start(bf16[4,512,512]{2,1,0:T(8,128)(2,1)} %get-tuple-element.26.h_ref) | copy-start | bytes 6291460
  72.8 1.2 %copy-start.1 = (bf16[512,1024]{1,0:T(8,128)(2,1)S(1)}, bf16[512,1024]{1,0:T(8,128)(2,1)}, u32[]{:S(2)}) copy-start(bf16[512,1024]{1,0:T(8,128)(2,1)} %get-tuple-element.23.x_ref) | copy-start | bytes 3145732
  74.0 1.2 %copy-start.2 = (bf16[512,1024]{1,0:T(8,128)(2,1)S(1)}, bf16[512,1024]{1,0:T(8,128)(2,1)}, u32[]{:S(2)}) copy-start(bf16[512,1024]{1,0:T(8,128)(2,1)} %get-tuple-element.24.dy_ref) | copy-start | bytes 3145732
  75.2 0.9 %copy-start.3 = (f32[512,128]{1,0:T(8,128)S(1)}, f32[512,128]{1,0:T(8,128)}, u32[]{:S(2)}) copy-start(f32[512,128]{1,0:T(8,128)} %get-tuple-element.25.gt_ref) | copy-start | bytes 786436
  76.2 11.4 %copy-start.6 = (bf16[64,1024]{1,0:T(8,128)(2,1)S(1)}, bf16[64,1024]{1,0:T(8,128)(2,1)}, u32[]{:S(2)}) copy-start(bf16[64,1024]{1,0:T(8,128)(2,1)} %get-tuple-element.54) | copy-start | bytes 393220
  76.2 12.1 %copy-start.5 = (bf16[64,1024]{1,0:T(8,128)(2,1)S(1)}, bf16[64,1024]{1,0:T(8,128)(2,1)}, u32[]{:S(2)}) copy-start(bf16[64,1024]{1,0:T(8,128)(2,1)} %get-tuple-element.55) | copy-start | bytes 393220
  76.2 12.7 %copy-start.4 = (bf16[64,1024]{1,0:T(8,128)(2,1)S(1)}, bf16[64,1024]{1,0:T(8,128)(2,1)}, u32[]{:S(2)}) copy-start(bf16[64,1024]{1,0:T(8,128)(2,1)} %get-tuple-element.32) | copy-start | bytes 393220

commit v2 on v1

--- a/solution.py
+++ b/solution.py
@@ -28,10 +28,10 @@
 TN = (((0,), (0,)), ((), ()))
 
 
-def exchange_kernel(x_hbm, dy_hbm, xa_hbm, idx_ref, gate_ref, wg_hbm, wu_hbm, wd_hbm, wqkv_hbm, wo_hbm,
+def exchange_kernel(x_hbm, dy_hbm, xa_hbm, idx_ref, gate_ref, wg_hbm, wu_hbm, wd_hbm, wq_hbm, wk_hbm, wv_hbm, wo_hbm,
                     y_out, dx_out, dg_out, at_out, xall_out, dyall_out, h_out, da_out, db_out, gt_out,
-                    rows, wg, wu, wd, wqkv, wo, hid, dag, dbg, act, gfac, gt, gpad, gsend, grecv,
-                    dgs, dsend, drecv, dpad,
+                    rows, wg, wu, wd, wqkv, wo, hid, dag, dbg, act, gfac, gt, gsend, grecv,
+                    dgs, dsend, drecv,
                     part, pair, s1, r1, s2, r2,
                     in_sem, w_sem, out_sem, gs_sem, gr_sem, rs_s, rs_r, ag_s, ag_r, dd_s, dd_r):
     y = lax.axis_index('ei')
@@ -63,26 +63,27 @@
            for t, src in ((XA, xa_hbm), (XT, x_hbm), (DY, dy_hbm))]
     for cp in ins:
         cp.start()
-    wload = [pltpu.make_async_copy(wqkv_hbm, wqkv, w_sem.at[0]), pltpu.make_async_copy(wo_hbm, wo, w_sem.at[1])]
+    wload = [pltpu.make_async_copy(wq_hbm, wqkv.at[0:128], w_sem.at[0]),
+             pltpu.make_async_copy(wk_hbm, wqkv.at[128:192], w_sem.at[1]),
+             pltpu.make_async_copy(wv_hbm, wqkv.at[192:256], w_sem.at[2]),
+             pltpu.make_async_copy(wo_hbm, wo, w_sem.at[3])]
     for n, (src, dst) in enumerate(((wg_hbm, wg), (wu_hbm, wu), (wd_hbm, wd))):
         for e in range(EXP):
-            wload.append(pltpu.make_async_copy(src.at[e], dst.at[e], w_sem.at[2 + n * EXP + e]))
+            wload.append(pltpu.make_async_copy(src.at[e], dst.at[e], w_sem.at[4 + n * EXP + e]))
     for cp in wload:
         cp.start()
 
-    lane = lax.broadcasted_iota(jnp.int32, (ROWS, 128), 1)
-    lane_exp = (lane // 8) * 4 + lane % 4
-    is_gate = (lane % 8) < 4
-    in_range = lane < 64
-    table = jnp.zeros((ROWS, 128), F32)
+    row = lax.broadcasted_iota(jnp.int32, (64, ROWS), 0)
+    row_exp = (row // 8) * 4 + row % 4
+    is_gate = (row % 8) < 4
+    table = jnp.zeros((64, ROWS), F32)
     for j in range(TOPK):
-        hit = (lane_exp == idx_ref[:, j:j + 1]) & in_range
-        table = table + jnp.where(hit, jnp.where(is_gate, gate_ref[:, j:j + 1], 1.0), 0.0)
-    gpad[...] = jnp.zeros((128, 128), F32)
-    gpad[pl.ds(pl.multiple_of(c * ROWS, ROWS), ROWS), :] = table
-    table_t = gpad[...].T
+        hit = row_exp == idx_ref[j:j + 1, :]
+        table = table + jnp.where(hit, jnp.where(is_gate, gate_ref[j:j + 1, :], 1.0), 0.0)
+    blank = jnp.zeros((64, ROWS), F32)
+    wide = jnp.where(c == 0, jnp.concatenate([table, blank], axis=1), jnp.concatenate([blank, table], axis=1))
     for d in range(8):
-        gsend[d] = table_t[d * 8:(d + 1) * 8, :]
+        gsend[d] = wide[d * 8:(d + 1) * 8, :]
     grecv[me] = gsend[me]
     dgs[...] = jnp.zeros((TOK, 128), F32)
     part[1] = jnp.zeros(part.shape[1:], F32)
@@ -198,14 +199,14 @@
 
     ag_done(XA)
 
-    wload[0].wait()
-    wload[1].wait()
+    for cp in wload[:4]:
+        cp.wait()
     causal_r = lax.broadcasted_iota(jnp.int32, (256, 128), 0) % 128
     causal_c = lax.broadcasted_iota(jnp.int32, (256, 128), 1)
     keep = (causal_r >= causal_c) & (causal_r // 64 == causal_c // 64)
     for q in range(4):
         xs = rows[XA, q * 128:(q + 1) * 128, :]
-        qkv = jnp.dot(xs, wqkv[...], preferred_element_type=F32).astype(BF)
+        qkv = lax.dot_general(xs, wqkv[...], NT, preferred_element_type=F32).astype(BF)
         qs = jnp.concatenate([qkv[:, 0:64], qkv[:, 64:128]], axis=0)
         sc = lax.dot_general(qs, qkv[:, 128:192], NT, preferred_element_type=F32) * (64 ** -0.5)
         sc = jnp.where(keep, sc, -1e30)
@@ -230,7 +231,7 @@
             pltpu.make_async_copy(gt, gt_out, out_sem.at[2])]
     for cp in outs:
         cp.start()
-    for cp in wload[2:]:
+    for cp in wload[4:]:
         cp.wait()
     lane_t = lax.broadcasted_iota(jnp.int32, (256, 128), 1)
 
@@ -305,15 +306,11 @@
     rs_final(1, y_out)
     for cp in dg_cps:
         cp.wait_recv()
-    dpad[...] = jnp.zeros((128, 128), F32)
-    for d in range(8):
-        dpad[d * 8:(d + 1) * 8, :] = drecv[d]
-    gpad[...] = dpad[...].T
-    mine = gpad[pl.ds(pl.multiple_of(c * ROWS, ROWS), ROWS), :]
+    both = drecv[...].reshape(64, 128)
+    mine = jnp.where(c == 0, both[:, 0:ROWS], both[:, ROWS:128])
     for j in range(TOPK):
-        ij = idx_ref[:, j:j + 1]
-        hit = lane == (ij // 4) * 8 + ij % 4
-        dg_out[:, j:j + 1] = jnp.sum(jnp.where(hit, mine, 0.0), axis=1, keepdims=True)
+        hit = row_exp == idx_ref[j:j + 1, :]
+        dg_out[j:j + 1, :] = jnp.sum(jnp.where(hit & is_gate, mine, 0.0), axis=0, keepdims=True)
     rs_stage2(2)
     rs_final(2, dx_out)
 
@@ -328,7 +325,7 @@
             cp.wait_send()
 
 
-def exchange(x, dy, xa, idx, gates, wg, wu, wd, wqkv, wo):
+def exchange(x, dy, xa, idx, gates, wg, wu, wd, wq, wk, wv, wo):
     any_spec = pl.BlockSpec(memory_space=pl.ANY)
     vmem = pl.BlockSpec(memory_space=pltpu.VMEM)
     sds = jax.ShapeDtypeStruct
@@ -336,38 +333,42 @@
     return pl.pallas_call(
         exchange_kernel,
         name='exchange',
-        out_shape=[sds((ROWS, D), BF), sds((ROWS, D), BF), sds((ROWS, TOPK), F32), sds((ROWS, D), BF),
+        out_shape=[sds((ROWS, D), BF), sds((ROWS, D), BF), sds((TOPK, ROWS), F32), sds((ROWS, D), BF),
                    sds((TOK, D), BF), sds((TOK, D), BF),
                    sds((EXP, TOK, FF), BF), sds((EXP, TOK, FF), BF), sds((EXP, TOK, FF), BF), sds((TOK, 128), F32)],
-        in_specs=[any_spec, any_spec, any_spec, vmem, vmem] + [any_spec] * 5,
+        in_specs=[any_spec, any_spec, any_spec, vmem, vmem] + [any_spec] * 7,
         out_specs=[vmem] * 4 + [any_spec] * 6,
         scratch_shapes=[
             pltpu.VMEM((3, TOK, D), BF),
             pltpu.VMEM((EXP, D, FF), BF), pltpu.VMEM((EXP, D, FF), BF), pltpu.VMEM((EXP, FF, D), BF),
-            pltpu.VMEM((D, 256), BF), pltpu.VMEM((128, D), BF),
+            pltpu.VMEM((256, D), BF), pltpu.VMEM((128, D), BF),
             pltpu.VMEM((EXP, TOK, FF), BF), pltpu.VMEM((EXP, TOK, FF), BF), pltpu.VMEM((EXP, TOK, FF), BF),
             pltpu.VMEM((EXP, TOK, FF), F32), pltpu.VMEM((EXP, TOK, FF), F32),
-            pltpu.VMEM((TOK, 128), F32), pltpu.VMEM((128, 128), F32),
+            pltpu.VMEM((TOK, 128), F32),
             pltpu.VMEM((8, 8, 128), F32), pltpu.VMEM((8, 8, 128), F32),
             pltpu.VMEM((TOK, 128), F32), pltpu.VMEM((4, 8, 128), F32), pltpu.VMEM((8, 8, 128), F32),
-            pltpu.VMEM((128, 128), F32),
             pltpu.VMEM((3, 2, 2, 4, ROWS, HALF), F32), pltpu.VMEM((3, 2, 4, ROWS, HALF), F32),
             pltpu.VMEM((3, 2, 2, ROWS, HALF), F32), pltpu.VMEM((3, 2, 2, ROWS, HALF), F32),
             pltpu.VMEM((3, 2, ROWS, HALF), F32), pltpu.VMEM((3, 2, ROWS, HALF), F32),
-            dma((3,)), dma((2 + 3 * EXP,)), dma((3 + 3 * EXP,)), dma((7,)), dma((7,)),
+            dma((3,)), dma((4 + 3 * EXP,)), dma((3 + 3 * EXP,)), dma((7,)), dma((7,)),
             dma((3, RS_COPIES)), dma((3, RS_COPIES)), dma((3, GATHER_COPIES)), dma((3, GATHER_COPIES)),
             dma((7,)), dma((7,)),
         ],
         compiler_params=pltpu.CompilerParams(collective_id=0, has_side_effects=True, vmem_limit_bytes=60 * 1024 * 1024),
-    )(x, dy, xa, idx, gates, wg, wu, wd, wqkv, wo)
-
-
-def grads_kernel(x_ref, dy_ref, gt_ref, h_ref, da_ref, db_ref, dwg_ref, dwu_ref, dwd_ref, xt):
+    )(x, dy, xa, idx, gates, wg, wu, wd, wq, wk, wv, wo)
+
+
+def grads_kernel(x_ref, dy_ref, gt_ref, h_ref, da_ref, db_ref, y_in, dx_in, at_in, dg_in,
+                 dwg_ref, dwu_ref, dwd_ref, y_out, dx_out, at_out, dg_out, xt):
     e = pl.program_id(0)
 
     @pl.when(e == 0)
     def _():
         xt[...] = x_ref[...].T
+        y_out[...] = y_in[...]
+        dx_out[...] = dx_in[...]
+        at_out[...] = at_in[...]
+        dg_out[...] = dg_in[...]
 
     dwg_ref[0] = jnp.dot(xt[...], da_ref[0], preferred_element_type=F32)
     dwu_ref[0] = jnp.dot(xt[...], db_ref[0], preferred_element_type=F32)
@@ -377,7 +378,7 @@
     dwd_ref[0] = lax.dot_general(h_ref[0], do, TN, preferred_element_type=F32)
 
 
-def weight_grads(xall, dyall, gt, h, da, db):
+def weight_grads(xall, dyall, gt, h, da, db, y_t, dx_t, at, dg):
     sds = jax.ShapeDtypeStruct
     whole = lambda shape: pl.BlockSpec(shape, lambda e: (0, 0))
     per = lambda a, b: pl.BlockSpec((1, a, b), lambda e: (e, 0, 0))
@@ -385,22 +386,24 @@
         grads_kernel,
         name='weight_grads',
         grid=(EXP,),
-        out_shape=[sds((EXP, D, FF), F32), sds((EXP, D, FF), F32), sds((EXP, FF, D), F32)],
-        in_specs=[whole((TOK, D)), whole((TOK, D)), whole((TOK, 128)), per(TOK, FF), per(TOK, FF), per(TOK, FF)],
-        out_specs=[per(D, FF), per(D, FF), per(FF, D)],
+        out_shape=[sds((EXP, D, FF), F32), sds((EXP, D, FF), F32), sds((EXP, FF, D), F32),
+                   sds((ROWS, D), BF), sds((ROWS, D), BF), sds((ROWS, D), BF), sds((TOPK, ROWS), F32)],
+        in_specs=[whole((TOK, D)), whole((TOK, D)), whole((TOK, 128)), per(TOK, FF), per(TOK, FF), per(TOK, FF)]
+        + [whole((ROWS, D))] * 3 + [whole((TOPK, ROWS))],
+        out_specs=[per(D, FF), per(D, FF), per(FF, D)] + [whole((ROWS, D))] * 3 + [whole((TOPK, ROWS))],
         scratch_shapes=[pltpu.VMEM((D, TOK), BF)],
-        compiler_params=pltpu.CompilerParams(vmem_limit_bytes=48 * 1024 * 1024),
-    )(xall, dyall, gt, h, da, db)
+        compiler_params=pltpu.CompilerParams(vmem_limit_bytes=62 * 1024 * 1024),
+    )(xall, dyall, gt, h, da, db, y_t, dx_t, at, dg)
 
 
 def solution(mesh):
     def local_step(x_tokens, expert_idx, gate_vals, dy_tokens, w_gate, w_up, w_down, x_attn, w_query, w_key, w_value, w_out):
-        wqkv = jnp.concatenate([w_query.reshape(D, 128), w_key.reshape(D, 64), w_value.reshape(D, 64)], axis=1)
-        wo = w_out.reshape(128, D)
-        y_t, dx_t, dg, at, xall, dyall, h, da, db, gt = exchange(
-            x_tokens, dy_tokens, x_attn.reshape(ROWS, D), expert_idx, gate_vals, w_gate, w_up, w_down, wqkv, wo)
-        dwg, dwu, dwd = weight_grads(xall, dyall, gt, h, da, db)
-        return y_t, dx_t, dg, dwg, dwu, dwd, at.reshape(1, ROWS, D)
+        y_p, dx_p, dg_p, at_p, xall, dyall, h, da, db, gt = exchange(
+            x_tokens, dy_tokens, x_attn.reshape(ROWS, D), expert_idx.T, gate_vals.T, w_gate, w_up, w_down,
+            w_query.transpose(1, 2, 0).reshape(128, D), w_key.transpose(1, 2, 0).reshape(64, D),
+            w_value.transpose(1, 2, 0).reshape(64, D), w_out.reshape(128, D))
+        dwg, dwu, dwd, y_t, dx_t, at, dg = weight_grads(xall, dyall, gt, h, da, db, y_p, dx_p, at_p, dg_p)
+        return y_t, dx_t, dg.T, dwg, dwu, dwd, at.reshape(1, ROWS, D)
 
     spec_rows = P(TOKEN_AXES, None)
     spec_seqs = P(TOKEN_AXES, None, None)

time: 90.1 us -> 76.7 us (0.85)
  local copies, waits for them, and re-layouts: 14.4 us -> 0 us
  Pallas kernels: 73.5 us -> 75.8 us
  other arithmetic: 0.97 us -> 0 us
    unnamed x22 -> x0, local copies, waits for them, and re-layouts: 13.3 us -> none
    pallas_call x1, Pallas kernels: 11.4 us -> 13 us  [weight_grads(): pl.pallas_call(grads_kernel, name='weight_grads', grid=(EXP,), out_shape=...]
    reshape x1 -> x0, local copies, waits for them, and re-layouts: 1.12 us -> none  [local_step(): w_query.reshape(D, 128)]
    concatenate x1 -> x0, other arithmetic: 0.97 us -> none  [local_step(): jnp.concatenate([w_query.reshape(D, 128), w_key.reshape(D, 64), w_value.r...]
where the time goes in v2:
time: 76.7 us; the launch traced here: 76.4 us
  Pallas kernels  75.8 us (99%)
    pallas_call x1, Pallas kernels, exchange(): pl.pallas_call(exchange_kernel, name='exchange', out_shape=[sds((ROWS, D)...  62.8 us
    pallas_call x1, Pallas kernels, weight_grads(): pl.pallas_call(grads_kernel, name='weight_grads', grid=(EXP,), out_shape=...  13 us

profile of v2, /device:TPU:0, one launch (start us, length us, event | category | flops | bytes accessed | tf_op | source)
XLA Modules:
  0.0 76.4 jit_solution(11107088195040337861)
XLA Ops:
  0.6 62.8 %exchange.1 = (bf16[64,1024]{1,0:T(8,128)(2,1)}, bf16[64,1024]{1,0:T(8,128)(2,1)}, f32[8,64]{1,0:T(8,128)}, bf16[64,1024]{1,0:T(8,128)(2,1)}, bf16[512,1024]{1,0...) custom-call(bf16[64,1024]{1,0:T(8,128)(2,1)} %x_hbm.1, ...), custom_call_target="tpu_custom_call" | custom-call | tf_op jit(solution)/shard_map/exchange/pallas_call | solution.py:333
  63.4 13.0 %weight_grads.1 = (f32[4,1024,512]{2,1,0:T(8,128)}, f32[4,1024,512]{2,1,0:T(8,128)}, f32[4,512,1024]{2,1,0:T(8,128)}, bf16[64,1024]{1,0:T(8,128)(2,1)}, bf16[64,...) custom-call(bf16[512,1024]{1,0:T(8,128)(2,1)} %get-tuple-element.24.x_ref, ...), custom_call_target="tpu_custom_call" | custom-call | tf_op jit(solution)/shard_map/weight_grads/pallas_call | solution.py:385

commit v3 on v2

v3 whole, which is shorter than its diff:
```python
import functools

import jax
import jax.numpy as jnp
from jax import lax
from jax.experimental import pallas as pl
from jax.experimental.pallas import tpu as pltpu
from jax.sharding import PartitionSpec as P

MESH = pl.DeviceIdType.MESH
GROUP_AXES = ('ei', 'eo')
TOKEN_AXES = ('dp', 'ei', 'eo')
BF = jnp.bfloat16
F32 = jnp.float32

ROWS = 64
TOK = 512
D = 1024
FF = 512
HALF = 512
EXP = 4
TOPK = 8
GATHER_COPIES = 11
RS_COPIES = 14
XA, XT, DY = 0, 1, 2

NT = (((1,), (1,)), ((), ()))
TN = (((0,), (0,)), ((), ()))


def exchange_kernel(x_hbm, dy_hbm, xa_hbm, idx_ref, gate_ref, wg_hbm, wu_hbm, wd_hbm, wq_hbm, wk_hbm, wv_hbm, wo_hbm,
                    y_out, dg_out, tox_out, toy_out, own_out, xall_out, dyall_out, h_out, da_out, db_out, gt_out,
                    rows, wg, wu, wd, wqkv, wo, hid, osv, dag, dbg, act, gfac, gt, gsend, grecv,
                    dgs, dsend, drecv,
                    sums, part, pair, s1, r1, s2, r2,
                    in_sem, w_sem, out_sem, gs_sem, gr_sem, rs_s, rs_r, ag_s, ag_r, dd_s, dd_r):
    y = lax.axis_index('ei')
    o = lax.axis_index('eo')
    z = lax.axis_index('dp')
    x = o // 2
    c = o % 2
    me = y * 4 + o
    q0 = 2 * y + x
    qx = 2 * y + (1 - x)
    qy = 2 * (1 - y) + x
    qd = 2 * (1 - y) + (1 - x)

    def dev(fx, fy, fc):
        xx = (1 - x) if fx else x
        yy = (1 - y) if fy else y
        cc = (1 - c) if fc else c
        return (z, yy, xx * 2 + cc)

    sib, xn, yn = dev(0, 0, 1), dev(1, 0, 0), dev(0, 1, 0)
    rels = [(fx, fy, fc) for fx in (0, 1) for fy in (0, 1) for fc in (0, 1) if fx or fy or fc]

    barrier = pltpu.get_barrier_semaphore()
    for rel in rels:
        pl.semaphore_signal(barrier, inc=1, device_id=dev(*rel), device_id_type=MESH)

    own = pl.ds(pl.multiple_of(me * ROWS, ROWS), ROWS)
    ins = [pltpu.make_async_copy(src, rows.at[t, own], in_sem.at[t])
           for t, src in ((XT, x_hbm), (DY, dy_hbm), (XA, xa_hbm))]
    for cp in ins:
        cp.start()

    def expert_load(e):
        return [pltpu.make_async_copy(src.at[e], dst.at[e], w_sem.at[4 + n * EXP + e])
                for n, (src, dst) in enumerate(((wg_hbm, wg), (wu_hbm, wu), (wd_hbm, wd)))]

    for e in range(EXP):
        for cp in expert_load(e):
            cp.start()
    wload = [pltpu.make_async_copy(wq_hbm, wqkv.at[0:128], w_sem.at[0]),
             pltpu.make_async_copy(wk_hbm, wqkv.at[128:192], w_sem.at[1]),
             pltpu.make_async_copy(wv_hbm, wqkv.at[192:256], w_sem.at[2]),
             pltpu.make_async_copy(wo_hbm, wo, w_sem.at[3])]
    for cp in wload:
        cp.start()

    row = lax.broadcasted_iota(jnp.int32, (64, ROWS), 0)
    row_exp = (row // 8) * 4 + row % 4
    is_gate = (row % 8) < 4
    table = jnp.zeros((64, ROWS), F32)
    for j in range(TOPK):
        hit = row_exp == idx_ref[j:j + 1, :]
        table = table + jnp.where(hit, jnp.where(is_gate, gate_ref[j:j + 1, :], 1.0), 0.0)
    blank = jnp.zeros((64, ROWS), F32)
    wide = jnp.where(c == 0, jnp.concatenate([table, blank], axis=1), jnp.concatenate([blank, table], axis=1))
    for d in range(8):
        gsend[d] = wide[d * 8:(d + 1) * 8, :]
    grecv[me] = gsend[me]
    dgs[...] = jnp.zeros((TOK, 128), F32)
    part[1] = jnp.zeros(part.shape[1:], F32)
    part[2] = jnp.zeros(part.shape[1:], F32)

    def blk(t, q, off=0, n=ROWS):
        return rows.at[t, pl.ds(pl.multiple_of(q * 128 + c * ROWS + off, 32), n)]

    def remote(src, dst, ss, rs, where):
        return pltpu.make_async_remote_copy(src, dst, ss, rs, device_id=where, device_id_type=MESH)

    hr = ROWS // 2

    def gather_copies(t):
        def cp(k, ref, where):
            return remote(ref, ref, ag_s.at[t, k], ag_r.at[t, k], where)
        return [cp(0, blk(t, q0), sib),
                cp(1, blk(t, q0, 0, hr), xn), cp(2, blk(t, q0, hr, hr), xn),
                cp(3, blk(t, q0, hr, hr), yn), cp(4, blk(t, q0, 0, hr), yn),
                cp(5, blk(t, qx, 0, hr), yn), cp(6, blk(t, qy, hr, hr), xn),
                cp(7, blk(t, qx), sib), cp(8, blk(t, qy), sib),
                cp(9, blk(t, qd, 0, hr), sib), cp(10, blk(t, qd, hr, hr), sib)]

    ag = [gather_copies(t) for t in range(3)]

    def ag_own(t):
        for k in (1, 3, 2, 4, 0):
            ag[t][k].start()

    def ag_forward(t):
        ag[t][1].wait_recv()
        ag[t][5].start()
        ag[t][3].wait_recv()
        ag[t][6].start()

    def ag_pair(t):
        ag[t][2].wait_recv()
        ag[t][7].start()
        ag[t][4].wait_recv()
        ag[t][8].start()

    def ag_last(t):
        ag[t][5].wait_recv()
        ag[t][9].start()
        ag[t][6].wait_recv()
        ag[t][10].start()

    def ag_wait(t, *ks):
        for k in ks:
            ag[t][k].wait_recv()

    def tile_copies(send, recv, ss, rs, chip_tiles):
        cps = {}
        for k, (fx, fy, fc) in enumerate(rels):
            where = dev(fx, fy, fc)
            qq = 2 * where[1] + where[2] // 2
            src = send.at[qq] if chip_tiles else send.at[where[1] * 4 + where[2]]
            cps[fx, fy, fc] = remote(src, recv.at[me], ss.at[k], rs.at[k], where)
        return cps

    gate_cps = tile_copies(gsend, grecv, gs_sem, gr_sem, False)
    dg_cps = tile_copies(dsend, drecv, dd_s, dd_r, True)
    chips = (q0, qx, qy, qd)
    OWN, X, Y, DI = 0, 1, 2, 3
    first = (X, Y)
    second = (Y, X)

    def rs_copies(n):
        def cp(k, src, dst, where):
            return remote(src, dst, rs_s.at[n, k], rs_r.at[n, k], where)
        cps = [cp(2 * k + h, part.at[n, 1 - c, h, chips[k]], pair.at[n, h, chips[k]], sib) for k in range(4) for h in range(2)]
        for h in range(2):
            one, two = (xn, yn) if h == 0 else (yn, xn)
            cps += [cp(8 + 3 * h, s1.at[n, h, 0], r1.at[n, h, 0], one), cp(9 + 3 * h, s1.at[n, h, 1], r1.at[n, h, 1], one),
                    cp(10 + 3 * h, s2.at[n, h], r2.at[n, h], two)]
        return cps

    rsc = [rs_copies(n) for n in range(3)]

    def rs_pair(n, k):
        rsc[n][2 * k].start()
        rsc[n][2 * k + 1].start()

    def chip_sum(n, h, k):
        return part[n, c, h, chips[k]] + pair[n, h, chips[k]]

    def rs_far(n):
        for h in range(2):
            rsc[n][2 * DI + h].wait_recv()
            s1[n, h, 0] = chip_sum(n, h, DI)
            rsc[n][8 + 3 * h].start()

    def rs_near(n, h):
        k = first[h]
        rsc[n][2 * k + h].wait_recv()
        s1[n, h, 1] = chip_sum(n, h, k)
        rsc[n][9 + 3 * h].start()

    def rs_second(n):
        for h in range(2):
            k = second[h]
            rsc[n][2 * k + h].wait_recv()
            rsc[n][8 + 3 * h].wait_recv()
            s2[n, h] = chip_sum(n, h, k) + r1[n, h, 0]
            rsc[n][10 + 3 * h].start()

    def rs_final(n, out_ref):
        for h in range(2):
            rsc[n][2 * OWN + h].wait_recv()
            rsc[n][9 + 3 * h].wait_recv()
            rsc[n][10 + 3 * h].wait_recv()
            total = chip_sum(n, h, OWN) + r1[n, h, 1] + r2[n, h]
            out_ref[:, h * HALF:(h + 1) * HALF] = total.astype(BF)

    def gate_table(k):
        fx, fy = k % 2, k // 2
        for fc in (0, 1):
            if (fx, fy, fc) in gate_cps:
                gate_cps[fx, fy, fc].wait_recv()
        q = chips[k]
        tile = grecv[2 * q] + grecv[2 * q + 1]
        gt[pl.ds(pl.multiple_of(q * 128, 128), 128), :] = jnp.concatenate([tile, jnp.zeros((120, 128), F32)], axis=0).T

    def pick(tile, e):
        lane = lax.broadcasted_iota(jnp.int32, tile.shape, 1)
        return jnp.sum(jnp.where(lane == e, tile, 0.0), axis=1, keepdims=True)

    def accumulate(n, q, val):
        for cc in range(2):
            for h in range(2):
                part[n, cc, h, q] += val[cc * 64:(cc + 1) * 64, h * HALF:(h + 1) * HALF]

    def experts(step, hooks):
        def body(e, carry):
            step(e)
            for at, fn in hooks.items():
                @pl.when(e == at)
                def _():
                    fn()
            return carry
        lax.fori_loop(0, EXP, body, 0)

    def forward(k, load=False):
        q = chips[k]
        sl = pl.ds(pl.multiple_of(q * 128, 128), 128)

        def step(e):
            if load:
                for cp in expert_load(e):
                    cp.wait()
            xs = rows[XT, sl, :]
            a = jnp.dot(xs, wg[e], preferred_element_type=F32)
            b = jnp.dot(xs, wu[e], preferred_element_type=F32)
            tile = gt[sl, :]
            mark = pick(tile, e + 4) > 0.5
            sg = jax.nn.sigmoid(a)
            ac = a * sg
            act[e, sl, :] = jnp.where(mark, ac, 0.0)
            gfac[e, sl, :] = jnp.where(mark, b * sg * (1.0 + a * (1.0 - sg)), 0.0)
            hh = jnp.where(mark, ac * b, 0.0).astype(BF)
            hid[e, sl, :] = hh
            ob = jnp.dot(hh, wd[e], preferred_element_type=F32).astype(BF)
            osv[e, sl, :] = ob
            accumulate(1, q, pick(tile, e) * ob.astype(F32))
        return step

    def backward(qa, qb, base, gates):
        sl = pl.ds(pl.multiple_of(base, 256), 256)

        def step(e):
            g = pick(gt[sl, :], e)
            dyf = rows[DY, sl, :].astype(F32)
            do = (g * dyf).astype(BF)
            dh = lax.dot_general(do, wd[e], NT, preferred_element_type=F32).astype(BF).astype(F32)
            da = (dh * gfac[e, sl, :]).astype(BF)
            db = (dh * act[e, sl, :]).astype(BF)
            dag[e, sl, :] = da
            dbg[e, sl, :] = db
            if gates:
                lane = lax.broadcasted_iota(jnp.int32, (256, 128), 1)
                for r in (slice(0, 256), slice(256, 512)):
                    dg = jnp.sum(rows[DY, r, :].astype(F32) * osv[e, r, :].astype(F32), axis=1, keepdims=True)
                    dgs[r, :] += jnp.where(lane == e, dg, 0.0)
            dx = (lax.dot_general(da, wg[e], NT, preferred_element_type=F32)
                  + lax.dot_general(db, wu[e], NT, preferred_element_type=F32)).astype(BF).astype(F32)
            accumulate(2, qa, dx[0:128])
            accumulate(2, qb, dx[128:256])
        return step

    def attention_context():
        ag_wait(XA, 0, 7, 8, 9, 10)
        for cp in wload:
            cp.wait()
        causal_r = lax.broadcasted_iota(jnp.int32, (256, 128), 0) % 128
        causal_c = lax.broadcasted_iota(jnp.int32, (256, 128), 1)
        keep = (causal_r >= causal_c) & (causal_r // 64 == causal_c // 64)
        qkv = lax.dot_general(rows[XA], wqkv[...], NT, preferred_element_type=F32).astype(BF)
        qkvs = [qkv[q * 128:(q + 1) * 128] for q in range(4)]
        scs = [lax.dot_general(jnp.concatenate([v[:, 0:64], v[:, 64:128]], axis=0), v[:, 128:192], NT,
                               preferred_element_type=F32) * (64 ** -0.5) for v in qkvs]
        scs = [jnp.where(keep, sc, -1e30) for sc in scs]
        mxs = [jnp.max(sc, axis=1, keepdims=True) for sc in scs]
        exs = [jnp.exp(sc - mx) for sc, mx in zip(scs, mxs)]
        sms = [jnp.sum(ex, axis=1, keepdims=True) for ex in exs]
        prs = [(ex / sm).astype(BF) for ex, sm in zip(exs, sms)]
        ctxs = [jnp.dot(pr, v[:, 192:256], preferred_element_type=F32).astype(BF) for pr, v in zip(prs, qkvs)]
        return jnp.concatenate([jnp.concatenate([v[0:128], v[128:256]], axis=1) for v in ctxs], axis=0)

    def attention_out(ctx):
        for q in range(4):
            out = jnp.dot(ctx[q * 128:(q + 1) * 128], wo[...], preferred_element_type=F32)
            for cc in range(2):
                for h in range(2):
                    part[0, cc, h, q] = out[cc * 64:(cc + 1) * 64, h * HALF:(h + 1) * HALF]

    def leave(i, n):
        for h in range(2):
            cols = slice(h * HALF, (h + 1) * HALF)
            rsc[n][2 * first[h] + h].wait_recv()
            near = chip_sum(n, h, first[h])
            rsc[n][2 * second[h] + h].wait_recv()
            rsc[n][8 + 3 * h].wait_recv()
            far = chip_sum(n, h, second[h]) + r1[n, h, 0]
            rsc[n][2 * OWN + h].wait_recv()
            mine = chip_sum(n, h, OWN)
            sums[X - 1, i, :, cols] = near if h == 0 else far
            sums[Y - 1, i, :, cols] = far if h == 0 else near
            sums[2, i, :, cols] = mine
        cps = [pltpu.make_async_copy(sums.at[k, i], dst.at[i], out_sem.at[6 + 2 * k + i])
               for k, dst in enumerate((tox_out, toy_out, own_out))]
        for cp in cps:
            cp.start()
        return cps

    for cp in ins:
        cp.wait()
    pl.semaphore_wait(barrier, len(rels))
    for cp in gate_cps.values():
        cp.start()
    ag_own(XT)
    ag_own(XA)
    gate_table(OWN)
    ag_wait(XT, 0)
    experts(forward(OWN, True), {2: lambda: ag_forward(XT)})
    rs_pair(1, OWN)
    ag_pair(XT)
    gate_table(X)
    ag_wait(XT, 7)
    experts(forward(X), {0: lambda: (ag_forward(XA), ag_own(DY)), 2: lambda: ag_pair(XA)})
    rs_pair(1, X)
    gate_table(Y)
    ag_wait(XT, 8)
    experts(forward(Y), {0: lambda: ag_last(XT), 2: lambda: ag_last(XA), 3: lambda: (ag_forward(DY), rs_near(1, 0))})
    rs_pair(1, Y)
    gate_table(DI)
    ag_wait(XT, 9, 10)
    gate_out = pltpu.make_async_copy(gt, gt_out, out_sem.at[2])
    gate_out.start()
    rows_out = pltpu.make_async_copy(rows.at[XT], xall_out, out_sem.at[0])
    rows_out.start()
    experts(forward(DI), {1: lambda: rs_near(1, 1), 2: lambda: ag_pair(DY)})
    rs_pair(1, DI)
    hid_out = pltpu.make_async_copy(hid, h_out, out_sem.at[3])
    hid_out.start()
    ctx = attention_context()
    ag_last(DY)
    rs_far(1)
    attention_out(ctx)
    for k in (DI, X, Y, OWN):
        rs_pair(0, k)
    ag_wait(DY, 0, 7, 8, 9, 10)
    dys_out = pltpu.make_async_copy(rows.at[DY], dyall_out, out_sem.at[1])
    dys_out.start()
    experts(backward(2 * (1 - y), 2 * (1 - y) + 1, (1 - y) * 256, True), {1: lambda: rs_far(0)})
    rs_pair(2, DI)
    rs_pair(2, Y)
    for q in range(4):
        dsend[q] = dgs[q * 128:(q + 1) * 128, :].T[0:8, :]
    drecv[me] = dsend[q0]
    for cp in dg_cps.values():
        cp.start()
    experts(backward(2 * y, 2 * y + 1, y * 256, False), {1: lambda: rs_far(2), 3: lambda: rs_second(1)})
    rs_pair(2, X)
    rs_pair(2, OWN)
    da_cp = pltpu.make_async_copy(dag, da_out, out_sem.at[4])
    db_cp = pltpu.make_async_copy(dbg, db_out, out_sem.at[5])
    da_cp.start()
    db_cp.start()
    leaving = leave(0, 0)
    leaving += leave(1, 2)
    for cp in dg_cps.values():
        cp.wait_recv()
    both = drecv[...].reshape(64, 128)
    mine = jnp.where(c == 0, both[:, 0:ROWS], both[:, ROWS:128])
    for j in range(TOPK):
        hit = row_exp == idx_ref[j:j + 1, :]
        dg_out[j:j + 1, :] = jnp.sum(jnp.where(hit & is_gate, mine, 0.0), axis=0, keepdims=True)
    rs_final(1, y_out)

    for cp in [gate_out, rows_out, dys_out, hid_out, da_cp, db_cp] + leaving:
        cp.wait()
    for group in ag + [list(gate_cps.values()), list(dg_cps.values())]:
        for cp in group:
            cp.wait_send()
    for n in range(3):
        for k, cp in enumerate(rsc[n]):
            if n == 1 or k < 8 or k in (8, 11):
                cp.wait_send()


def exchange(x, dy, xa, idx, gates, wg, wu, wd, wq, wk, wv, wo):
    any_spec = pl.BlockSpec(memory_space=pl.ANY)
    vmem = pl.BlockSpec(memory_space=pltpu.VMEM)
    sds = jax.ShapeDtypeStruct
    dma = pltpu.SemaphoreType.DMA
    return pl.pallas_call(
        exchange_kernel,
        name='exchange',
        out_shape=[sds((ROWS, D), BF), sds((TOPK, ROWS), F32)] + [sds((2, ROWS, D), F32)] * 3 + [
                   sds((TOK, D), BF), sds((TOK, D), BF),
                   sds((EXP, TOK, FF), BF), sds((EXP, TOK, FF), BF), sds((EXP, TOK, FF), BF), sds((TOK, 128), F32)],
        in_specs=[any_spec, any_spec, any_spec, vmem, vmem] + [any_spec] * 7,
        out_specs=[vmem] * 2 + [any_spec] * 9,
        scratch_shapes=[
            pltpu.VMEM((3, TOK, D), BF),
            pltpu.VMEM((EXP, D, FF), BF), pltpu.VMEM((EXP, D, FF), BF), pltpu.VMEM((EXP, FF, D), BF),
            pltpu.VMEM((256, D), BF), pltpu.VMEM((128, D), BF),
            pltpu.VMEM((EXP, TOK, FF), BF), pltpu.VMEM((EXP, TOK, D), BF),
            pltpu.VMEM((EXP, TOK, FF), BF), pltpu.VMEM((EXP, TOK, FF), BF),
            pltpu.VMEM((EXP, TOK, FF), F32), pltpu.VMEM((EXP, TOK, FF), F32),
            pltpu.VMEM((TOK, 128), F32),
            pltpu.VMEM((8, 8, 128), F32), pltpu.VMEM((8, 8, 128), F32),
            pltpu.VMEM((TOK, 128), F32), pltpu.VMEM((4, 8, 128), F32), pltpu.VMEM((8, 8, 128), F32),
            pltpu.VMEM((3, 2, ROWS, D), F32),
            pltpu.VMEM((3, 2, 2, 4, ROWS, HALF), F32), pltpu.VMEM((3, 2, 4, ROWS, HALF), F32),
            pltpu.VMEM((3, 2, 2, ROWS, HALF), F32), pltpu.VMEM((3, 2, 2, ROWS, HALF), F32),
            pltpu.VMEM((3, 2, ROWS, HALF), F32), pltpu.VMEM((3, 2, ROWS, HALF), F32),
            dma((3,)), dma((4 + 3 * EXP,)), dma((12,)), dma((7,)), dma((7,)),
            dma((3, RS_COPIES)), dma((3, RS_COPIES)), dma((3, GATHER_COPIES)), dma((3, GATHER_COPIES)),
            dma((7,)), dma((7,)),
        ],
        compiler_params=pltpu.CompilerParams(collective_id=0, has_side_effects=True, vmem_limit_bytes=60 * 1024 * 1024),
    )(x, dy, xa, idx, gates, wg, wu, wd, wq, wk, wv, wo)


def grads_kernel(x_ref, dy_ref, gt_ref, h_ref, da_ref, db_ref, y_in, dg_in,
                 dwg_ref, dwu_ref, dwd_ref, y_out, dg_out, xt):
    e = pl.program_id(0)

    @pl.when(e == 0)
    def _():
        xt[...] = x_ref[...].T
        y_out[...] = y_in[...]
        dg_out[...] = dg_in[...]

    dwg_ref[0] = jnp.dot(xt[...], da_ref[0], preferred_element_type=F32)
    dwu_ref[0] = jnp.dot(xt[...], db_ref[0], preferred_element_type=F32)
    lane = lax.broadcasted_iota(jnp.int32, (TOK, 128), 1)
    g = jnp.sum(jnp.where(lane == e, gt_ref[...], 0.0), axis=1, keepdims=True)
    do = (g * dy_ref[...].astype(F32)).astype(BF)
    dwd_ref[0] = lax.dot_general(h_ref[0], do, TN, preferred_element_type=F32)


def weight_grads(xall, dyall, gt, h, da, db, y_t, dg):
    sds = jax.ShapeDtypeStruct
    whole = lambda shape: pl.BlockSpec(shape, lambda e: (0, 0))
    per = lambda a, b: pl.BlockSpec((1, a, b), lambda e: (e, 0, 0))
    return pl.pallas_call(
        grads_kernel,
        name='weight_grads',
        grid=(EXP,),
        out_shape=[sds((EXP, D, FF), F32), sds((EXP, D, FF), F32), sds((EXP, FF, D), F32),
                   sds((ROWS, D), BF), sds((TOPK, ROWS), F32)],
        in_specs=[whole((TOK, D)), whole((TOK, D)), whole((TOK, 128)), per(TOK, FF), per(TOK, FF), per(TOK, FF)]
        + [whole((ROWS, D))] + [whole((TOPK, ROWS))],
        out_specs=[per(D, FF), per(D, FF), per(FF, D)] + [whole((ROWS, D))] + [whole((TOPK, ROWS))],
        scratch_shapes=[pltpu.VMEM((D, TOK), BF)],
        cost_estimate=pl.CostEstimate(flops=3 * 2 * EXP * TOK * D * FF, bytes_accessed=34 * 1024 * 1024, transcendentals=0),
        compiler_params=pltpu.CompilerParams(vmem_limit_bytes=62 * 1024 * 1024),
    )(xall, dyall, gt, h, da, db, y_t, dg)


def solution(mesh):
    def local_step(x_tokens, expert_idx, gate_vals, dy_tokens, w_gate, w_up, w_down, x_attn, w_query, w_key, w_value, w_out):
        y_p, dg_p, to_x, to_y, own, xall, dyall, h, da, db, gt = exchange(
            x_tokens, dy_tokens, x_attn.reshape(ROWS, D), expert_idx.T, gate_vals.T, w_gate, w_up, w_down,
            w_query.transpose(1, 2, 0).reshape(128, D), w_key.transpose(1, 2, 0).reshape(64, D),
            w_value.transpose(1, 2, 0).reshape(64, D), w_out.reshape(128, D))
        from_x = lax.ppermute(to_x, GROUP_AXES, [(g, g ^ 2) for g in range(8)])
        from_y = lax.ppermute(to_y, GROUP_AXES, [(g, g ^ 4) for g in range(8)])
        dwg, dwu, dwd, y_t, dg = weight_grads(xall, dyall, gt, h, da, db, y_p, dg_p)
        both = (own + from_x + from_y).astype(BF)
        at, dx_t = both[0], both[1]
        return y_t, dx_t, dg.T, dwg, dwu, dwd, at.reshape(1, ROWS, D)

    spec_rows = P(TOKEN_AXES, None)
    spec_seqs = P(TOKEN_AXES, None, None)
    spec_experts = P(GROUP_AXES, None, None)
    spec_heads = P(None, GROUP_AXES, None)
    return jax.shard_map(local_step, mesh=mesh,
                         in_specs=(spec_rows, spec_rows, spec_rows, spec_rows, spec_experts, spec_experts, spec_experts, spec_seqs, spec_heads, spec_heads, spec_heads, spec_experts),
                         out_specs=(spec_rows, spec_rows, spec_rows, spec_seqs, spec_seqs, spec_seqs, spec_seqs),
                         check_vma=False)
```

time: 76.7 us -> 61.6 us (0.80)
  Pallas kernels: 75.8 us -> 57.8 us
  starting transfers between devices: 0 us -> 2 us
    pallas_call x1, Pallas kernels: 62.8 us -> 44.8 us  [exchange(): pl.pallas_call(exchange_kernel, name='exchange', out_shape=[sds((ROWS, D)...]
    ppermute x0 -> x2, starting transfers between devices: none -> 2 us  [the longest x1 1.17 us: local_step(): from_y = lax.ppermute(to_y, GROUP_AXES, [(g, g ^ 4) for g in range(8)])]
  transfers between devices with their start and end apart: 0 -> 2, of which waited for: 0 -> 0; matrix products, arithmetic and copies ran while one was open for 0% -> 0% of each run, Pallas kernels for 0% -> 21%
where the time goes in v3:
time: 61.6 us; the launch traced here: 61.3 us
  Pallas kernels  57.8 us (94%)
  starting transfers between devices  2 us (3%)
  local copies, waits for them, and re-layouts  0.72 us (1%)
  between operations  0.67 us (1%)
    pallas_call x1, Pallas kernels, exchange(): pl.pallas_call(exchange_kernel, name='exchange', out_shape=[sds((ROWS, D)...  44.8 us
    pallas_call x1, Pallas kernels, weight_grads(): pl.pallas_call(grads_kernel, name='weight_grads', grid=(EXP,), out_shape=...  13 us
  transfers between devices with their start and end apart: 2, of which 0 were waited for; matrix products, arithmetic and copies ran while one was open for 0% of the time, Pallas kernels for 21%

profile of v3, /device:TPU:0, one launch (start us, length us, event | category | flops | bytes accessed | tf_op | source)
XLA Modules:
  0.0 61.3 jit_solution(6413607855940233715)
XLA Ops:
  0.6 44.8 %exchange.1 = (bf16[64,1024]{1,0:T(8,128)(2,1)}, f32[8,64]{1,0:T(8,128)}, f32[2,64,1024]{2,1,0:T(8,128)}, f32[2,64,1024]{2,1,0:T(8,128)}, f32[2,64,1024]{2,1,0:T...) custom-call(bf16[64,1024]{1,0:T(8,128)(2,1)} %x_hbm.1, ...), custom_call_target="tpu_custom_call" | custom-call | tf_op jit(solution)/shard_map/exchange/pallas_call | solution.py:407
  45.5 0.8 %collective-permute-start = (f32[2,64,1024]{2,1,0:T(8,128)}, f32[2,64,1024]{2,1,0:T(8,128)S(1)}, u32[]{:S(2)}, u32[]{:S(2)}) collective-permute-start(f32[2,64,1024]{2,1,0:T(8,128)} %get-tuple-element.33), channel_id=1, source_target_pairs={{0,2},{1,3},{2,0},{3,1},{4,6},{5,7},{6,4},{7,5}} | collective-permute-start | bytes 1572872 | tf_op jit(solution)/shard_map/ppermute | solution.py:480
  46.3 1.2 %collective-permute-start.1 = (f32[2,64,1024]{2,1,0:T(8,128)}, f32[2,64,1024]{2,1,0:T(8,128)S(1)}, u32[]{:S(2)}, u32[]{:S(2)}) collective-permute-start(f32[2,64,1024]{2,1,0:T(8,128)} %get-tuple-element.34), channel_id=1, source_target_pairs={{0,4},{1,5},{2,6},{3,7},{4,0},{5,1},{6,2},{7,3}} | collective-permute-start | bytes 1572872 | tf_op jit(solution)/shard_map/ppermute | solution.py:481
  47.5 0.0 copy-start
  47.5 13.0 %weight_grads.1 = (f32[4,1024,512]{2,1,0:T(8,128)}, f32[4,1024,512]{2,1,0:T(8,128)}, f32[4,512,1024]{2,1,0:T(8,128)}, bf16[64,1024]{1,0:T(8,128)(2,1)}, f32[8,64]{1,0:T(8,128)}) custom-call(bf16[512,1024]{1,0:T(8,128)(2,1)} %get-tuple-element.23.x_ref, bf16[512,1024]{1,0:T(8,128)(2,1)} %get-tuple-element.24.dy_ref, f32[512,128]{1,0:T(8,128)} %get-tuple-element.25.gt_ref, ...), custom_call_target="tpu_custom_call" | custom-call | flops 6442450944 | bytes 35651584 | tf_op jit(solution)/shard_map/weight_grads/pallas_call | solution.py:459
  60.5 0.0 collective-permute-done
  60.5 0.0 collective-permute-done.1
  60.5 0.0 copy-done
  60.5 0.1 add_convert_fusion
  60.6 0.7 %fusion = (bf16[1,64,1024]{2,1,0:T(8,128)(2,1)}, bf16[64,1024]{1,0:T(8,128)(2,1)}) fusion(bf16[2,64,1024]{2,1,0:T(8,128)(2,1)S(1)} %add_convert_fusion), kind=kLoop, calls=%fused_computation.2 | loop fusion | bytes 524288 | tf_op jit(solution)/shard_map/slice | solution.py:484
Async XLA Ops:
  45.5 15.0 %collective-permute-start = (f32[2,64,1024]{2,1,0:T(8,128)}, f32[2,64,1024]{2,1,0:T(8,128)S(1)}, u32[]{:S(2)}, u32[]{:S(2)}) collective-permute-start(f32[2,64,1024]{2,1,0:T(8,128)} %get-tuple-element.33), channel_id=1, source_target_pairs={{0,2},{1,3},{2,0},{3,1},{4,6},{5,7},{6,4},{7,5}} | collective-permute-start | bytes 1572872 | tf_op jit(solution)/shard_map/ppermute | solution.py:480
  46.3 14.2 %collective-permute-start.1 = (f32[2,64,1024]{2,1,0:T(8,128)}, f32[2,64,1024]{2,1,0:T(8,128)S(1)}, u32[]{:S(2)}, u32[]{:S(2)}) collective-permute-start(f32[2,64,1024]{2,1,0:T(8,128)} %get-tuple-element.34), channel_id=1, source_target_pairs={{0,4},{1,5},{2,6},{3,7},{4,0},{5,1},{6,2},{7,3}} | collective-permute-start | bytes 1572872 | tf_op jit(solution)/shard_map/ppermute | solution.py:481
  47.5 13.0 %copy-start = (f32[2,64,1024]{2,1,0:T(8,128)S(1)}, f32[2,64,1024]{2,1,0:T(8,128)}, u32[]{:S(2)}) copy-start(f32[2,64,1024]{2,1,0:T(8,128)} %get-tuple-element.32) | copy-start | bytes 1572868

commit v4 on v3

--- a/solution.py
+++ b/solution.py
@@ -20,17 +20,15 @@
 HALF = 512
 EXP = 4
 TOPK = 8
-GATHER_COPIES = 11
-RS_COPIES = 14
 XA, XT, DY = 0, 1, 2
 
 NT = (((1,), (1,)), ((), ()))
 TN = (((0,), (0,)), ((), ()))
 
 
-def exchange_kernel(x_hbm, dy_hbm, xa_hbm, idx_ref, gate_ref, wg_hbm, wu_hbm, wd_hbm, wq_hbm, wk_hbm, wv_hbm, wo_hbm,
+def exchange_kernel(x_hbm, dy_hbm, xa_hbm, idx_hbm, gate_hbm, wg_hbm, wu_hbm, wd_hbm, wq_hbm, wk_hbm, wv_hbm, wo_hbm,
                     y_out, dg_out, tox_out, toy_out, own_out, xall_out, dyall_out, h_out, da_out, db_out, gt_out,
-                    rows, wg, wu, wd, wqkv, wo, hid, osv, dag, dbg, act, gfac, gt, gsend, grecv,
+                    idx_ref, gate_ref, y_ref, dg_ref, rows, wg, wu, wd, wqkv, wo, hid, osv, dag, dbg, act, gfac, gt, gsend, grecv,
                     dgs, dsend, drecv,
                     sums, part, pair, s1, r1, s2, r2,
                     in_sem, w_sem, out_sem, gs_sem, gr_sem, rs_s, rs_r, ag_s, ag_r, dd_s, dd_r):
@@ -59,25 +57,28 @@
         pl.semaphore_signal(barrier, inc=1, device_id=dev(*rel), device_id_type=MESH)
 
     own = pl.ds(pl.multiple_of(me * ROWS, ROWS), ROWS)
-    ins = [pltpu.make_async_copy(src, rows.at[t, own], in_sem.at[t])
-           for t, src in ((XT, x_hbm), (DY, dy_hbm), (XA, xa_hbm))]
-    for cp in ins:
+    tables = [pltpu.make_async_copy(idx_hbm, idx_ref, in_sem.at[1]), pltpu.make_async_copy(gate_hbm, gate_ref, in_sem.at[2])]
+    for cp in tables:
         cp.start()
+    for t, src in ((XT, x_hbm), (DY, dy_hbm), (XA, xa_hbm)):
+        pltpu.make_async_copy(src, rows.at[t, own], in_sem.at[0]).start()
 
     def expert_load(e):
-        return [pltpu.make_async_copy(src.at[e], dst.at[e], w_sem.at[4 + n * EXP + e])
-                for n, (src, dst) in enumerate(((wg_hbm, wg), (wu_hbm, wu), (wd_hbm, wd)))]
+        return [pltpu.make_async_copy(src.at[e], dst.at[e], w_sem.at[1 + e])
+                for src, dst in ((wg_hbm, wg), (wu_hbm, wu), (wd_hbm, wd))]
 
     for e in range(EXP):
         for cp in expert_load(e):
             cp.start()
     wload = [pltpu.make_async_copy(wq_hbm, wqkv.at[0:128], w_sem.at[0]),
-             pltpu.make_async_copy(wk_hbm, wqkv.at[128:192], w_sem.at[1]),
-             pltpu.make_async_copy(wv_hbm, wqkv.at[192:256], w_sem.at[2]),
-             pltpu.make_async_copy(wo_hbm, wo, w_sem.at[3])]
+             pltpu.make_async_copy(wk_hbm, wqkv.at[128:192], w_sem.at[0]),
+             pltpu.make_async_copy(wv_hbm, wqkv.at[192:256], w_sem.at[0]),
+             pltpu.make_async_copy(wo_hbm, wo, w_sem.at[0])]
     for cp in wload:
         cp.start()
 
+    for cp in tables:
+        cp.wait()
     row = lax.broadcasted_iota(jnp.int32, (64, ROWS), 0)
     row_exp = (row // 8) * 4 + row % 4
     is_gate = (row % 8) < 4
@@ -102,9 +103,14 @@
 
     hr = ROWS // 2
 
+    def gather_slot(t, k):
+        if t == XT:
+            return min(k, 9)
+        return (10 if t == XA else 17) + (k - 1 if 1 <= k <= 6 else 6)
+
     def gather_copies(t):
         def cp(k, ref, where):
-            return remote(ref, ref, ag_s.at[t, k], ag_r.at[t, k], where)
+            return remote(ref, ref, ag_s.at[t], ag_r.at[gather_slot(t, k)], where)
         return [cp(0, blk(t, q0), sib),
                 cp(1, blk(t, q0, 0, hr), xn), cp(2, blk(t, q0, hr, hr), xn),
                 cp(3, blk(t, q0, hr, hr), yn), cp(4, blk(t, q0, 0, hr), yn),
@@ -136,17 +142,17 @@
         ag[t][6].wait_recv()
         ag[t][10].start()
 
-    def ag_wait(t, *ks):
-        for k in ks:
-            ag[t][k].wait_recv()
+    def ag_rows(t, k, n):
+        ref = rows.at[t, 0:n]
+        return remote(ref, ref, ag_s.at[t], ag_r.at[gather_slot(t, k)], sib)
 
     def tile_copies(send, recv, ss, rs, chip_tiles):
         cps = {}
-        for k, (fx, fy, fc) in enumerate(rels):
+        for fx, fy, fc in rels:
             where = dev(fx, fy, fc)
             qq = 2 * where[1] + where[2] // 2
             src = send.at[qq] if chip_tiles else send.at[where[1] * 4 + where[2]]
-            cps[fx, fy, fc] = remote(src, recv.at[me], ss.at[k], rs.at[k], where)
+            cps[fx, fy, fc] = remote(src, recv.at[me], ss.at[0], rs.at[0 if chip_tiles else fx + 2 * fy], where)
         return cps
 
     gate_cps = tile_copies(gsend, grecv, gs_sem, gr_sem, False)
@@ -156,9 +162,23 @@
     first = (X, Y)
     second = (Y, X)
 
+    def rs_slot(n, k):
+        if k >= 8:
+            kind = (k - 8) % 3
+            group = 2 if kind == 0 else 1
+        else:
+            group = 0 if k // 2 == DI else 1
+            if n == 1 and k // 2 in (X, Y):
+                group = 3 if k == 2 * X else 4 if k == 2 * Y + 1 else 5
+        return (0, 3, 9)[n] + group
+
+    def rs_wait(n, k, count):
+        ref = pair.at[n, 0, 0:2] if count == 2 else pair.at[n, :, 0:3] if count == 6 else pair.at[n, 0, 0]
+        remote(ref, ref, rs_s.at[n, 0], rs_r.at[rs_slot(n, k)], sib).wait_recv()
+
     def rs_copies(n):
         def cp(k, src, dst, where):
-            return remote(src, dst, rs_s.at[n, k], rs_r.at[n, k], where)
+            return remote(src, dst, rs_s.at[n, 0 if k < 8 else 1], rs_r.at[rs_slot(n, k)], where)
         cps = [cp(2 * k + h, part.at[n, 1 - c, h, chips[k]], pair.at[n, h, chips[k]], sib) for k in range(4) for h in range(2)]
         for h in range(2):
             one, two = (xn, yn) if h == 0 else (yn, xn)
@@ -176,38 +196,34 @@
         return part[n, c, h, chips[k]] + pair[n, h, chips[k]]
 
     def rs_far(n):
+        rs_wait(n, 2 * DI, 2)
         for h in range(2):
-            rsc[n][2 * DI + h].wait_recv()
             s1[n, h, 0] = chip_sum(n, h, DI)
             rsc[n][8 + 3 * h].start()
 
     def rs_near(n, h):
         k = first[h]
-        rsc[n][2 * k + h].wait_recv()
+        rs_wait(n, 2 * k + h, 1)
         s1[n, h, 1] = chip_sum(n, h, k)
         rsc[n][9 + 3 * h].start()
 
     def rs_second(n):
+        rs_wait(n, 2 * Y, 2)
+        rs_wait(n, 8, 2)
         for h in range(2):
             k = second[h]
-            rsc[n][2 * k + h].wait_recv()
-            rsc[n][8 + 3 * h].wait_recv()
             s2[n, h] = chip_sum(n, h, k) + r1[n, h, 0]
             rsc[n][10 + 3 * h].start()
 
     def rs_final(n, out_ref):
+        rs_wait(n, 2 * OWN, 6)
         for h in range(2):
-            rsc[n][2 * OWN + h].wait_recv()
-            rsc[n][9 + 3 * h].wait_recv()
-            rsc[n][10 + 3 * h].wait_recv()
             total = chip_sum(n, h, OWN) + r1[n, h, 1] + r2[n, h]
             out_ref[:, h * HALF:(h + 1) * HALF] = total.astype(BF)
 
     def gate_table(k):
-        fx, fy = k % 2, k // 2
-        for fc in (0, 1):
-            if (fx, fy, fc) in gate_cps:
-                gate_cps[fx, fy, fc].wait_recv()
+        tiles = grecv.at[0:1 if k == OWN else 2]
+        remote(tiles, tiles, gs_sem.at[0], gr_sem.at[k], sib).wait_recv()
         q = chips[k]
         tile = grecv[2 * q] + grecv[2 * q + 1]
         gt[pl.ds(pl.multiple_of(q * 128, 128), 128), :] = jnp.concatenate([tile, jnp.zeros((120, 128), F32)], axis=0).T
@@ -237,8 +253,7 @@
 
         def step(e):
             if load:
-                for cp in expert_load(e):
-                    cp.wait()
+                pltpu.make_async_copy(wg_hbm.at[0:3], wg.at[0:3], w_sem.at[1 + e]).wait()
             xs = rows[XT, sl, :]
             a = jnp.dot(xs, wg[e], preferred_element_type=F32)
             b = jnp.dot(xs, wu[e], preferred_element_type=F32)
@@ -279,9 +294,8 @@
         return step
 
     def attention_context():
-        ag_wait(XA, 0, 7, 8, 9, 10)
-        for cp in wload:
-            cp.wait()
+        ag_rows(XA, 0, 4 * ROWS).wait_recv()
+        pltpu.make_async_copy(xall_out.at[0:384], rows.at[XA, 0:384], w_sem.at[0]).wait()
         causal_r = lax.broadcasted_iota(jnp.int32, (256, 128), 0) % 128
         causal_c = lax.broadcasted_iota(jnp.int32, (256, 128), 1)
         keep = (causal_r >= causal_c) & (causal_r // 64 == causal_c // 64)
@@ -305,46 +319,42 @@
                     part[0, cc, h, q] = out[cc * 64:(cc + 1) * 64, h * HALF:(h + 1) * HALF]
 
     def leave(i, n):
+        rs_wait(n, 2 * OWN, 6)
+        rs_wait(n, 8, 2)
         for h in range(2):
             cols = slice(h * HALF, (h + 1) * HALF)
-            rsc[n][2 * first[h] + h].wait_recv()
             near = chip_sum(n, h, first[h])
-            rsc[n][2 * second[h] + h].wait_recv()
-            rsc[n][8 + 3 * h].wait_recv()
             far = chip_sum(n, h, second[h]) + r1[n, h, 0]
-            rsc[n][2 * OWN + h].wait_recv()
             mine = chip_sum(n, h, OWN)
             sums[X - 1, i, :, cols] = near if h == 0 else far
             sums[Y - 1, i, :, cols] = far if h == 0 else near
             sums[2, i, :, cols] = mine
-        cps = [pltpu.make_async_copy(sums.at[k, i], dst.at[i], out_sem.at[6 + 2 * k + i])
+        cps = [pltpu.make_async_copy(sums.at[k, i], dst.at[i], out_sem.at[6 + k])
                for k, dst in enumerate((tox_out, toy_out, own_out))]
         for cp in cps:
             cp.start()
-        return cps
-
-    for cp in ins:
-        cp.wait()
+
+    pltpu.make_async_copy(xall_out.at[0:3 * ROWS], rows.at[XA, 0:3 * ROWS], in_sem.at[0]).wait()
     pl.semaphore_wait(barrier, len(rels))
     for cp in gate_cps.values():
         cp.start()
     ag_own(XT)
     ag_own(XA)
     gate_table(OWN)
-    ag_wait(XT, 0)
+    ag[XT][0].wait_recv()
     experts(forward(OWN, True), {2: lambda: ag_forward(XT)})
     rs_pair(1, OWN)
     ag_pair(XT)
     gate_table(X)
-    ag_wait(XT, 7)
+    ag[XT][7].wait_recv()
     experts(forward(X), {0: lambda: (ag_forward(XA), ag_own(DY)), 2: lambda: ag_pair(XA)})
     rs_pair(1, X)
     gate_table(Y)
-    ag_wait(XT, 8)
+    ag[XT][8].wait_recv()
     experts(forward(Y), {0: lambda: ag_last(XT), 2: lambda: ag_last(XA), 3: lambda: (ag_forward(DY), rs_near(1, 0))})
     rs_pair(1, Y)
     gate_table(DI)
-    ag_wait(XT, 9, 10)
+    ag_rows(XT, 9, ROWS).wait_recv()
     gate_out = pltpu.make_async_copy(gt, gt_out, out_sem.at[2])
     gate_out.start()
     rows_out = pltpu.make_async_copy(rows.at[XT], xall_out, out_sem.at[0])
@@ -359,10 +369,10 @@
     attention_out(ctx)
     for k in (DI, X, Y, OWN):
         rs_pair(0, k)
-    ag_wait(DY, 0, 7, 8, 9, 10)
+    ag_rows(DY, 0, 4 * ROWS).wait_recv()
     dys_out = pltpu.make_async_copy(rows.at[DY], dyall_out, out_sem.at[1])
     dys_out.start()
-    experts(backward(2 * (1 - y), 2 * (1 - y) + 1, (1 - y) * 256, True), {1: lambda: rs_far(0)})
+    experts(backward(2 * (1 - y), 2 * (1 - y) + 1, (1 - y) * 256, True), {0: lambda: rs_far(0), 3: lambda: rs_second(1)})
     rs_pair(2, DI)
     rs_pair(2, Y)
     for q in range(4):
@@ -370,38 +380,44 @@
     drecv[me] = dsend[q0]
     for cp in dg_cps.values():
         cp.start()
-    experts(backward(2 * y, 2 * y + 1, y * 256, False), {1: lambda: rs_far(2), 3: lambda: rs_second(1)})
+    experts(backward(2 * y, 2 * y + 1, y * 256, False), {0: lambda: rs_far(2)})
     rs_pair(2, X)
     rs_pair(2, OWN)
     da_cp = pltpu.make_async_copy(dag, da_out, out_sem.at[4])
     db_cp = pltpu.make_async_copy(dbg, db_out, out_sem.at[5])
     da_cp.start()
     db_cp.start()
-    leaving = leave(0, 0)
-    leaving += leave(1, 2)
-    for cp in dg_cps.values():
-        cp.wait_recv()
+    leave(0, 0)
+    rs_wait_dg = drecv.at[0:7]
+    remote(rs_wait_dg, rs_wait_dg, dd_s.at[0], dd_r.at[0], sib).wait_recv()
     both = drecv[...].reshape(64, 128)
     mine = jnp.where(c == 0, both[:, 0:ROWS], both[:, ROWS:128])
     for j in range(TOPK):
         hit = row_exp == idx_ref[j:j + 1, :]
-        dg_out[j:j + 1, :] = jnp.sum(jnp.where(hit & is_gate, mine, 0.0), axis=0, keepdims=True)
-    rs_final(1, y_out)
-
-    for cp in [gate_out, rows_out, dys_out, hid_out, da_cp, db_cp] + leaving:
+        dg_ref[j:j + 1, :] = jnp.sum(jnp.where(hit & is_gate, mine, 0.0), axis=0, keepdims=True)
+    rs_final(1, y_ref)
+    small = [pltpu.make_async_copy(y_ref, y_out, out_sem.at[9]), pltpu.make_async_copy(dg_ref, dg_out, out_sem.at[10])]
+    for cp in small:
+        cp.start()
+    leave(1, 2)
+
+    for cp in [gate_out, rows_out, dys_out, hid_out, da_cp, db_cp] + small:
         cp.wait()
-    for group in ag + [list(gate_cps.values()), list(dg_cps.values())]:
-        for cp in group:
-            cp.wait_send()
+    for k, dst in enumerate((tox_out, toy_out, own_out)):
+        pltpu.make_async_copy(sums.at[k], dst, out_sem.at[6 + k]).wait()
+    for t in range(3):
+        ref = rows.at[t, 0:7 * ROWS]
+        remote(ref, ref, ag_s.at[t], ag_r.at[0], sib).wait_send()
+    tiles = gsend.at[0:7]
+    remote(tiles, tiles, gs_sem.at[0], gr_sem.at[0], sib).wait_send()
+    remote(tiles, tiles, dd_s.at[0], dd_r.at[0], sib).wait_send()
     for n in range(3):
-        for k, cp in enumerate(rsc[n]):
-            if n == 1 or k < 8 or k in (8, 11):
-                cp.wait_send()
+        for ref, k in ((part.at[n, 0], 0), (pair.at[n, :, 0:3] if n == 1 else pair.at[n, 0, 0:2], 1)):
+            remote(ref, ref, rs_s.at[n, k], rs_r.at[0], sib).wait_send()
 
 
 def exchange(x, dy, xa, idx, gates, wg, wu, wd, wq, wk, wv, wo):
     any_spec = pl.BlockSpec(memory_space=pl.ANY)
-    vmem = pl.BlockSpec(memory_space=pltpu.VMEM)
     sds = jax.ShapeDtypeStruct
     dma = pltpu.SemaphoreType.DMA
     return pl.pallas_call(
@@ -410,9 +426,10 @@
         out_shape=[sds((ROWS, D), BF), sds((TOPK, ROWS), F32)] + [sds((2, ROWS, D), F32)] * 3 + [
                    sds((TOK, D), BF), sds((TOK, D), BF),
                    sds((EXP, TOK, FF), BF), sds((EXP, TOK, FF), BF), sds((EXP, TOK, FF), BF), sds((TOK, 128), F32)],
-        in_specs=[any_spec, any_spec, any_spec, vmem, vmem] + [any_spec] * 7,
-        out_specs=[vmem] * 2 + [any_spec] * 9,
+        in_specs=[any_spec] * 12,
+        out_specs=[any_spec] * 11,
         scratch_shapes=[
+            pltpu.VMEM((TOPK, ROWS), jnp.int32), pltpu.VMEM((TOPK, ROWS), F32), pltpu.VMEM((ROWS, D), BF), pltpu.VMEM((TOPK, ROWS), F32),
             pltpu.VMEM((3, TOK, D), BF),
             pltpu.VMEM((EXP, D, FF), BF), pltpu.VMEM((EXP, D, FF), BF), pltpu.VMEM((EXP, FF, D), BF),
             pltpu.VMEM((256, D), BF), pltpu.VMEM((128, D), BF),
@@ -426,9 +443,8 @@
             pltpu.VMEM((3, 2, 2, 4, ROWS, HALF), F32), pltpu.VMEM((3, 2, 4, ROWS, HALF), F32),
             pltpu.VMEM((3, 2, 2, ROWS, HALF), F32), pltpu.VMEM((3, 2, 2, ROWS, HALF), F32),
             pltpu.VMEM((3, 2, ROWS, HALF), F32), pltpu.VMEM((3, 2, ROWS, HALF), F32),
-            dma((3,)), dma((4 + 3 * EXP,)), dma((12,)), dma((7,)), dma((7,)),
-            dma((3, RS_COPIES)), dma((3, RS_COPIES)), dma((3, GATHER_COPIES)), dma((3, GATHER_COPIES)),
-            dma((7,)), dma((7,)),
+            dma((3,)), dma((1 + EXP,)), dma((11,)), dma((1,)), dma((4,)),
+            dma((3, 2)), dma((12,)), dma((3,)), dma((24,)), dma((1,)), dma((1,)),
         ],
         compiler_params=pltpu.CompilerParams(collective_id=0, has_side_effects=True, vmem_limit_bytes=60 * 1024 * 1024),
     )(x, dy, xa, idx, gates, wg, wu, wd, wq, wk, wv, wo)

time: 61.6 us -> 58 us (0.942)
  Pallas kernels: 57.8 us -> 54.2 us
    pallas_call x1, Pallas kernels: 44.8 us -> 41.2 us  [exchange(): pl.pallas_call(exchange_kernel, name='exchange', out_shape=[sds((ROWS, D)...]
  transfers between devices with their start and end apart: 2 -> 2, of which waited for: 0 -> 0; matrix products, arithmetic and copies ran while one was open for 0% -> 0% of each run, Pallas kernels for 21% -> 23%
where the time goes in v4:
time: 58 us; the launch traced here: 57.8 us
  Pallas kernels  54.2 us (93%)
  starting transfers between devices  2.08 us (4%)
  local copies, waits for them, and re-layouts  0.72 us (1%)
  between operations  0.67 us (1%)
    pallas_call x1, Pallas kernels, exchange(): pl.pallas_call(exchange_kernel, name='exchange', out_shape=[sds((ROWS, D)...  41.2 us
    pallas_call x1, Pallas kernels, weight_grads(): pl.pallas_call(grads_kernel, name='weight_grads', grid=(EXP,), out_shape=...  13 us
    ppermute x1, starting transfers between devices, local_step(): from_y = lax.ppermute(to_y, GROUP_AXES, [(g, g ^ 4) for g in range(8)])  1.2 us
  transfers between devices with their start and end apart: 2, of which 0 were waited for; matrix products, arithmetic and copies ran while one was open for 0% of the time, Pallas kernels for 23%

profile of v4, /device:TPU:0, one launch (start us, length us, event | category | flops | bytes accessed | tf_op | source)
XLA Modules:
  0.0 57.8 jit_solution(17098888220994568904)
XLA Ops:
  0.6 41.2 %exchange.1 = (bf16[64,1024]{1,0:T(8,128)(2,1)}, f32[8,64]{1,0:T(8,128)}, f32[2,64,1024]{2,1,0:T(8,128)}, f32[2,64,1024]{2,1,0:T(8,128)}, f32[2,64,1024]{2,1,0:T...) custom-call(bf16[64,1024]{1,0:T(8,128)(2,1)} %x_hbm.1, ...), custom_call_target="tpu_custom_call" | custom-call | tf_op jit(solution)/shard_map/exchange/pallas_call | solution.py:423
  41.9 0.9 %collective-permute-start = (f32[2,64,1024]{2,1,0:T(8,128)}, f32[2,64,1024]{2,1,0:T(8,128)S(1)}, u32[]{:S(2)}, u32[]{:S(2)}) collective-permute-start(f32[2,64,1024]{2,1,0:T(8,128)} %get-tuple-element.33), channel_id=1, source_target_pairs={{0,2},{1,3},{2,0},{3,1},{4,6},{5,7},{6,4},{7,5}} | collective-permute-start | bytes 1572872 | tf_op jit(solution)/shard_map/ppermute | solution.py:496
  42.8 1.2 %collective-permute-start.1 = (f32[2,64,1024]{2,1,0:T(8,128)}, f32[2,64,1024]{2,1,0:T(8,128)S(1)}, u32[]{:S(2)}, u32[]{:S(2)}) collective-permute-start(f32[2,64,1024]{2,1,0:T(8,128)} %get-tuple-element.34), channel_id=1, source_target_pairs={{0,4},{1,5},{2,6},{3,7},{4,0},{5,1},{6,2},{7,3}} | collective-permute-start | bytes 1572872 | tf_op jit(solution)/shard_map/ppermute | solution.py:497
  44.0 0.0 copy-start
  44.0 13.0 %weight_grads.1 = (f32[4,1024,512]{2,1,0:T(8,128)}, f32[4,1024,512]{2,1,0:T(8,128)}, f32[4,512,1024]{2,1,0:T(8,128)}, bf16[64,1024]{1,0:T(8,128)(2,1)}, f32[8,64]{1,0:T(8,128)}) custom-call(bf16[512,1024]{1,0:T(8,128)(2,1)} %get-tuple-element.23.x_ref, bf16[512,1024]{1,0:T(8,128)(2,1)} %get-tuple-element.24.dy_ref, f32[512,128]{1,0:T(8,128)} %get-tuple-element.25.gt_ref, ...), custom_call_target="tpu_custom_call" | custom-call | flops 6442450944 | bytes 35651584 | tf_op jit(solution)/shard_map/weight_grads/pallas_call | solution.py:475
  57.0 0.0 collective-permute-done
  57.0 0.0 collective-permute-done.1
  57.0 0.0 copy-done
  57.0 0.1 add_convert_fusion
  57.1 0.7 %fusion = (bf16[1,64,1024]{2,1,0:T(8,128)(2,1)}, bf16[64,1024]{1,0:T(8,128)(2,1)}) fusion(bf16[2,64,1024]{2,1,0:T(8,128)(2,1)S(1)} %add_convert_fusion), kind=kLoop, calls=%fused_computation.2 | loop fusion | bytes 524288 | tf_op jit(solution)/shard_map/slice | solution.py:500
Async XLA Ops:
  41.9 15.1 %collective-permute-start = (f32[2,64,1024]{2,1,0:T(8,128)}, f32[2,64,1024]{2,1,0:T(8,128)S(1)}, u32[]{:S(2)}, u32[]{:S(2)}) collective-permute-start(f32[2,64,1024]{2,1,0:T(8,128)} %get-tuple-element.33), channel_id=1, source_target_pairs={{0,2},{1,3},{2,0},{3,1},{4,6},{5,7},{6,4},{7,5}} | collective-permute-start | bytes 1572872 | tf_op jit(solution)/shard_map/ppermute | solution.py:496
  42.8 14.2 %collective-permute-start.1 = (f32[2,64,1024]{2,1,0:T(8,128)}, f32[2,64,1024]{2,1,0:T(8,128)S(1)}, u32[]{:S(2)}, u32[]{:S(2)}) collective-permute-start(f32[2,64,1024]{2,1,0:T(8,128)} %get-tuple-element.34), channel_id=1, source_target_pairs={{0,4},{1,5},{2,6},{3,7},{4,0},{5,1},{6,2},{7,3}} | collective-permute-start | bytes 1572872 | tf_op jit(solution)/shard_map/ppermute | solution.py:497
  44.0 13.0 %copy-start = (f32[2,64,1024]{2,1,0:T(8,128)S(1)}, f32[2,64,1024]{2,1,0:T(8,128)}, u32[]{:S(2)}) copy-start(f32[2,64,1024]{2,1,0:T(8,128)} %get-tuple-element.32) | copy-start | bytes 1572868

commit v5 on v4

--- a/solution.py
+++ b/solution.py
@@ -124,6 +124,14 @@
         for k in (1, 3, 2, 4, 0):
             ag[t][k].start()
 
+    def ag_own_a(t):
+        ag[t][1].start()
+        ag[t][3].start()
+
+    def ag_own_b(t):
+        for k in (2, 4, 0):
+            ag[t][k].start()
+
     def ag_forward(t):
         ag[t][1].wait_recv()
         ag[t][5].start()
@@ -247,27 +255,37 @@
             return carry
         lax.fori_loop(0, EXP, body, 0)
 
-    def forward(k, load=False):
-        q = chips[k]
-        sl = pl.ds(pl.multiple_of(q * 128, 128), 128)
+    def chip_rows(k):
+        return pl.ds(pl.multiple_of(chips[k] * 128, 128), 128)
+
+    def forward(ks, load=False):
+        def stack(ref, *at):
+            return jnp.concatenate([ref[(*at, chip_rows(k), slice(None))] for k in ks], axis=0)
 
         def step(e):
             if load:
                 pltpu.make_async_copy(wg_hbm.at[0:3], wg.at[0:3], w_sem.at[1 + e]).wait()
-            xs = rows[XT, sl, :]
+
+            def put(ref, val):
+                for i, k in enumerate(ks):
+                    ref[e, chip_rows(k), :] = val[i * 128:(i + 1) * 128]
+
+            xs = stack(rows, XT)
             a = jnp.dot(xs, wg[e], preferred_element_type=F32)
             b = jnp.dot(xs, wu[e], preferred_element_type=F32)
-            tile = gt[sl, :]
+            tile = stack(gt)
             mark = pick(tile, e + 4) > 0.5
             sg = jax.nn.sigmoid(a)
             ac = a * sg
-            act[e, sl, :] = jnp.where(mark, ac, 0.0)
-            gfac[e, sl, :] = jnp.where(mark, b * sg * (1.0 + a * (1.0 - sg)), 0.0)
+            put(act, jnp.where(mark, ac, 0.0))
+            put(gfac, jnp.where(mark, b * sg * (1.0 + a * (1.0 - sg)), 0.0))
             hh = jnp.where(mark, ac * b, 0.0).astype(BF)
-            hid[e, sl, :] = hh
+            put(hid, hh)
             ob = jnp.dot(hh, wd[e], preferred_element_type=F32).astype(BF)
-            osv[e, sl, :] = ob
-            accumulate(1, q, pick(tile, e) * ob.astype(F32))
+            put(osv, ob)
+            yb = pick(tile, e) * ob.astype(F32)
+            for i, k in enumerate(ks):
+                accumulate(1, chips[k], yb[i * 128:(i + 1) * 128])
         return step
 
     def backward(qa, qb, base, gates):
@@ -342,24 +360,25 @@
     ag_own(XA)
     gate_table(OWN)
     ag[XT][0].wait_recv()
-    experts(forward(OWN, True), {2: lambda: ag_forward(XT)})
+    experts(forward([OWN], True), {2: lambda: ag_forward(XT)})
     rs_pair(1, OWN)
     ag_pair(XT)
     gate_table(X)
+    gate_table(Y)
+    ag_own_a(DY)
     ag[XT][7].wait_recv()
-    experts(forward(X), {0: lambda: (ag_forward(XA), ag_own(DY)), 2: lambda: ag_pair(XA)})
+    ag[XT][8].wait_recv()
+    experts(forward([X, Y]), {0: lambda: (ag_forward(XA), ag_own_b(DY)), 1: lambda: ag_pair(XA), 2: lambda: ag_last(XT)})
     rs_pair(1, X)
-    gate_table(Y)
-    ag[XT][8].wait_recv()
-    experts(forward(Y), {0: lambda: ag_last(XT), 2: lambda: ag_last(XA), 3: lambda: (ag_forward(DY), rs_near(1, 0))})
     rs_pair(1, Y)
     gate_table(DI)
-    ag_rows(XT, 9, ROWS).wait_recv()
+    ag_forward(DY)
     gate_out = pltpu.make_async_copy(gt, gt_out, out_sem.at[2])
     gate_out.start()
+    ag_rows(XT, 9, ROWS).wait_recv()
     rows_out = pltpu.make_async_copy(rows.at[XT], xall_out, out_sem.at[0])
     rows_out.start()
-    experts(forward(DI), {1: lambda: rs_near(1, 1), 2: lambda: ag_pair(DY)})
+    experts(forward([DI]), {1: lambda: (rs_near(1, 0), rs_near(1, 1), ag_last(XA)), 2: lambda: ag_pair(DY)})
     rs_pair(1, DI)
     hid_out = pltpu.make_async_copy(hid, h_out, out_sem.at[3])
     hid_out.start()
@@ -372,7 +391,7 @@
     ag_rows(DY, 0, 4 * ROWS).wait_recv()
     dys_out = pltpu.make_async_copy(rows.at[DY], dyall_out, out_sem.at[1])
     dys_out.start()
-    experts(backward(2 * (1 - y), 2 * (1 - y) + 1, (1 - y) * 256, True), {0: lambda: rs_far(0), 3: lambda: rs_second(1)})
+    experts(backward(2 * (1 - y), 2 * (1 - y) + 1, (1 - y) * 256, True), {0: lambda: rs_far(0), 2: lambda: rs_second(1)})
     rs_pair(2, DI)
     rs_pair(2, Y)
     for q in range(4):

time: 58 us -> 56.5 us (0.974)
  Pallas kernels: 54.2 us -> 52.8 us
    pallas_call x1, Pallas kernels: 41.2 us -> 39.8 us  [exchange(): pl.pallas_call(exchange_kernel, name='exchange', out_shape=[sds((ROWS, D)...]
where the time goes in v5:
time: 56.5 us; the launch traced here: 56.3 us
  Pallas kernels  52.8 us (93%)
  starting transfers between devices  2.03 us (4%)
  local copies, waits for them, and re-layouts  0.72 us (1%)
  between operations  0.67 us (1%)
    pallas_call x1, Pallas kernels, exchange(): pl.pallas_call(exchange_kernel, name='exchange', out_shape=[sds((ROWS, D)...  39.8 us
    pallas_call x1, Pallas kernels, weight_grads(): pl.pallas_call(grads_kernel, name='weight_grads', grid=(EXP,), out_shape=...  13 us
    ppermute x1, starting transfers between devices, local_step(): from_y = lax.ppermute(to_y, GROUP_AXES, [(g, g ^ 4) for g in range(8)])  1.48 us
  transfers between devices with their start and end apart: 2, of which 0 were waited for; matrix products, arithmetic and copies ran while one was open for 0% of the time, Pallas kernels for 23%

profile of v5, /device:TPU:0, one launch (start us, length us, event | category | flops | bytes accessed | tf_op | source)
XLA Modules:
  0.0 56.3 jit_solution(7225751177409623144)
XLA Ops:
  0.6 39.8 %exchange.1 = (bf16[64,1024]{1,0:T(8,128)(2,1)}, f32[8,64]{1,0:T(8,128)}, f32[2,64,1024]{2,1,0:T(8,128)}, f32[2,64,1024]{2,1,0:T(8,128)}, f32[2,64,1024]{2,1,0:T...) custom-call(bf16[64,1024]{1,0:T(8,128)(2,1)} %x_hbm.1, ...), custom_call_target="tpu_custom_call" | custom-call | tf_op jit(solution)/shard_map/exchange/pallas_call | solution.py:442
  40.4 0.6 collective-permute-start
  41.0 1.5 %collective-permute-start.1 = (f32[2,64,1024]{2,1,0:T(8,128)}, f32[2,64,1024]{2,1,0:T(8,128)S(1)}, u32[]{:S(2)}, u32[]{:S(2)}) collective-permute-start(f32[2,64,1024]{2,1,0:T(8,128)} %get-tuple-element.34), channel_id=1, source_target_pairs={{0,4},{1,5},{2,6},{3,7},{4,0},{5,1},{6,2},{7,3}} | collective-permute-start | bytes 1572872 | tf_op jit(solution)/shard_map/ppermute | solution.py:516
  42.4 0.0 copy-start
  42.4 13.0 %weight_grads.1 = (f32[4,1024,512]{2,1,0:T(8,128)}, f32[4,1024,512]{2,1,0:T(8,128)}, f32[4,512,1024]{2,1,0:T(8,128)}, bf16[64,1024]{1,0:T(8,128)(2,1)}, f32[8,64]{1,0:T(8,128)}) custom-call(bf16[512,1024]{1,0:T(8,128)(2,1)} %get-tuple-element.23.x_ref, bf16[512,1024]{1,0:T(8,128)(2,1)} %get-tuple-element.24.dy_ref, f32[512,128]{1,0:T(8,128)} %get-tuple-element.25.gt_ref, ...), custom_call_target="tpu_custom_call" | custom-call | flops 6442450944 | bytes 35651584 | tf_op jit(solution)/shard_map/weight_grads/pallas_call | solution.py:494
  55.5 0.0 collective-permute-done
  55.5 0.0 collective-permute-done.1
  55.5 0.0 copy-done
  55.5 0.1 add_convert_fusion
  55.6 0.7 %fusion = (bf16[1,64,1024]{2,1,0:T(8,128)(2,1)}, bf16[64,1024]{1,0:T(8,128)(2,1)}) fusion(bf16[2,64,1024]{2,1,0:T(8,128)(2,1)S(1)} %add_convert_fusion), kind=kLoop, calls=%fused_computation.2 | loop fusion | bytes 524288 | tf_op jit(solution)/shard_map/slice | solution.py:519
Async XLA Ops:
  40.4 15.0 %collective-permute-start = (f32[2,64,1024]{2,1,0:T(8,128)}, f32[2,64,1024]{2,1,0:T(8,128)S(1)}, u32[]{:S(2)}, u32[]{:S(2)}) collective-permute-start(f32[2,64,1024]{2,1,0:T(8,128)} %get-tuple-element.33), channel_id=1, source_target_pairs={{0,2},{1,3},{2,0},{3,1},{4,6},{5,7},{6,4},{7,5}} | collective-permute-start | bytes 1572872 | tf_op jit(solution)/shard_map/ppermute | solution.py:515
  41.0 14.5 %collective-permute-start.1 = (f32[2,64,1024]{2,1,0:T(8,128)}, f32[2,64,1024]{2,1,0:T(8,128)S(1)}, u32[]{:S(2)}, u32[]{:S(2)}) collective-permute-start(f32[2,64,1024]{2,1,0:T(8,128)} %get-tuple-element.34), channel_id=1, source_target_pairs={{0,4},{1,5},{2,6},{3,7},{4,0},{5,1},{6,2},{7,3}} | collective-permute-start | bytes 1572872 | tf_op jit(solution)/shard_map/ppermute | solution.py:516
  42.4 13.0 %copy-start = (f32[2,64,1024]{2,1,0:T(8,128)S(1)}, f32[2,64,1024]{2,1,0:T(8,128)}, u32[]{:S(2)}) copy-start(f32[2,64,1024]{2,1,0:T(8,128)} %get-tuple-element.32) | copy-start | bytes 1572868

commit v6 on v5

--- a/solution.py
+++ b/solution.py
@@ -27,11 +27,11 @@
 
 
 def exchange_kernel(x_hbm, dy_hbm, xa_hbm, idx_hbm, gate_hbm, wg_hbm, wu_hbm, wd_hbm, wq_hbm, wk_hbm, wv_hbm, wo_hbm,
-                    y_out, dg_out, tox_out, toy_out, own_out, xall_out, dyall_out, h_out, da_out, db_out, gt_out,
-                    idx_ref, gate_ref, y_ref, dg_ref, rows, wg, wu, wd, wqkv, wo, hid, osv, dag, dbg, act, gfac, gt, gsend, grecv,
+                    y_out, dg_out, tox, toy, owns, xall, dyall, hid, dag, dbg, gt,
+                    idx_ref, gate_ref, rows, wg, wu, wd, wqkv, wo, osv, act, gfac, gsend, grecv,
                     dgs, dsend, drecv,
-                    sums, part, pair, s1, r1, s2, r2,
-                    in_sem, w_sem, out_sem, gs_sem, gr_sem, rs_s, rs_r, ag_s, ag_r, dd_s, dd_r):
+                    part, pair, s1, r1, s2, r2,
+                    in_sem, w_sem, gs_sem, gr_sem, rs_s, rs_r, ag_s, ag_r, dd_s, dd_r):
     y = lax.axis_index('ei')
     o = lax.axis_index('eo')
     z = lax.axis_index('dp')
@@ -313,7 +313,7 @@
 
     def attention_context():
         ag_rows(XA, 0, 4 * ROWS).wait_recv()
-        pltpu.make_async_copy(xall_out.at[0:384], rows.at[XA, 0:384], w_sem.at[0]).wait()
+        pltpu.make_async_copy(wg_hbm.at[0, 0:768], wg.at[0, 0:768], w_sem.at[0]).wait()
         causal_r = lax.broadcasted_iota(jnp.int32, (256, 128), 0) % 128
         causal_c = lax.broadcasted_iota(jnp.int32, (256, 128), 1)
         keep = (causal_r >= causal_c) & (causal_r // 64 == causal_c // 64)
@@ -344,15 +344,10 @@
             near = chip_sum(n, h, first[h])
             far = chip_sum(n, h, second[h]) + r1[n, h, 0]
             mine = chip_sum(n, h, OWN)
-            sums[X - 1, i, :, cols] = near if h == 0 else far
-            sums[Y - 1, i, :, cols] = far if h == 0 else near
-            sums[2, i, :, cols] = mine
-        cps = [pltpu.make_async_copy(sums.at[k, i], dst.at[i], out_sem.at[6 + k])
-               for k, dst in enumerate((tox_out, toy_out, own_out))]
-        for cp in cps:
-            cp.start()
-
-    pltpu.make_async_copy(xall_out.at[0:3 * ROWS], rows.at[XA, 0:3 * ROWS], in_sem.at[0]).wait()
+            tox[i, :, cols] = near if h == 0 else far
+            toy[i, :, cols] = far if h == 0 else near
+            owns[i, :, cols] = mine
+    pltpu.make_async_copy(wg_hbm.at[0, 0:6 * ROWS], wg.at[0, 0:6 * ROWS], in_sem.at[0]).wait()
     pl.semaphore_wait(barrier, len(rels))
     for cp in gate_cps.values():
         cp.start()
@@ -373,15 +368,10 @@
     rs_pair(1, Y)
     gate_table(DI)
     ag_forward(DY)
-    gate_out = pltpu.make_async_copy(gt, gt_out, out_sem.at[2])
-    gate_out.start()
     ag_rows(XT, 9, ROWS).wait_recv()
-    rows_out = pltpu.make_async_copy(rows.at[XT], xall_out, out_sem.at[0])
-    rows_out.start()
+    xall[...] = rows[XT]
     experts(forward([DI]), {1: lambda: (rs_near(1, 0), rs_near(1, 1), ag_last(XA)), 2: lambda: ag_pair(DY)})
     rs_pair(1, DI)
-    hid_out = pltpu.make_async_copy(hid, h_out, out_sem.at[3])
-    hid_out.start()
     ctx = attention_context()
     ag_last(DY)
     rs_far(1)
@@ -389,8 +379,7 @@
     for k in (DI, X, Y, OWN):
         rs_pair(0, k)
     ag_rows(DY, 0, 4 * ROWS).wait_recv()
-    dys_out = pltpu.make_async_copy(rows.at[DY], dyall_out, out_sem.at[1])
-    dys_out.start()
+    dyall[...] = rows[DY]
     experts(backward(2 * (1 - y), 2 * (1 - y) + 1, (1 - y) * 256, True), {0: lambda: rs_far(0), 2: lambda: rs_second(1)})
     rs_pair(2, DI)
     rs_pair(2, Y)
@@ -402,10 +391,6 @@
     experts(backward(2 * y, 2 * y + 1, y * 256, False), {0: lambda: rs_far(2)})
     rs_pair(2, X)
     rs_pair(2, OWN)
-    da_cp = pltpu.make_async_copy(dag, da_out, out_sem.at[4])
-    db_cp = pltpu.make_async_copy(dbg, db_out, out_sem.at[5])
-    da_cp.start()
-    db_cp.start()
     leave(0, 0)
     rs_wait_dg = drecv.at[0:7]
     remote(rs_wait_dg, rs_wait_dg, dd_s.at[0], dd_r.at[0], sib).wait_recv()
@@ -413,17 +398,10 @@
     mine = jnp.where(c == 0, both[:, 0:ROWS], both[:, ROWS:128])
     for j in range(TOPK):
         hit = row_exp == idx_ref[j:j + 1, :]
-        dg_ref[j:j + 1, :] = jnp.sum(jnp.where(hit & is_gate, mine, 0.0), axis=0, keepdims=True)
-    rs_final(1, y_ref)
-    small = [pltpu.make_async_copy(y_ref, y_out, out_sem.at[9]), pltpu.make_async_copy(dg_ref, dg_out, out_sem.at[10])]
-    for cp in small:
-        cp.start()
+        dg_out[j:j + 1, :] = jnp.sum(jnp.where(hit & is_gate, mine, 0.0), axis=0, keepdims=True)
+    rs_final(1, y_out)
     leave(1, 2)
 
-    for cp in [gate_out, rows_out, dys_out, hid_out, da_cp, db_cp] + small:
-        cp.wait()
-    for k, dst in enumerate((tox_out, toy_out, own_out)):
-        pltpu.make_async_copy(sums.at[k], dst, out_sem.at[6 + k]).wait()
     for t in range(3):
         ref = rows.at[t, 0:7 * ROWS]
         remote(ref, ref, ag_s.at[t], ag_r.at[0], sib).wait_send()
@@ -437,35 +415,31 @@
 
 def exchange(x, dy, xa, idx, gates, wg, wu, wd, wq, wk, wv, wo):
     any_spec = pl.BlockSpec(memory_space=pl.ANY)
-    sds = jax.ShapeDtypeStruct
+    vmem = pl.BlockSpec(memory_space=pltpu.VMEM)
     dma = pltpu.SemaphoreType.DMA
     return pl.pallas_call(
         exchange_kernel,
         name='exchange',
-        out_shape=[sds((ROWS, D), BF), sds((TOPK, ROWS), F32)] + [sds((2, ROWS, D), F32)] * 3 + [
-                   sds((TOK, D), BF), sds((TOK, D), BF),
-                   sds((EXP, TOK, FF), BF), sds((EXP, TOK, FF), BF), sds((EXP, TOK, FF), BF), sds((TOK, 128), F32)],
+        out_shape=[pltpu.VMEM((ROWS, D), BF), pltpu.VMEM((TOPK, ROWS), F32)] + [pltpu.VMEM((2, ROWS, D), F32)] * 3 + [pltpu.VMEM((TOK, D), BF)] * 2
+        + [pltpu.VMEM((EXP, TOK, FF), BF)] * 3 + [pltpu.VMEM((TOK, 128), F32)],
         in_specs=[any_spec] * 12,
-        out_specs=[any_spec] * 11,
+        out_specs=[vmem] * 11,
         scratch_shapes=[
-            pltpu.VMEM((TOPK, ROWS), jnp.int32), pltpu.VMEM((TOPK, ROWS), F32), pltpu.VMEM((ROWS, D), BF), pltpu.VMEM((TOPK, ROWS), F32),
+            pltpu.VMEM((TOPK, ROWS), jnp.int32), pltpu.VMEM((TOPK, ROWS), F32),
             pltpu.VMEM((3, TOK, D), BF),
             pltpu.VMEM((EXP, D, FF), BF), pltpu.VMEM((EXP, D, FF), BF), pltpu.VMEM((EXP, FF, D), BF),
             pltpu.VMEM((256, D), BF), pltpu.VMEM((128, D), BF),
-            pltpu.VMEM((EXP, TOK, FF), BF), pltpu.VMEM((EXP, TOK, D), BF),
-            pltpu.VMEM((EXP, TOK, FF), BF), pltpu.VMEM((EXP, TOK, FF), BF),
+            pltpu.VMEM((EXP, TOK, D), BF),
             pltpu.VMEM((EXP, TOK, FF), F32), pltpu.VMEM((EXP, TOK, FF), F32),
-            pltpu.VMEM((TOK, 128), F32),
             pltpu.VMEM((8, 8, 128), F32), pltpu.VMEM((8, 8, 128), F32),
             pltpu.VMEM((TOK, 128), F32), pltpu.VMEM((4, 8, 128), F32), pltpu.VMEM((8, 8, 128), F32),
-            pltpu.VMEM((3, 2, ROWS, D), F32),
             pltpu.VMEM((3, 2, 2, 4, ROWS, HALF), F32), pltpu.VMEM((3, 2, 4, ROWS, HALF), F32),
             pltpu.VMEM((3, 2, 2, ROWS, HALF), F32), pltpu.VMEM((3, 2, 2, ROWS, HALF), F32),
             pltpu.VMEM((3, 2, ROWS, HALF), F32), pltpu.VMEM((3, 2, ROWS, HALF), F32),
-            dma((3,)), dma((1 + EXP,)), dma((11,)), dma((1,)), dma((4,)),
+            dma((3,)), dma((1 + EXP,)), dma((1,)), dma((4,)),
             dma((3, 2)), dma((12,)), dma((3,)), dma((24,)), dma((1,)), dma((1,)),
         ],
-        compiler_params=pltpu.CompilerParams(collective_id=0, has_side_effects=True, vmem_limit_bytes=60 * 1024 * 1024),
+        compiler_params=pltpu.CompilerParams(collective_id=0, has_side_effects=True, vmem_limit_bytes=50 * 1024 * 1024),
     )(x, dy, xa, idx, gates, wg, wu, wd, wq, wk, wv, wo)
 
 
@@ -479,16 +453,17 @@
         y_out[...] = y_in[...]
         dg_out[...] = dg_in[...]
 
-    dwg_ref[0] = jnp.dot(xt[...], da_ref[0], preferred_element_type=F32)
-    dwu_ref[0] = jnp.dot(xt[...], db_ref[0], preferred_element_type=F32)
+    dwg_ref[0] = jnp.dot(xt[...], da_ref[e], preferred_element_type=F32)
+    dwu_ref[0] = jnp.dot(xt[...], db_ref[e], preferred_element_type=F32)
     lane = lax.broadcasted_iota(jnp.int32, (TOK, 128), 1)
     g = jnp.sum(jnp.where(lane == e, gt_ref[...], 0.0), axis=1, keepdims=True)
     do = (g * dy_ref[...].astype(F32)).astype(BF)
-    dwd_ref[0] = lax.dot_general(h_ref[0], do, TN, preferred_element_type=F32)
+    dwd_ref[0] = lax.dot_general(h_ref[e], do, TN, preferred_element_type=F32)
 
 
 def weight_grads(xall, dyall, gt, h, da, db, y_t, dg):
     sds = jax.ShapeDtypeStruct
+    args = [pltpu.with_memory_space_constraint(v, pltpu.VMEM) for v in (xall, dyall, gt, h, da, db, y_t, dg)]
     whole = lambda shape: pl.BlockSpec(shape, lambda e: (0, 0))
     per = lambda a, b: pl.BlockSpec((1, a, b), lambda e: (e, 0, 0))
     return pl.pallas_call(
@@ -497,13 +472,12 @@
         grid=(EXP,),
         out_shape=[sds((EXP, D, FF), F32), sds((EXP, D, FF), F32), sds((EXP, FF, D), F32),
                    sds((ROWS, D), BF), sds((TOPK, ROWS), F32)],
-        in_specs=[whole((TOK, D)), whole((TOK, D)), whole((TOK, 128)), per(TOK, FF), per(TOK, FF), per(TOK, FF)]
-        + [whole((ROWS, D))] + [whole((TOPK, ROWS))],
+        in_specs=[pl.BlockSpec(memory_space=pltpu.VMEM)] * 8,
         out_specs=[per(D, FF), per(D, FF), per(FF, D)] + [whole((ROWS, D))] + [whole((TOPK, ROWS))],
         scratch_shapes=[pltpu.VMEM((D, TOK), BF)],
         cost_estimate=pl.CostEstimate(flops=3 * 2 * EXP * TOK * D * FF, bytes_accessed=34 * 1024 * 1024, transcendentals=0),
-        compiler_params=pltpu.CompilerParams(vmem_limit_bytes=62 * 1024 * 1024),
-    )(xall, dyall, gt, h, da, db, y_t, dg)
+        compiler_params=pltpu.CompilerParams(vmem_limit_bytes=40 * 1024 * 1024),
+    )(*args)
 
 
 def solution(mesh):

time: 56.5 us -> 54.3 us (0.961)
  Pallas kernels: 52.8 us -> 48.9 us
  waiting for transfers between devices: 0.01 us -> 1.78 us
    pallas_call x1, Pallas kernels: 13 us -> 10.1 us  [weight_grads(): pl.pallas_call(grads_kernel, name='weight_grads', grid=(EXP,), out_shape=...]
    ppermute x1, waiting for transfers between devices: 0.01 us -> 1.46 us  [local_step(): from_x = lax.ppermute(to_x, GROUP_AXES, [(g, g ^ 2) for g in range(8)])]
    pallas_call x1, Pallas kernels: 39.8 us -> 38.8 us  [exchange(): pl.pallas_call(exchange_kernel, name='exchange', out_shape=[pltpu.VMEM((R...]
  transfers between devices with their start and end apart: 2 -> 2, of which waited for: 0 -> 2; matrix products, arithmetic and copies ran while one was open for 0% -> 0% of each run, Pallas kernels for 23% -> 19%
where the time goes in v6:
time: 54.3 us; the launch traced here: 54.2 us
  Pallas kernels  48.9 us (90%)
  starting transfers between devices  2.03 us (4%)
  waiting for transfers between devices  1.78 us (3%)
  local copies, waits for them, and re-layouts  0.72 us (1%)
  between operations  0.65 us (1%)
    pallas_call x1, Pallas kernels, exchange(): pl.pallas_call(exchange_kernel, name='exchange', out_shape=[pltpu.VMEM((R...  38.8 us
    pallas_call x1, Pallas kernels, weight_grads(): pl.pallas_call(grads_kernel, name='weight_grads', grid=(EXP,), out_shape=...  10.1 us
    ppermute x1, starting transfers between devices, local_step(): from_y = lax.ppermute(to_y, GROUP_AXES, [(g, g ^ 4) for g in range(8)])  1.49 us
    ppermute x1, waiting for transfers between devices, local_step(): from_x = lax.ppermute(to_x, GROUP_AXES, [(g, g ^ 2) for g in range(8)])  1.46 us
  transfers between devices with their start and end apart: 2, of which 2 were waited for; matrix products, arithmetic and copies ran while one was open for 0% of the time, Pallas kernels for 19%

profile of v6, /device:TPU:0, one launch (start us, length us, event | category | flops | bytes accessed | tf_op | source)
XLA Modules:
  0.0 54.2 jit_solution(396809159663368457)
XLA Ops:
  0.6 38.8 %exchange.1 = (bf16[64,1024]{1,0:T(8,128)(2,1)S(1)}, f32[8,64]{1,0:T(8,128)S(1)}, f32[2,64,1024]{2,1,0:T(8,128)S(1)}, f32[2,64,1024]{2,1,0:T(8,128)S(1)}, f32[2,...) custom-call(bf16[64,1024]{1,0:T(8,128)(2,1)} %x_hbm.1, ...), custom_call_target="tpu_custom_call" | custom-call | tf_op jit(solution)/shard_map/exchange/pallas_call | solution.py:420
  39.4 0.5 %collective-permute-start = (f32[2,64,1024]{2,1,0:T(8,128)S(1)}, f32[2,64,1024]{2,1,0:T(8,128)S(1)}, u32[]{:S(2)}, u32[]{:S(2)}) collective-permute-start(f32[2,64,1024]{2,1,0:T(8,128)S(1)} %get-tuple-element.33), channel_id=1, source_target_pairs={{0,2},{1,3},{2,0},{3,1},{4,6},{5,7},{6,4},{7,5}} | collective-permute-start | bytes 1572872 | tf_op jit(solution)/shard_map/ppermute | solution.py:489
  40.0 1.5 %collective-permute-start.1 = (f32[2,64,1024]{2,1,0:T(8,128)S(1)}, f32[2,64,1024]{2,1,0:T(8,128)S(1)}, u32[]{:S(2)}, u32[]{:S(2)}) collective-permute-start(f32[2,64,1024]{2,1,0:T(8,128)S(1)} %get-tuple-element.34), channel_id=1, source_target_pairs={{0,4},{1,5},{2,6},{3,7},{4,0},{5,1},{6,2},{7,3}} | collective-permute-start | bytes 1572872 | tf_op jit(solution)/shard_map/ppermute | solution.py:490
  41.4 10.1 %weight_grads.1 = (f32[4,1024,512]{2,1,0:T(8,128)}, f32[4,1024,512]{2,1,0:T(8,128)}, f32[4,512,1024]{2,1,0:T(8,128)}, bf16[64,1024]{1,0:T(8,128)(2,1)}, f32[8,64]{1,0:T(8,128)}) custom-call(bf16[512,1024]{1,0:T(8,128)(2,1)S(1)} %get-tuple-element.23.x_ref, bf16[512,1024]{1,0:T(8,128)(2,1)S(1)} %get-tuple-element.24.dy_ref, ...), custom_call_target="tpu_custom_call" | custom-call | flops 6442450944 | bytes 35651584 | tf_op jit(solution)/shard_map/weight_grads/pallas_call | solution.py:469
  51.6 1.5 %collective-permute-done = f32[2,64,1024]{2,1,0:T(8,128)S(1)} collective-permute-done((f32[2,64,1024]{2,1,0:T(8,128)S(1)}, f32[2,64,1024]{2,1,0:T(8,128)S(1)}, u32[]{:S(2)}, u32[]{:S(2)}) %collective-permute-start) | collective-permute-done | bytes 524320 | tf_op jit(solution)/shard_map/ppermute | solution.py:489
  53.0 0.3 collective-permute-done.1
  53.4 0.1 add_convert_fusion
  53.5 0.7 %fusion = (bf16[1,64,1024]{2,1,0:T(8,128)(2,1)}, bf16[64,1024]{1,0:T(8,128)(2,1)}) fusion(bf16[2,64,1024]{2,1,0:T(8,128)(2,1)S(1)} %add_convert_fusion), kind=kLoop, calls=%fused_computation.2 | loop fusion | bytes 524288 | tf_op jit(solution)/shard_map/slice | solution.py:493
Async XLA Ops:
  39.4 13.6 %collective-permute-start = (f32[2,64,1024]{2,1,0:T(8,128)S(1)}, f32[2,64,1024]{2,1,0:T(8,128)S(1)}, u32[]{:S(2)}, u32[]{:S(2)}) collective-permute-start(f32[2,64,1024]{2,1,0:T(8,128)S(1)} %get-tuple-element.33), channel_id=1, source_target_pairs={{0,2},{1,3},{2,0},{3,1},{4,6},{5,7},{6,4},{7,5}} | collective-permute-start | bytes 1572872 | tf_op jit(solution)/shard_map/ppermute | solution.py:489
  40.0 13.4 %collective-permute-start.1 = (f32[2,64,1024]{2,1,0:T(8,128)S(1)}, f32[2,64,1024]{2,1,0:T(8,128)S(1)}, u32[]{:S(2)}, u32[]{:S(2)}) collective-permute-start(f32[2,64,1024]{2,1,0:T(8,128)S(1)} %get-tuple-element.34), channel_id=1, source_target_pairs={{0,4},{1,5},{2,6},{3,7},{4,0},{5,1},{6,2},{7,3}} | collective-permute-start | bytes 1572872 | tf_op jit(solution)/shard_map/ppermute | solution.py:490

commit v7 on v6

--- a/solution.py
+++ b/solution.py
@@ -27,11 +27,11 @@
 
 
 def exchange_kernel(x_hbm, dy_hbm, xa_hbm, idx_hbm, gate_hbm, wg_hbm, wu_hbm, wd_hbm, wq_hbm, wk_hbm, wv_hbm, wo_hbm,
-                    y_out, dg_out, tox, toy, owns, xall, dyall, hid, dag, dbg, gt,
-                    idx_ref, gate_ref, rows, wg, wu, wd, wqkv, wo, osv, act, gfac, gsend, grecv,
+                    y_out, dg_out, tox, toy, own_dx, own_at, xt, dyall, hid, dag, dbg, gt,
+                    idx_ref, gate_ref, rows, wg, wu, wd, wqkv, wo, wo_in, ctx, ctx_in, osv, act, gfac, gsend, grecv,
                     dgs, dsend, drecv,
                     part, pair, s1, r1, s2, r2,
-                    in_sem, w_sem, gs_sem, gr_sem, rs_s, rs_r, ag_s, ag_r, dd_s, dd_r):
+                    in_sem, w_sem, gs_sem, gr_sem, rs_s, rs_r, ag_s, ag_r, dd_s, dd_r, hd_s, hd_r):
     y = lax.axis_index('ei')
     o = lax.axis_index('eo')
     z = lax.axis_index('dp')
@@ -73,7 +73,8 @@
     wload = [pltpu.make_async_copy(wq_hbm, wqkv.at[0:128], w_sem.at[0]),
              pltpu.make_async_copy(wk_hbm, wqkv.at[128:192], w_sem.at[0]),
              pltpu.make_async_copy(wv_hbm, wqkv.at[192:256], w_sem.at[0]),
-             pltpu.make_async_copy(wo_hbm, wo, w_sem.at[0])]
+             pltpu.make_async_copy(wo_hbm.at[:, 0:HALF], wo.at[0], w_sem.at[0]),
+             pltpu.make_async_copy(wo_hbm.at[:, HALF:D], wo.at[1], w_sem.at[0])]
     for cp in wload:
         cp.start()
 
@@ -228,6 +229,13 @@
         for h in range(2):
             total = chip_sum(n, h, OWN) + r1[n, h, 1] + r2[n, h]
             out_ref[:, h * HALF:(h + 1) * HALF] = total.astype(BF)
+
+    def head_copy(src, dst, slot, where):
+        return remote(src, dst, hd_s.at[slot // 2], hd_r.at[slot], where)
+
+    wo_cps = [head_copy(wo.at[h], wo_in.at[h], h, (xn, yn)[h]) for h in range(2)]
+    ctx_cps = [head_copy(ctx.at[q], ctx_in.at[h, i], 2 + h, (xn, yn)[h])
+               for h, qn in ((0, qx), (1, qy)) for i, q in ((0, qn), (1, qd))]
 
     def gate_table(k):
         tiles = grecv.at[0:1 if k == OWN else 2]
@@ -327,26 +335,42 @@
         sms = [jnp.sum(ex, axis=1, keepdims=True) for ex in exs]
         prs = [(ex / sm).astype(BF) for ex, sm in zip(exs, sms)]
         ctxs = [jnp.dot(pr, v[:, 192:256], preferred_element_type=F32).astype(BF) for pr, v in zip(prs, qkvs)]
-        return jnp.concatenate([jnp.concatenate([v[0:128], v[128:256]], axis=1) for v in ctxs], axis=0)
-
-    def attention_out(ctx):
-        for q in range(4):
-            out = jnp.dot(ctx[q * 128:(q + 1) * 128], wo[...], preferred_element_type=F32)
-            for cc in range(2):
-                for h in range(2):
-                    part[0, cc, h, q] = out[cc * 64:(cc + 1) * 64, h * HALF:(h + 1) * HALF]
-
-    def leave(i, n):
+        for q, v in enumerate(ctxs):
+            ctx[q] = jnp.concatenate([v[0:128], v[128:256]], axis=1)
+
+    def attention_out():
+        for h in range(2):
+            wo_cps[h].wait_recv()
+            both = ctx_in.at[h]
+            head_copy(both, both, 2 + h, sib).wait_recv()
+            for i, k in ((0, OWN), (1, second[h])):
+                out = (jnp.dot(ctx[chips[k]], wo[h], preferred_element_type=F32)
+                       + jnp.dot(ctx_in[h, i], wo_in[h], preferred_element_type=F32))
+                for cc in range(2):
+                    part[0, cc, h, chips[k]] = out[cc * 64:(cc + 1) * 64]
+        for h in range(2):
+            rsc[0][2 * OWN + h].start()
+            rsc[0][2 * second[h] + h].start()
+
+    def leave_attention():
+        ref = pair.at[0, 0]
+        remote(ref, ref, rs_s.at[0, 0], rs_r.at[rs_slot(0, 2 * OWN)], sib).wait_recv()
+        for h, dst in ((0, toy), (1, tox)):
+            dst[:, D:D + HALF] = chip_sum(0, h, second[h])
+            own_at[:, h * HALF:(h + 1) * HALF] = chip_sum(0, h, OWN)
+
+    def leave_dx():
+        n = 2
         rs_wait(n, 2 * OWN, 6)
         rs_wait(n, 8, 2)
         for h in range(2):
             cols = slice(h * HALF, (h + 1) * HALF)
             near = chip_sum(n, h, first[h])
             far = chip_sum(n, h, second[h]) + r1[n, h, 0]
-            mine = chip_sum(n, h, OWN)
-            tox[i, :, cols] = near if h == 0 else far
-            toy[i, :, cols] = far if h == 0 else near
-            owns[i, :, cols] = mine
+            tox[:, cols] = near if h == 0 else far
+            toy[:, cols] = far if h == 0 else near
+            own_dx[:, cols] = chip_sum(n, h, OWN)
+
     pltpu.make_async_copy(wg_hbm.at[0, 0:6 * ROWS], wg.at[0, 0:6 * ROWS], in_sem.at[0]).wait()
     pl.semaphore_wait(barrier, len(rels))
     for cp in gate_cps.values():
@@ -369,18 +393,15 @@
     gate_table(DI)
     ag_forward(DY)
     ag_rows(XT, 9, ROWS).wait_recv()
-    xall[...] = rows[XT]
-    experts(forward([DI]), {1: lambda: (rs_near(1, 0), rs_near(1, 1), ag_last(XA)), 2: lambda: ag_pair(DY)})
+    experts(forward([DI]), {1: lambda: (rs_near(1, 0), rs_near(1, 1), ag_last(XA)), 2: lambda: ag_pair(DY), 3: lambda: ag_last(DY)})
     rs_pair(1, DI)
-    ctx = attention_context()
-    ag_last(DY)
+    attention_context()
     rs_far(1)
-    attention_out(ctx)
-    for k in (DI, X, Y, OWN):
-        rs_pair(0, k)
+    for cp in ctx_cps + wo_cps:
+        cp.start()
     ag_rows(DY, 0, 4 * ROWS).wait_recv()
     dyall[...] = rows[DY]
-    experts(backward(2 * (1 - y), 2 * (1 - y) + 1, (1 - y) * 256, True), {0: lambda: rs_far(0), 2: lambda: rs_second(1)})
+    experts(backward(2 * (1 - y), 2 * (1 - y) + 1, (1 - y) * 256, True), {3: lambda: rs_second(1)})
     rs_pair(2, DI)
     rs_pair(2, Y)
     for q in range(4):
@@ -391,7 +412,7 @@
     experts(backward(2 * y, 2 * y + 1, y * 256, False), {0: lambda: rs_far(2)})
     rs_pair(2, X)
     rs_pair(2, OWN)
-    leave(0, 0)
+    attention_out()
     rs_wait_dg = drecv.at[0:7]
     remote(rs_wait_dg, rs_wait_dg, dd_s.at[0], dd_r.at[0], sib).wait_recv()
     both = drecv[...].reshape(64, 128)
@@ -400,7 +421,9 @@
         hit = row_exp == idx_ref[j:j + 1, :]
         dg_out[j:j + 1, :] = jnp.sum(jnp.where(hit & is_gate, mine, 0.0), axis=0, keepdims=True)
     rs_final(1, y_out)
-    leave(1, 2)
+    leave_attention()
+    xt[...] = rows[XT].T
+    leave_dx()
 
     for t in range(3):
         ref = rows.at[t, 0:7 * ROWS]
@@ -408,9 +431,11 @@
     tiles = gsend.at[0:7]
     remote(tiles, tiles, gs_sem.at[0], gr_sem.at[0], sib).wait_send()
     remote(tiles, tiles, dd_s.at[0], dd_r.at[0], sib).wait_send()
-    for n in range(3):
-        for ref, k in ((part.at[n, 0], 0), (pair.at[n, :, 0:3] if n == 1 else pair.at[n, 0, 0:2], 1)):
-            remote(ref, ref, rs_s.at[n, k], rs_r.at[0], sib).wait_send()
+    for ref, n, k in ((pair.at[0, 0], 0, 0), (part.at[1, 0], 1, 0), (part.at[2, 0], 2, 0),
+                      (pair.at[1, :, 0:3], 1, 1), (pair.at[2, 0, 0:2], 2, 1)):
+        remote(ref, ref, rs_s.at[n, k], rs_r.at[0], sib).wait_send()
+    remote(wo, wo, hd_s.at[0], hd_r.at[0], sib).wait_send()
+    remote(ctx, ctx, hd_s.at[1], hd_r.at[0], sib).wait_send()
 
 
 def exchange(x, dy, xa, idx, gates, wg, wu, wd, wq, wk, wv, wo):
@@ -420,15 +445,16 @@
     return pl.pallas_call(
         exchange_kernel,
         name='exchange',
-        out_shape=[pltpu.VMEM((ROWS, D), BF), pltpu.VMEM((TOPK, ROWS), F32)] + [pltpu.VMEM((2, ROWS, D), F32)] * 3 + [pltpu.VMEM((TOK, D), BF)] * 2
+        out_shape=[pltpu.VMEM((ROWS, D), BF), pltpu.VMEM((TOPK, ROWS), F32)] + [pltpu.VMEM((ROWS, D + HALF), F32)] * 2 + [pltpu.VMEM((ROWS, D), F32)] * 2 + [pltpu.VMEM((D, TOK), BF), pltpu.VMEM((TOK, D), BF)]
         + [pltpu.VMEM((EXP, TOK, FF), BF)] * 3 + [pltpu.VMEM((TOK, 128), F32)],
         in_specs=[any_spec] * 12,
-        out_specs=[vmem] * 11,
+        out_specs=[vmem] * 12,
         scratch_shapes=[
             pltpu.VMEM((TOPK, ROWS), jnp.int32), pltpu.VMEM((TOPK, ROWS), F32),
             pltpu.VMEM((3, TOK, D), BF),
             pltpu.VMEM((EXP, D, FF), BF), pltpu.VMEM((EXP, D, FF), BF), pltpu.VMEM((EXP, FF, D), BF),
-            pltpu.VMEM((256, D), BF), pltpu.VMEM((128, D), BF),
+            pltpu.VMEM((256, D), BF), pltpu.VMEM((2, 128, HALF), BF), pltpu.VMEM((2, 128, HALF), BF),
+            pltpu.VMEM((4, 128, 128), BF), pltpu.VMEM((2, 2, 128, 128), BF),
             pltpu.VMEM((EXP, TOK, D), BF),
             pltpu.VMEM((EXP, TOK, FF), F32), pltpu.VMEM((EXP, TOK, FF), F32),
             pltpu.VMEM((8, 8, 128), F32), pltpu.VMEM((8, 8, 128), F32),
@@ -437,60 +463,89 @@
             pltpu.VMEM((3, 2, 2, ROWS, HALF), F32), pltpu.VMEM((3, 2, 2, ROWS, HALF), F32),
             pltpu.VMEM((3, 2, ROWS, HALF), F32), pltpu.VMEM((3, 2, ROWS, HALF), F32),
             dma((3,)), dma((1 + EXP,)), dma((1,)), dma((4,)),
-            dma((3, 2)), dma((12,)), dma((3,)), dma((24,)), dma((1,)), dma((1,)),
+            dma((3, 2)), dma((12,)), dma((3,)), dma((24,)), dma((1,)), dma((1,)), dma((2,)), dma((4,)),
         ],
         compiler_params=pltpu.CompilerParams(collective_id=0, has_side_effects=True, vmem_limit_bytes=50 * 1024 * 1024),
     )(x, dy, xa, idx, gates, wg, wu, wd, wq, wk, wv, wo)
 
 
-def grads_kernel(x_ref, dy_ref, gt_ref, h_ref, da_ref, db_ref, y_in, dg_in,
-                 dwg_ref, dwu_ref, dwd_ref, y_out, dg_out, xt):
-    e = pl.program_id(0)
-
-    @pl.when(e == 0)
-    def _():
-        xt[...] = x_ref[...].T
-        y_out[...] = y_in[...]
-        dg_out[...] = dg_in[...]
-
-    dwg_ref[0] = jnp.dot(xt[...], da_ref[e], preferred_element_type=F32)
-    dwu_ref[0] = jnp.dot(xt[...], db_ref[e], preferred_element_type=F32)
-    lane = lax.broadcasted_iota(jnp.int32, (TOK, 128), 1)
-    g = jnp.sum(jnp.where(lane == e, gt_ref[...], 0.0), axis=1, keepdims=True)
-    do = (g * dy_ref[...].astype(F32)).astype(BF)
-    dwd_ref[0] = lax.dot_general(h_ref[e], do, TN, preferred_element_type=F32)
-
-
-def weight_grads(xall, dyall, gt, h, da, db, y_t, dg):
+def grads_kernel(xt_ref, dy_ref, gt_ref, h_ref, da_ref, db_ref, y_in, dg_in, dwg_out, dwu_out, dwd_out, y_out, dg_out,
+                 gate_buf, up_buf, down_buf, sem, small_sem):
+    small = [pltpu.make_async_copy(y_in, y_out, small_sem.at[0]), pltpu.make_async_copy(dg_in, dg_out, small_sem.at[1])]
+    for cp in small:
+        cp.start()
+
+    def leave(e, slot, n):
+        buf, out = ((gate_buf, dwg_out), (up_buf, dwu_out), (down_buf, dwd_out))[n]
+        return pltpu.make_async_copy(buf.at[slot], out.at[e], sem.at[n, slot])
+
+    def body(e, carry):
+        slot = e % 2
+
+        @pl.when(e >= 2)
+        def _():
+            for n in range(3):
+                leave(e - 2, slot, n).wait()
+        gate_buf[slot] = jnp.dot(xt_ref[...], da_ref[e], preferred_element_type=F32)
+        leave(e, slot, 0).start()
+        up_buf[slot] = jnp.dot(xt_ref[...], db_ref[e], preferred_element_type=F32)
+        leave(e, slot, 1).start()
+        lane = lax.broadcasted_iota(jnp.int32, (TOK, 128), 1)
+        g = jnp.sum(jnp.where(lane == e, gt_ref[...], 0.0), axis=1, keepdims=True)
+        do = (g * dy_ref[...].astype(F32)).astype(BF)
+        down_buf[slot] = lax.dot_general(h_ref[e], do, TN, preferred_element_type=F32)
+        leave(e, slot, 2).start()
+        return carry
+
+    lax.fori_loop(0, EXP, body, 0)
+    for e in (EXP - 2, EXP - 1):
+        for n in range(3):
+            leave(e, e % 2, n).wait()
+    for cp in small:
+        cp.wait()
+
+
+def weight_grads(*args):
     sds = jax.ShapeDtypeStruct
-    args = [pltpu.with_memory_space_constraint(v, pltpu.VMEM) for v in (xall, dyall, gt, h, da, db, y_t, dg)]
-    whole = lambda shape: pl.BlockSpec(shape, lambda e: (0, 0))
-    per = lambda a, b: pl.BlockSpec((1, a, b), lambda e: (e, 0, 0))
+    args = [pltpu.with_memory_space_constraint(v, pltpu.VMEM) for v in args]
     return pl.pallas_call(
         grads_kernel,
         name='weight_grads',
-        grid=(EXP,),
         out_shape=[sds((EXP, D, FF), F32), sds((EXP, D, FF), F32), sds((EXP, FF, D), F32),
                    sds((ROWS, D), BF), sds((TOPK, ROWS), F32)],
         in_specs=[pl.BlockSpec(memory_space=pltpu.VMEM)] * 8,
-        out_specs=[per(D, FF), per(D, FF), per(FF, D)] + [whole((ROWS, D))] + [whole((TOPK, ROWS))],
-        scratch_shapes=[pltpu.VMEM((D, TOK), BF)],
+        out_specs=[pl.BlockSpec(memory_space=pl.ANY)] * 5,
+        scratch_shapes=[pltpu.VMEM((2, D, FF), F32), pltpu.VMEM((2, D, FF), F32), pltpu.VMEM((2, FF, D), F32),
+                        pltpu.SemaphoreType.DMA((3, 2)), pltpu.SemaphoreType.DMA((2,))],
         cost_estimate=pl.CostEstimate(flops=3 * 2 * EXP * TOK * D * FF, bytes_accessed=34 * 1024 * 1024, transcendentals=0),
         compiler_params=pltpu.CompilerParams(vmem_limit_bytes=40 * 1024 * 1024),
     )(*args)
 
 
+def combine_kernel(dx_ref, at_ref, x_ref, y_ref, dx_out, at_out):
+    dx_out[...] = (dx_ref[...] + x_ref[:, 0:D] + y_ref[:, 0:D]).astype(BF)
+    at_out[:, 0:HALF] = (at_ref[:, 0:HALF] + y_ref[:, D:D + HALF]).astype(BF)
+    at_out[:, HALF:D] = (at_ref[:, HALF:D] + x_ref[:, D:D + HALF]).astype(BF)
+
+
+def combine(*args):
+    sds = jax.ShapeDtypeStruct
+    args = [pltpu.with_memory_space_constraint(v, pltpu.VMEM) for v in args]
+    vmem = pl.BlockSpec(memory_space=pltpu.VMEM)
+    return pl.pallas_call(combine_kernel, name='combine', out_shape=[sds((ROWS, D), BF)] * 2,
+                          in_specs=[vmem] * 4, out_specs=[vmem] * 2)(*args)
+
+
 def solution(mesh):
     def local_step(x_tokens, expert_idx, gate_vals, dy_tokens, w_gate, w_up, w_down, x_attn, w_query, w_key, w_value, w_out):
-        y_p, dg_p, to_x, to_y, own, xall, dyall, h, da, db, gt = exchange(
+        y_p, dg_p, to_x, to_y, own_dx, own_at, xt, dyall, h, da, db, gt = exchange(
             x_tokens, dy_tokens, x_attn.reshape(ROWS, D), expert_idx.T, gate_vals.T, w_gate, w_up, w_down,
             w_query.transpose(1, 2, 0).reshape(128, D), w_key.transpose(1, 2, 0).reshape(64, D),
             w_value.transpose(1, 2, 0).reshape(64, D), w_out.reshape(128, D))
         from_x = lax.ppermute(to_x, GROUP_AXES, [(g, g ^ 2) for g in range(8)])
         from_y = lax.ppermute(to_y, GROUP_AXES, [(g, g ^ 4) for g in range(8)])
-        dwg, dwu, dwd, y_t, dg = weight_grads(xall, dyall, gt, h, da, db, y_p, dg_p)
-        both = (own + from_x + from_y).astype(BF)
-        at, dx_t = both[0], both[1]
+        dwg, dwu, dwd, y_t, dg = weight_grads(xt, dyall, gt, h, da, db, y_p, dg_p)
+        dx_t, at = combine(own_dx, own_at, from_x, from_y)
         return y_t, dx_t, dg.T, dwg, dwu, dwd, at.reshape(1, ROWS, D)
 
     spec_rows = P(TOKEN_AXES, None)

time: 54.3 us -> 53 us (0.976)
  waiting for transfers between devices: 1.78 us -> 0.06 us
  Pallas kernels: 48.9 us -> 50.2 us
  local copies, waits for them, and re-layouts: 0.72 us -> 0 us
    pallas_call x1, Pallas kernels: 38.8 us -> 40.3 us  [exchange(): pl.pallas_call(exchange_kernel, name='exchange', out_shape=[pltpu.VMEM((R...]
    ppermute x1, waiting for transfers between devices: 1.46 us -> 0.01 us  [local_step(): from_x = lax.ppermute(to_x, GROUP_AXES, [(g, g ^ 2) for g in range(8)])]
    slice x1 -> x0, local copies, waits for them, and re-layouts: 0.72 us -> none  [local_step(): at, dx_t = (both[0], both[1])]
    pallas_call x1 -> x2, Pallas kernels: 10.1 us -> 9.91 us  [the longest x1 9.16 us: weight_grads(): pl.pallas_call(grads_kernel, name='weight_grads', out_shape=[sds((EXP, D,...]
  transfers between devices with their start and end apart: 2 -> 2, of which waited for: 2 -> 1; matrix products, arithmetic and copies ran while one was open for 0% -> 0% of each run, Pallas kernels for 19% -> 17%
where the time goes in v7:
time: 53 us; the launch traced here: 52.9 us
  Pallas kernels  50.2 us (95%)
  starting transfers between devices  2.03 us (4%)
  between operations  0.66 us (1%)
    pallas_call x1, Pallas kernels, exchange(): pl.pallas_call(exchange_kernel, name='exchange', out_shape=[pltpu.VMEM((R...  40.3 us
    pallas_call x1, Pallas kernels, weight_grads(): pl.pallas_call(grads_kernel, name='weight_grads', out_shape=[sds((EXP, D,...  9.16 us
    ppermute x1, starting transfers between devices, local_step(): from_y = lax.ppermute(to_y, GROUP_AXES, [(g, g ^ 4) for g in range(8)])  1.32 us
  transfers between devices with their start and end apart: 2, of which 1 were waited for; matrix products, arithmetic and copies ran while one was open for 0% of the time, Pallas kernels for 17%

profile of v7, /device:TPU:0, one launch (start us, length us, event | category | flops | bytes accessed | tf_op | source)
XLA Modules:
  0.0 52.9 jit_solution(8510385931489302453)
XLA Ops:
  0.6 40.3 %exchange.1 = (bf16[64,1024]{1,0:T(8,128)(2,1)S(1)}, f32[8,64]{1,0:T(8,128)S(1)}, f32[64,1536]{1,0:T(8,128)S(1)}, f32[64,1536]{1,0:T(8,128)S(1)}, f32[64,1024]{1...) custom-call(bf16[64,1024]{1,0:T(8,128)(2,1)} %x_hbm.1, ...), custom_call_target="tpu_custom_call" | custom-call | tf_op jit(solution)/shard_map/exchange/pallas_call | solution.py:445
  40.9 0.7 %collective-permute-start = (f32[64,1536]{1,0:T(8,128)S(1)}, f32[64,1536]{1,0:T(8,128)S(1)}, u32[]{:S(2)}, u32[]{:S(2)}) collective-permute-start(f32[64,1536]{1,0:T(8,128)S(1)} %get-tuple-element.37), channel_id=1, source_target_pairs={{0,2},{1,3},{2,0},{3,1},{4,6},{5,7},{6,4},{7,5}} | collective-permute-start | bytes 1179656 | tf_op jit(solution)/shard_map/ppermute | solution.py:545
  41.6 1.3 %collective-permute-start.1 = (f32[64,1536]{1,0:T(8,128)S(1)}, f32[64,1536]{1,0:T(8,128)S(1)}, u32[]{:S(2)}, u32[]{:S(2)}) collective-permute-start(f32[64,1536]{1,0:T(8,128)S(1)} %get-tuple-element.38), channel_id=1, source_target_pairs={{0,4},{1,5},{2,6},{3,7},{4,0},{5,1},{6,2},{7,3}} | collective-permute-start | bytes 1179656 | tf_op jit(solution)/shard_map/ppermute | solution.py:546
  42.9 9.2 %weight_grads.1 = (f32[4,1024,512]{2,1,0:T(8,128)}, f32[4,1024,512]{2,1,0:T(8,128)}, f32[4,512,1024]{2,1,0:T(8,128)}, bf16[64,1024]{1,0:T(8,128)(2,1)}, f32[8,64]{1,0:T(8,128)}) custom-call(bf16[1024,512]{1,0:T(8,128)(2,1)S(1)} %get-tuple-element.26.xt_ref, bf16[512,1024]{1,0:T(8,128)(2,1)S(1)} %get-tuple-element.27.dy_ref, ...), custom_call_target="tpu_custom_call" | custom-call | flops 6442450944 | bytes 35651584 | tf_op jit(solution)/shard_map/weight_grads/pallas_call | solution.py:511
  52.1 0.0 collective-permute-done.x_ref
  52.1 0.1 collective-permute-done.1.y_ref
  52.2 0.8 %combine.1 = (bf16[64,1024]{1,0:T(8,128)(2,1)}, bf16[64,1024]{1,0:T(8,128)(2,1)}) custom-call(f32[64,1024]{1,0:T(8,128)S(1)} %get-tuple-element.35.dx_ref, f32[64,1024]{1,0:T(8,128)S(1)} %get-tuple-element.36.at_ref, f32[64,1536]{1,0:T(8,128)S(1)} %collective-permute-done.x_ref, f32[64,1536]{1,0:T(8,128)S(1)} %collective-permute-done.1.y_ref), custom_call_target="tpu_custom_call" | custom-call | tf_op jit(solution)/shard_map/combine/pallas_call | solution.py:535
Async XLA Ops:
  40.9 11.2 %collective-permute-start = (f32[64,1536]{1,0:T(8,128)S(1)}, f32[64,1536]{1,0:T(8,128)S(1)}, u32[]{:S(2)}, u32[]{:S(2)}) collective-permute-start(f32[64,1536]{1,0:T(8,128)S(1)} %get-tuple-element.37), channel_id=1, source_target_pairs={{0,2},{1,3},{2,0},{3,1},{4,6},{5,7},{6,4},{7,5}} | collective-permute-start | bytes 1179656 | tf_op jit(solution)/shard_map/ppermute | solution.py:545
  41.6 10.6 %collective-permute-start.1 = (f32[64,1536]{1,0:T(8,128)S(1)}, f32[64,1536]{1,0:T(8,128)S(1)}, u32[]{:S(2)}, u32[]{:S(2)}) collective-permute-start(f32[64,1536]{1,0:T(8,128)S(1)} %get-tuple-element.38), channel_id=1, source_target_pairs={{0,4},{1,5},{2,6},{3,7},{4,0},{5,1},{6,2},{7,3}} | collective-permute-start | bytes 1179656 | tf_op jit(solution)/shard_map/ppermute | solution.py:546

commit v8 on v7

--- a/solution.py
+++ b/solution.py
@@ -61,7 +61,7 @@
     for cp in tables:
         cp.start()
     for t, src in ((XT, x_hbm), (DY, dy_hbm), (XA, xa_hbm)):
-        pltpu.make_async_copy(src, rows.at[t, own], in_sem.at[0]).start()
+        pltpu.make_async_copy(src, rows.at[t, own], in_sem.at[0 if t == XT else 3]).start()
 
     def expert_load(e):
         return [pltpu.make_async_copy(src.at[e], dst.at[e], w_sem.at[1 + e])
@@ -80,21 +80,17 @@
 
     for cp in tables:
         cp.wait()
-    row = lax.broadcasted_iota(jnp.int32, (64, ROWS), 0)
-    row_exp = (row // 8) * 4 + row % 4
-    is_gate = (row % 8) < 4
-    table = jnp.zeros((64, ROWS), F32)
+    exp_row = lax.broadcasted_iota(jnp.int32, (32, ROWS), 0)
+    table = jnp.zeros((32, ROWS), F32)
+    marks = jnp.zeros((32, ROWS), F32)
     for j in range(TOPK):
-        hit = row_exp == idx_ref[j:j + 1, :]
-        table = table + jnp.where(hit, jnp.where(is_gate, gate_ref[j:j + 1, :], 1.0), 0.0)
-    blank = jnp.zeros((64, ROWS), F32)
-    wide = jnp.where(c == 0, jnp.concatenate([table, blank], axis=1), jnp.concatenate([blank, table], axis=1))
+        hit = exp_row == idx_ref[j:j + 1, :]
+        table = table + jnp.where(hit, gate_ref[j:j + 1, :], 0.0)
+        marks = marks + jnp.where(hit, 1.0, 0.0)
+    wide = jnp.concatenate([table, marks], axis=1)
     for d in range(8):
-        gsend[d] = wide[d * 8:(d + 1) * 8, :]
+        gsend[d] = wide[d * EXP:(d + 1) * EXP, :]
     grecv[me] = gsend[me]
-    dgs[...] = jnp.zeros((TOK, 128), F32)
-    part[1] = jnp.zeros(part.shape[1:], F32)
-    part[2] = jnp.zeros(part.shape[1:], F32)
 
     def blk(t, q, off=0, n=ROWS):
         return rows.at[t, pl.ds(pl.multiple_of(q * 128 + c * ROWS + off, 32), n)]
@@ -105,9 +101,9 @@
     hr = ROWS // 2
 
     def gather_slot(t, k):
-        if t == XT:
-            return min(k, 9)
-        return (10 if t == XA else 17) + (k - 1 if 1 <= k <= 6 else 6)
+        if 1 <= k <= 6:
+            return 3 * t + (0 if k in (1, 3) else 1 if k in (2, 4) else 2)
+        return 9 + t if t != XT else {0: 12, 7: 13, 8: 14}.get(k, 10)
 
     def gather_copies(t):
         def cp(k, ref, where):
@@ -134,21 +130,18 @@
             ag[t][k].start()
 
     def ag_forward(t):
-        ag[t][1].wait_recv()
+        ag_rows(t, 1, ROWS).wait_recv()
         ag[t][5].start()
-        ag[t][3].wait_recv()
         ag[t][6].start()
 
     def ag_pair(t):
-        ag[t][2].wait_recv()
+        ag_rows(t, 2, ROWS).wait_recv()
         ag[t][7].start()
-        ag[t][4].wait_recv()
         ag[t][8].start()
 
     def ag_last(t):
-        ag[t][5].wait_recv()
+        ag_rows(t, 5, ROWS).wait_recv()
         ag[t][9].start()
-        ag[t][6].wait_recv()
         ag[t][10].start()
 
     def ag_rows(t, k, n):
@@ -233,7 +226,7 @@
     def head_copy(src, dst, slot, where):
         return remote(src, dst, hd_s.at[slot // 2], hd_r.at[slot], where)
 
-    wo_cps = [head_copy(wo.at[h], wo_in.at[h], h, (xn, yn)[h]) for h in range(2)]
+    wo_cps = [head_copy(wo.at[h, r:r + 64], wo_in.at[h, r:r + 64], h, (xn, yn)[h]) for r in (0, 64) for h in range(2)]
     ctx_cps = [head_copy(ctx.at[q], ctx_in.at[h, i], 2 + h, (xn, yn)[h])
                for h, qn in ((0, qx), (1, qy)) for i, q in ((0, qn), (1, qd))]
 
@@ -241,7 +234,9 @@
         tiles = grecv.at[0:1 if k == OWN else 2]
         remote(tiles, tiles, gs_sem.at[0], gr_sem.at[k], sib).wait_recv()
         q = chips[k]
-        tile = grecv[2 * q] + grecv[2 * q + 1]
+        t0, t1 = grecv[2 * q], grecv[2 * q + 1]
+        tile = jnp.concatenate([jnp.concatenate([t0[:, :ROWS], t1[:, :ROWS]], axis=1),
+                                jnp.concatenate([t0[:, ROWS:], t1[:, ROWS:]], axis=1)], axis=0)
         gt[pl.ds(pl.multiple_of(q * 128, 128), 128), :] = jnp.concatenate([tile, jnp.zeros((120, 128), F32)], axis=0).T
 
     def pick(tile, e):
@@ -321,7 +316,6 @@
 
     def attention_context():
         ag_rows(XA, 0, 4 * ROWS).wait_recv()
-        pltpu.make_async_copy(wg_hbm.at[0, 0:768], wg.at[0, 0:768], w_sem.at[0]).wait()
         causal_r = lax.broadcasted_iota(jnp.int32, (256, 128), 0) % 128
         causal_c = lax.broadcasted_iota(jnp.int32, (256, 128), 1)
         keep = (causal_r >= causal_c) & (causal_r // 64 == causal_c // 64)
@@ -340,7 +334,7 @@
 
     def attention_out():
         for h in range(2):
-            wo_cps[h].wait_recv()
+            head_copy(wo_in.at[h], wo_in.at[h], h, sib).wait_recv()
             both = ctx_in.at[h]
             head_copy(both, both, 2 + h, sib).wait_recv()
             for i, k in ((0, OWN), (1, second[h])):
@@ -371,12 +365,16 @@
             toy[:, cols] = far if h == 0 else near
             own_dx[:, cols] = chip_sum(n, h, OWN)
 
-    pltpu.make_async_copy(wg_hbm.at[0, 0:6 * ROWS], wg.at[0, 0:6 * ROWS], in_sem.at[0]).wait()
+    pltpu.make_async_copy(x_hbm, rows.at[XT, own], in_sem.at[0]).wait()
     pl.semaphore_wait(barrier, len(rels))
+    ag_own(XT)
     for cp in gate_cps.values():
         cp.start()
-    ag_own(XT)
+    pltpu.make_async_copy(wg_hbm.at[0, 0:4 * ROWS], wg.at[0, 0:4 * ROWS], in_sem.at[3]).wait()
     ag_own(XA)
+    dgs[...] = jnp.zeros((TOK, 128), F32)
+    part[1] = jnp.zeros(part.shape[1:], F32)
+    part[2] = jnp.zeros(part.shape[1:], F32)
     gate_table(OWN)
     ag[XT][0].wait_recv()
     experts(forward([OWN], True), {2: lambda: ag_forward(XT)})
@@ -392,12 +390,16 @@
     rs_pair(1, Y)
     gate_table(DI)
     ag_forward(DY)
+    pltpu.make_async_copy(wg_hbm.at[0, 0:768], wg.at[0, 0:768], w_sem.at[0]).wait()
+    for cp in wo_cps[:2]:
+        cp.start()
     ag_rows(XT, 9, ROWS).wait_recv()
-    experts(forward([DI]), {1: lambda: (rs_near(1, 0), rs_near(1, 1), ag_last(XA)), 2: lambda: ag_pair(DY), 3: lambda: ag_last(DY)})
+    experts(forward([DI]), {1: lambda: (rs_near(1, 0), rs_near(1, 1), ag_last(XA)), 2: lambda: ag_pair(DY)})
     rs_pair(1, DI)
+    ag_last(DY)
     attention_context()
     rs_far(1)
-    for cp in ctx_cps + wo_cps:
+    for cp in ctx_cps + wo_cps[2:]:
         cp.start()
     ag_rows(DY, 0, 4 * ROWS).wait_recv()
     dyall[...] = rows[DY]
@@ -405,7 +407,7 @@
     rs_pair(2, DI)
     rs_pair(2, Y)
     for q in range(4):
-        dsend[q] = dgs[q * 128:(q + 1) * 128, :].T[0:8, :]
+        dsend[q] = dgs[q * 128:(q + 1) * 128, :].T[0:EXP, :]
     drecv[me] = dsend[q0]
     for cp in dg_cps.values():
         cp.start()
@@ -415,11 +417,11 @@
     attention_out()
     rs_wait_dg = drecv.at[0:7]
     remote(rs_wait_dg, rs_wait_dg, dd_s.at[0], dd_r.at[0], sib).wait_recv()
-    both = drecv[...].reshape(64, 128)
+    both = jnp.concatenate([drecv[d] for d in range(8)], axis=0)
     mine = jnp.where(c == 0, both[:, 0:ROWS], both[:, ROWS:128])
     for j in range(TOPK):
-        hit = row_exp == idx_ref[j:j + 1, :]
-        dg_out[j:j + 1, :] = jnp.sum(jnp.where(hit & is_gate, mine, 0.0), axis=0, keepdims=True)
+        hit = exp_row == idx_ref[j:j + 1, :]
+        dg_out[j:j + 1, :] = jnp.sum(jnp.where(hit, mine, 0.0), axis=0, keepdims=True)
     rs_final(1, y_out)
     leave_attention()
     xt[...] = rows[XT].T
@@ -457,13 +459,13 @@
             pltpu.VMEM((4, 128, 128), BF), pltpu.VMEM((2, 2, 128, 128), BF),
             pltpu.VMEM((EXP, TOK, D), BF),
             pltpu.VMEM((EXP, TOK, FF), F32), pltpu.VMEM((EXP, TOK, FF), F32),
-            pltpu.VMEM((8, 8, 128), F32), pltpu.VMEM((8, 8, 128), F32),
-            pltpu.VMEM((TOK, 128), F32), pltpu.VMEM((4, 8, 128), F32), pltpu.VMEM((8, 8, 128), F32),
+            pltpu.VMEM((8, EXP, 128), F32), pltpu.VMEM((8, EXP, 128), F32),
+            pltpu.VMEM((TOK, 128), F32), pltpu.VMEM((4, EXP, 128), F32), pltpu.VMEM((8, EXP, 128), F32),
             pltpu.VMEM((3, 2, 2, 4, ROWS, HALF), F32), pltpu.VMEM((3, 2, 4, ROWS, HALF), F32),
             pltpu.VMEM((3, 2, 2, ROWS, HALF), F32), pltpu.VMEM((3, 2, 2, ROWS, HALF), F32),
             pltpu.VMEM((3, 2, ROWS, HALF), F32), pltpu.VMEM((3, 2, ROWS, HALF), F32),
-            dma((3,)), dma((1 + EXP,)), dma((1,)), dma((4,)),
-            dma((3, 2)), dma((12,)), dma((3,)), dma((24,)), dma((1,)), dma((1,)), dma((2,)), dma((4,)),
+            dma((4,)), dma((1 + EXP,)), dma((1,)), dma((4,)),
+            dma((3, 2)), dma((12,)), dma((3,)), dma((15,)), dma((1,)), dma((1,)), dma((2,)), dma((4,)),
         ],
         compiler_params=pltpu.CompilerParams(collective_id=0, has_side_effects=True, vmem_limit_bytes=50 * 1024 * 1024),
     )(x, dy, xa, idx, gates, wg, wu, wd, wq, wk, wv, wo)

time: 53 us -> 52 us (0.981)
  Pallas kernels: 50.2 us -> 48.6 us
  waiting for transfers between devices: 0.06 us -> 0.69 us
    pallas_call x1, Pallas kernels: 40.3 us -> 38.6 us  [exchange(): pl.pallas_call(exchange_kernel, name='exchange', out_shape=[pltpu.VMEM((R...]
    ppermute x1, waiting for transfers between devices: 0.06 us -> 0.68 us  [local_step(): from_y = lax.ppermute(to_y, GROUP_AXES, [(g, g ^ 4) for g in range(8)])]
  transfers between devices with their start and end apart: 2 -> 2, of which waited for: 1 -> 1; matrix products, arithmetic and copies ran while one was open for 0% -> 0% of each run, Pallas kernels for 17% -> 18%
where the time goes in v8:
time: 52 us; the launch traced here: 51.9 us
  Pallas kernels  48.6 us (93%)
  starting transfers between devices  2.05 us (4%)
  waiting for transfers between devices  0.69 us (1%)
  between operations  0.66 us (1%)
    pallas_call x1, Pallas kernels, exchange(): pl.pallas_call(exchange_kernel, name='exchange', out_shape=[pltpu.VMEM((R...  38.6 us
    pallas_call x1, Pallas kernels, weight_grads(): pl.pallas_call(grads_kernel, name='weight_grads', out_shape=[sds((EXP, D,...  9.15 us
    ppermute x1, starting transfers between devices, local_step(): from_x = lax.ppermute(to_x, GROUP_AXES, [(g, g ^ 2) for g in range(8)])  1.15 us
  transfers between devices with their start and end apart: 2, of which 1 were waited for; matrix products, arithmetic and copies ran while one was open for 0% of the time, Pallas kernels for 18%

profile of v8, /device:TPU:0, one launch (start us, length us, event | category | flops | bytes accessed | tf_op | source)
XLA Modules:
  0.0 51.9 jit_solution(9301079343824654873)
XLA Ops:
  0.6 38.6 %exchange.1 = (bf16[64,1024]{1,0:T(8,128)(2,1)S(1)}, f32[8,64]{1,0:T(8,128)S(1)}, f32[64,1536]{1,0:T(8,128)S(1)}, f32[64,1536]{1,0:T(8,128)S(1)}, f32[64,1024]{1...) custom-call(bf16[64,1024]{1,0:T(8,128)(2,1)} %x_hbm.1, ...), custom_call_target="tpu_custom_call" | custom-call | tf_op jit(solution)/shard_map/exchange/pallas_call | solution.py:447
  39.3 1.1 %collective-permute-start = (f32[64,1536]{1,0:T(8,128)S(1)}, f32[64,1536]{1,0:T(8,128)S(1)}, u32[]{:S(2)}, u32[]{:S(2)}) collective-permute-start(f32[64,1536]{1,0:T(8,128)S(1)} %get-tuple-element.37), channel_id=1, source_target_pairs={{0,2},{1,3},{2,0},{3,1},{4,6},{5,7},{6,4},{7,5}} | collective-permute-start | bytes 1179656 | tf_op jit(solution)/shard_map/ppermute | solution.py:547
  40.4 0.9 %collective-permute-start.1 = (f32[64,1536]{1,0:T(8,128)S(1)}, f32[64,1536]{1,0:T(8,128)S(1)}, u32[]{:S(2)}, u32[]{:S(2)}) collective-permute-start(f32[64,1536]{1,0:T(8,128)S(1)} %get-tuple-element.38), channel_id=1, source_target_pairs={{0,4},{1,5},{2,6},{3,7},{4,0},{5,1},{6,2},{7,3}} | collective-permute-start | bytes 1179656 | tf_op jit(solution)/shard_map/ppermute | solution.py:548
  41.3 9.2 %weight_grads.1 = (f32[4,1024,512]{2,1,0:T(8,128)}, f32[4,1024,512]{2,1,0:T(8,128)}, f32[4,512,1024]{2,1,0:T(8,128)}, bf16[64,1024]{1,0:T(8,128)(2,1)}, f32[8,64]{1,0:T(8,128)}) custom-call(bf16[1024,512]{1,0:T(8,128)(2,1)S(1)} %get-tuple-element.26.xt_ref, bf16[512,1024]{1,0:T(8,128)(2,1)S(1)} %get-tuple-element.27.dy_ref, ...), custom_call_target="tpu_custom_call" | custom-call | flops 6442450944 | bytes 35651584 | tf_op jit(solution)/shard_map/weight_grads/pallas_call | solution.py:513
  50.5 0.0 collective-permute-done.x_ref
  50.5 0.7 %collective-permute-done.1.y_ref = f32[64,1536]{1,0:T(8,128)S(1)} collective-permute-done((f32[64,1536]{1,0:T(8,128)S(1)}, f32[64,1536]{1,0:T(8,128)S(1)}, u32[]{:S(2)}, u32[]{:S(2)}) %collective-permute-start.1) | collective-permute-done | bytes 393248 | tf_op jit(solution)/shard_map/ppermute | solution.py:548
  51.2 0.8 %combine.1 = (bf16[64,1024]{1,0:T(8,128)(2,1)}, bf16[64,1024]{1,0:T(8,128)(2,1)}) custom-call(f32[64,1024]{1,0:T(8,128)S(1)} %get-tuple-element.35.dx_ref, f32[64,1024]{1,0:T(8,128)S(1)} %get-tuple-element.36.at_ref, f32[64,1536]{1,0:T(8,128)S(1)} %collective-permute-done.x_ref, f32[64,1536]{1,0:T(8,128)S(1)} %collective-permute-done.1.y_ref), custom_call_target="tpu_custom_call" | custom-call | tf_op jit(solution)/shard_map/combine/pallas_call | solution.py:537
Async XLA Ops:
  39.3 11.2 %collective-permute-start = (f32[64,1536]{1,0:T(8,128)S(1)}, f32[64,1536]{1,0:T(8,128)S(1)}, u32[]{:S(2)}, u32[]{:S(2)}) collective-permute-start(f32[64,1536]{1,0:T(8,128)S(1)} %get-tuple-element.37), channel_id=1, source_target_pairs={{0,2},{1,3},{2,0},{3,1},{4,6},{5,7},{6,4},{7,5}} | collective-permute-start | bytes 1179656 | tf_op jit(solution)/shard_map/ppermute | solution.py:547
  40.4 10.8 %collective-permute-start.1 = (f32[64,1536]{1,0:T(8,128)S(1)}, f32[64,1536]{1,0:T(8,128)S(1)}, u32[]{:S(2)}, u32[]{:S(2)}) collective-permute-start(f32[64,1536]{1,0:T(8,128)S(1)} %get-tuple-element.38), channel_id=1, source_target_pairs={{0,4},{1,5},{2,6},{3,7},{4,0},{5,1},{6,2},{7,3}} | collective-permute-start | bytes 1179656 | tf_op jit(solution)/shard_map/ppermute | solution.py:548

commit v9 on v8

--- a/solution.py
+++ b/solution.py
@@ -31,7 +31,7 @@
                     idx_ref, gate_ref, rows, wg, wu, wd, wqkv, wo, wo_in, ctx, ctx_in, osv, act, gfac, gsend, grecv,
                     dgs, dsend, drecv,
                     part, pair, s1, r1, s2, r2,
-                    in_sem, w_sem, gs_sem, gr_sem, rs_s, rs_r, ag_s, ag_r, dd_s, dd_r, hd_s, hd_r):
+                    in_sem, w_sem, gs_sem, gr_sem, rs_s, rs_r, ag_s, ag_r, dd_r, hd_s, hd_r):
     y = lax.axis_index('ei')
     o = lax.axis_index('eo')
     z = lax.axis_index('dp')
@@ -78,20 +78,6 @@
     for cp in wload:
         cp.start()
 
-    for cp in tables:
-        cp.wait()
-    exp_row = lax.broadcasted_iota(jnp.int32, (32, ROWS), 0)
-    table = jnp.zeros((32, ROWS), F32)
-    marks = jnp.zeros((32, ROWS), F32)
-    for j in range(TOPK):
-        hit = exp_row == idx_ref[j:j + 1, :]
-        table = table + jnp.where(hit, gate_ref[j:j + 1, :], 0.0)
-        marks = marks + jnp.where(hit, 1.0, 0.0)
-    wide = jnp.concatenate([table, marks], axis=1)
-    for d in range(8):
-        gsend[d] = wide[d * EXP:(d + 1) * EXP, :]
-    grecv[me] = gsend[me]
-
     def blk(t, q, off=0, n=ROWS):
         return rows.at[t, pl.ds(pl.multiple_of(q * 128 + c * ROWS + off, 32), n)]
 
@@ -107,7 +93,7 @@
 
     def gather_copies(t):
         def cp(k, ref, where):
-            return remote(ref, ref, ag_s.at[t], ag_r.at[gather_slot(t, k)], where)
+            return remote(ref, ref, ag_s.at[0], ag_r.at[gather_slot(t, k)], where)
         return [cp(0, blk(t, q0), sib),
                 cp(1, blk(t, q0, 0, hr), xn), cp(2, blk(t, q0, hr, hr), xn),
                 cp(3, blk(t, q0, hr, hr), yn), cp(4, blk(t, q0, 0, hr), yn),
@@ -146,7 +132,7 @@
 
     def ag_rows(t, k, n):
         ref = rows.at[t, 0:n]
-        return remote(ref, ref, ag_s.at[t], ag_r.at[gather_slot(t, k)], sib)
+        return remote(ref, ref, ag_s.at[0], ag_r.at[gather_slot(t, k)], sib)
 
     def tile_copies(send, recv, ss, rs, chip_tiles):
         cps = {}
@@ -158,7 +144,7 @@
         return cps
 
     gate_cps = tile_copies(gsend, grecv, gs_sem, gr_sem, False)
-    dg_cps = tile_copies(dsend, drecv, dd_s, dd_r, True)
+    dg_cps = tile_copies(dsend, drecv, gs_sem, dd_r, True)
     chips = (q0, qx, qy, qd)
     OWN, X, Y, DI = 0, 1, 2, 3
     first = (X, Y)
@@ -172,15 +158,15 @@
             group = 0 if k // 2 == DI else 1
             if n == 1 and k // 2 in (X, Y):
                 group = 3 if k == 2 * X else 4 if k == 2 * Y + 1 else 5
-        return (0, 3, 9)[n] + group
+        return (-1, 1, 7)[n] + group
 
     def rs_wait(n, k, count):
         ref = pair.at[n, 0, 0:2] if count == 2 else pair.at[n, :, 0:3] if count == 6 else pair.at[n, 0, 0]
-        remote(ref, ref, rs_s.at[n, 0], rs_r.at[rs_slot(n, k)], sib).wait_recv()
+        remote(ref, ref, rs_s.at[0], rs_r.at[rs_slot(n, k)], sib).wait_recv()
 
     def rs_copies(n):
         def cp(k, src, dst, where):
-            return remote(src, dst, rs_s.at[n, 0 if k < 8 else 1], rs_r.at[rs_slot(n, k)], where)
+            return remote(src, dst, rs_s.at[0], rs_r.at[rs_slot(n, k)], where)
         cps = [cp(2 * k + h, part.at[n, 1 - c, h, chips[k]], pair.at[n, h, chips[k]], sib) for k in range(4) for h in range(2)]
         for h in range(2):
             one, two = (xn, yn) if h == 0 else (yn, xn)
@@ -224,7 +210,7 @@
             out_ref[:, h * HALF:(h + 1) * HALF] = total.astype(BF)
 
     def head_copy(src, dst, slot, where):
-        return remote(src, dst, hd_s.at[slot // 2], hd_r.at[slot], where)
+        return remote(src, dst, hd_s.at[0], hd_r.at[slot], where)
 
     wo_cps = [head_copy(wo.at[h, r:r + 64], wo_in.at[h, r:r + 64], h, (xn, yn)[h]) for r in (0, 64) for h in range(2)]
     ctx_cps = [head_copy(ctx.at[q], ctx_in.at[h, i], 2 + h, (xn, yn)[h])
@@ -348,7 +334,7 @@
 
     def leave_attention():
         ref = pair.at[0, 0]
-        remote(ref, ref, rs_s.at[0, 0], rs_r.at[rs_slot(0, 2 * OWN)], sib).wait_recv()
+        remote(ref, ref, rs_s.at[0], rs_r.at[rs_slot(0, 2 * OWN)], sib).wait_recv()
         for h, dst in ((0, toy), (1, tox)):
             dst[:, D:D + HALF] = chip_sum(0, h, second[h])
             own_at[:, h * HALF:(h + 1) * HALF] = chip_sum(0, h, OWN)
@@ -368,6 +354,20 @@
     pltpu.make_async_copy(x_hbm, rows.at[XT, own], in_sem.at[0]).wait()
     pl.semaphore_wait(barrier, len(rels))
     ag_own(XT)
+    for cp in tables:
+        cp.wait()
+
+    exp_row = lax.broadcasted_iota(jnp.int32, (32, ROWS), 0)
+    table = jnp.zeros((32, ROWS), F32)
+    marks = jnp.zeros((32, ROWS), F32)
+    for j in range(TOPK):
+        hit = exp_row == idx_ref[j:j + 1, :]
+        table = table + jnp.where(hit, gate_ref[j:j + 1, :], 0.0)
+        marks = marks + jnp.where(hit, 1.0, 0.0)
+    wide = jnp.concatenate([table, marks], axis=1)
+    for d in range(8):
+        gsend[d] = wide[d * EXP:(d + 1) * EXP, :]
+    grecv[me] = gsend[me]
     for cp in gate_cps.values():
         cp.start()
     pltpu.make_async_copy(wg_hbm.at[0, 0:4 * ROWS], wg.at[0, 0:4 * ROWS], in_sem.at[3]).wait()
@@ -416,7 +416,7 @@
     rs_pair(2, OWN)
     attention_out()
     rs_wait_dg = drecv.at[0:7]
-    remote(rs_wait_dg, rs_wait_dg, dd_s.at[0], dd_r.at[0], sib).wait_recv()
+    remote(rs_wait_dg, rs_wait_dg, gs_sem.at[0], dd_r.at[0], sib).wait_recv()
     both = jnp.concatenate([drecv[d] for d in range(8)], axis=0)
     mine = jnp.where(c == 0, both[:, 0:ROWS], both[:, ROWS:128])
     for j in range(TOPK):
@@ -427,17 +427,8 @@
     xt[...] = rows[XT].T
     leave_dx()
 
-    for t in range(3):
-        ref = rows.at[t, 0:7 * ROWS]
-        remote(ref, ref, ag_s.at[t], ag_r.at[0], sib).wait_send()
-    tiles = gsend.at[0:7]
-    remote(tiles, tiles, gs_sem.at[0], gr_sem.at[0], sib).wait_send()
-    remote(tiles, tiles, dd_s.at[0], dd_r.at[0], sib).wait_send()
-    for ref, n, k in ((pair.at[0, 0], 0, 0), (part.at[1, 0], 1, 0), (part.at[2, 0], 2, 0),
-                      (pair.at[1, :, 0:3], 1, 1), (pair.at[2, 0, 0:2], 2, 1)):
-        remote(ref, ref, rs_s.at[n, k], rs_r.at[0], sib).wait_send()
-    remote(wo, wo, hd_s.at[0], hd_r.at[0], sib).wait_send()
-    remote(ctx, ctx, hd_s.at[1], hd_r.at[0], sib).wait_send()
+    for ref, sem in ((rows.at[:, 0:7 * ROWS], ag_s), (act.at[:, 0:7 * ROWS], rs_s), (gt.at[0:56], gs_sem), (rows.at[:, 0:ROWS], hd_s)):
+        remote(ref, ref, sem.at[0], gr_sem.at[0], sib).wait_send()
 
 
 def exchange(x, dy, xa, idx, gates, wg, wu, wd, wq, wk, wv, wo):
@@ -465,7 +456,7 @@
             pltpu.VMEM((3, 2, 2, ROWS, HALF), F32), pltpu.VMEM((3, 2, 2, ROWS, HALF), F32),
             pltpu.VMEM((3, 2, ROWS, HALF), F32), pltpu.VMEM((3, 2, ROWS, HALF), F32),
             dma((4,)), dma((1 + EXP,)), dma((1,)), dma((4,)),
-            dma((3, 2)), dma((12,)), dma((3,)), dma((15,)), dma((1,)), dma((1,)), dma((2,)), dma((4,)),
+            dma((1,)), dma((10,)), dma((1,)), dma((15,)), dma((1,)), dma((1,)), dma((4,)),
         ],
         compiler_params=pltpu.CompilerParams(collective_id=0, has_side_effects=True, vmem_limit_bytes=50 * 1024 * 1024),
     )(x, dy, xa, idx, gates, wg, wu, wd, wq, wk, wv, wo)

time: 52 us -> 51.9 us (level)
  no operation moved by 1% of the time
where the time goes in v9:
time: 51.9 us; the launch traced here: 51.8 us
  Pallas kernels  48.5 us (93%)
  starting transfers between devices  2.05 us (4%)
  between operations  0.66 us (1%)
  waiting for transfers between devices  0.65 us (1%)
    pallas_call x1, Pallas kernels, exchange(): pl.pallas_call(exchange_kernel, name='exchange', out_shape=[pltpu.VMEM((R...  38.6 us
    pallas_call x1, Pallas kernels, weight_grads(): pl.pallas_call(grads_kernel, name='weight_grads', out_shape=[sds((EXP, D,...  9.15 us
    ppermute x1, starting transfers between devices, local_step(): from_x = lax.ppermute(to_x, GROUP_AXES, [(g, g ^ 2) for g in range(8)])  1.13 us
  transfers between devices with their start and end apart: 2, of which 1 were waited for; matrix products, arithmetic and copies ran while one was open for 0% of the time, Pallas kernels for 18%

profile of v9, /device:TPU:0, one launch (start us, length us, event | category | flops | bytes accessed | tf_op | source)
XLA Modules:
  0.0 51.8 jit_solution(12822955401184116141)
XLA Ops:
  0.6 38.6 %exchange.1 = (bf16[64,1024]{1,0:T(8,128)(2,1)S(1)}, f32[8,64]{1,0:T(8,128)S(1)}, f32[64,1536]{1,0:T(8,128)S(1)}, f32[64,1536]{1,0:T(8,128)S(1)}, f32[64,1024]{1...) custom-call(bf16[64,1024]{1,0:T(8,128)(2,1)} %x_hbm.1, ...), custom_call_target="tpu_custom_call" | custom-call | tf_op jit(solution)/shard_map/exchange/pallas_call | solution.py:438
  39.2 1.1 %collective-permute-start = (f32[64,1536]{1,0:T(8,128)S(1)}, f32[64,1536]{1,0:T(8,128)S(1)}, u32[]{:S(2)}, u32[]{:S(2)}) collective-permute-start(f32[64,1536]{1,0:T(8,128)S(1)} %get-tuple-element.37), channel_id=1, source_target_pairs={{0,2},{1,3},{2,0},{3,1},{4,6},{5,7},{6,4},{7,5}} | collective-permute-start | bytes 1179656 | tf_op jit(solution)/shard_map/ppermute | solution.py:538
  40.3 0.9 %collective-permute-start.1 = (f32[64,1536]{1,0:T(8,128)S(1)}, f32[64,1536]{1,0:T(8,128)S(1)}, u32[]{:S(2)}, u32[]{:S(2)}) collective-permute-start(f32[64,1536]{1,0:T(8,128)S(1)} %get-tuple-element.38), channel_id=1, source_target_pairs={{0,4},{1,5},{2,6},{3,7},{4,0},{5,1},{6,2},{7,3}} | collective-permute-start | bytes 1179656 | tf_op jit(solution)/shard_map/ppermute | solution.py:539
  41.2 9.2 %weight_grads.1 = (f32[4,1024,512]{2,1,0:T(8,128)}, f32[4,1024,512]{2,1,0:T(8,128)}, f32[4,512,1024]{2,1,0:T(8,128)}, bf16[64,1024]{1,0:T(8,128)(2,1)}, f32[8,64]{1,0:T(8,128)}) custom-call(bf16[1024,512]{1,0:T(8,128)(2,1)S(1)} %get-tuple-element.26.xt_ref, bf16[512,1024]{1,0:T(8,128)(2,1)S(1)} %get-tuple-element.27.dy_ref, ...), custom_call_target="tpu_custom_call" | custom-call | flops 6442450944 | bytes 35651584 | tf_op jit(solution)/shard_map/weight_grads/pallas_call | solution.py:504
  50.4 0.0 collective-permute-done.x_ref
  50.4 0.6 %collective-permute-done.1.y_ref = f32[64,1536]{1,0:T(8,128)S(1)} collective-permute-done((f32[64,1536]{1,0:T(8,128)S(1)}, f32[64,1536]{1,0:T(8,128)S(1)}, u32[]{:S(2)}, u32[]{:S(2)}) %collective-permute-start.1) | collective-permute-done | bytes 393248 | tf_op jit(solution)/shard_map/ppermute | solution.py:539
  51.1 0.8 %combine.1 = (bf16[64,1024]{1,0:T(8,128)(2,1)}, bf16[64,1024]{1,0:T(8,128)(2,1)}) custom-call(f32[64,1024]{1,0:T(8,128)S(1)} %get-tuple-element.35.dx_ref, f32[64,1024]{1,0:T(8,128)S(1)} %get-tuple-element.36.at_ref, f32[64,1536]{1,0:T(8,128)S(1)} %collective-permute-done.x_ref, f32[64,1536]{1,0:T(8,128)S(1)} %collective-permute-done.1.y_ref), custom_call_target="tpu_custom_call" | custom-call | tf_op jit(solution)/shard_map/combine/pallas_call | solution.py:528
Async XLA Ops:
  39.2 11.2 %collective-permute-start = (f32[64,1536]{1,0:T(8,128)S(1)}, f32[64,1536]{1,0:T(8,128)S(1)}, u32[]{:S(2)}, u32[]{:S(2)}) collective-permute-start(f32[64,1536]{1,0:T(8,128)S(1)} %get-tuple-element.37), channel_id=1, source_target_pairs={{0,2},{1,3},{2,0},{3,1},{4,6},{5,7},{6,4},{7,5}} | collective-permute-start | bytes 1179656 | tf_op jit(solution)/shard_map/ppermute | solution.py:538
  40.3 10.7 %collective-permute-start.1 = (f32[64,1536]{1,0:T(8,128)S(1)}, f32[64,1536]{1,0:T(8,128)S(1)}, u32[]{:S(2)}, u32[]{:S(2)}) collective-permute-start(f32[64,1536]{1,0:T(8,128)S(1)} %get-tuple-element.38), channel_id=1, source_target_pairs={{0,4},{1,5},{2,6},{3,7},{4,0},{5,1},{6,2},{7,3}} | collective-permute-start | bytes 1179656 | tf_op jit(solution)/shard_map/ppermute | solution.py:539

commit v10 on v9

--- a/solution.py
+++ b/solution.py
@@ -52,31 +52,27 @@
     sib, xn, yn = dev(0, 0, 1), dev(1, 0, 0), dev(0, 1, 0)
     rels = [(fx, fy, fc) for fx in (0, 1) for fy in (0, 1) for fc in (0, 1) if fx or fy or fc]
 
+    own = pl.ds(pl.multiple_of(me * ROWS, ROWS), ROWS)
+    pltpu.make_async_copy(x_hbm, rows.at[XT, own], in_sem.at[0]).start()
     barrier = pltpu.get_barrier_semaphore()
     for rel in rels:
         pl.semaphore_signal(barrier, inc=1, device_id=dev(*rel), device_id_type=MESH)
 
-    own = pl.ds(pl.multiple_of(me * ROWS, ROWS), ROWS)
     tables = [pltpu.make_async_copy(idx_hbm, idx_ref, in_sem.at[1]), pltpu.make_async_copy(gate_hbm, gate_ref, in_sem.at[2])]
     for cp in tables:
         cp.start()
-    for t, src in ((XT, x_hbm), (DY, dy_hbm), (XA, xa_hbm)):
-        pltpu.make_async_copy(src, rows.at[t, own], in_sem.at[0 if t == XT else 3]).start()
+    for t, src in ((DY, dy_hbm), (XA, xa_hbm)):
+        pltpu.make_async_copy(src, rows.at[t, own], in_sem.at[3]).start()
 
     def expert_load(e):
         return [pltpu.make_async_copy(src.at[e], dst.at[e], w_sem.at[1 + e])
                 for src, dst in ((wg_hbm, wg), (wu_hbm, wu), (wd_hbm, wd))]
 
-    for e in range(EXP):
-        for cp in expert_load(e):
-            cp.start()
     wload = [pltpu.make_async_copy(wq_hbm, wqkv.at[0:128], w_sem.at[0]),
              pltpu.make_async_copy(wk_hbm, wqkv.at[128:192], w_sem.at[0]),
              pltpu.make_async_copy(wv_hbm, wqkv.at[192:256], w_sem.at[0]),
              pltpu.make_async_copy(wo_hbm.at[:, 0:HALF], wo.at[0], w_sem.at[0]),
              pltpu.make_async_copy(wo_hbm.at[:, HALF:D], wo.at[1], w_sem.at[0])]
-    for cp in wload:
-        cp.start()
 
     def blk(t, q, off=0, n=ROWS):
         return rows.at[t, pl.ds(pl.multiple_of(q * 128 + c * ROWS + off, 32), n)]
@@ -352,6 +348,11 @@
             own_dx[:, cols] = chip_sum(n, h, OWN)
 
     pltpu.make_async_copy(x_hbm, rows.at[XT, own], in_sem.at[0]).wait()
+    for e in range(EXP):
+        for cp in expert_load(e):
+            cp.start()
+    for cp in wload:
+        cp.start()
     pl.semaphore_wait(barrier, len(rels))
     ag_own(XT)
     for cp in tables:

time: 51.9 us -> 49 us (0.944)
  Pallas kernels: 48.5 us -> 45.4 us
    pallas_call x1, Pallas kernels: 38.6 us -> 35.5 us  [exchange(): pl.pallas_call(exchange_kernel, name='exchange', out_shape=[pltpu.VMEM((R...]
  transfers between devices with their start and end apart: 2 -> 2, of which waited for: 1 -> 1; matrix products, arithmetic and copies ran while one was open for 0% -> 0% of each run, Pallas kernels for 18% -> 19%
where the time goes in v10:
time: 49 us; the launch traced here: 48.9 us
  Pallas kernels  45.4 us (93%)
  starting transfers between devices  2.05 us (4%)
  waiting for transfers between devices  0.79 us (2%)
  between operations  0.66 us (1%)
    pallas_call x1, Pallas kernels, exchange(): pl.pallas_call(exchange_kernel, name='exchange', out_shape=[pltpu.VMEM((R...  35.5 us
    pallas_call x1, Pallas kernels, weight_grads(): pl.pallas_call(grads_kernel, name='weight_grads', out_shape=[sds((EXP, D,...  9.15 us
    ppermute x1, starting transfers between devices, local_step(): from_x = lax.ppermute(to_x, GROUP_AXES, [(g, g ^ 2) for g in range(8)])  1.16 us
  transfers between devices with their start and end apart: 2, of which 1 were waited for; matrix products, arithmetic and copies ran while one was open for 0% of the time, Pallas kernels for 19%

profile of v10, /device:TPU:0, one launch (start us, length us, event | category | flops | bytes accessed | tf_op | source)
XLA Modules:
  0.0 48.9 jit_solution(9444095480302971521)
XLA Ops:
  0.6 35.5 %exchange.1 = (bf16[64,1024]{1,0:T(8,128)(2,1)S(1)}, f32[8,64]{1,0:T(8,128)S(1)}, f32[64,1536]{1,0:T(8,128)S(1)}, f32[64,1536]{1,0:T(8,128)S(1)}, f32[64,1024]{1...) custom-call(bf16[64,1024]{1,0:T(8,128)(2,1)} %x_hbm.1, ...), custom_call_target="tpu_custom_call" | custom-call | tf_op jit(solution)/shard_map/exchange/pallas_call | solution.py:439
  36.1 1.2 %collective-permute-start = (f32[64,1536]{1,0:T(8,128)S(1)}, f32[64,1536]{1,0:T(8,128)S(1)}, u32[]{:S(2)}, u32[]{:S(2)}) collective-permute-start(f32[64,1536]{1,0:T(8,128)S(1)} %get-tuple-element.37), channel_id=1, source_target_pairs={{0,2},{1,3},{2,0},{3,1},{4,6},{5,7},{6,4},{7,5}} | collective-permute-start | bytes 1179656 | tf_op jit(solution)/shard_map/ppermute | solution.py:539
  37.3 0.9 %collective-permute-start.1 = (f32[64,1536]{1,0:T(8,128)S(1)}, f32[64,1536]{1,0:T(8,128)S(1)}, u32[]{:S(2)}, u32[]{:S(2)}) collective-permute-start(f32[64,1536]{1,0:T(8,128)S(1)} %get-tuple-element.38), channel_id=1, source_target_pairs={{0,4},{1,5},{2,6},{3,7},{4,0},{5,1},{6,2},{7,3}} | collective-permute-start | bytes 1179656 | tf_op jit(solution)/shard_map/ppermute | solution.py:540
  38.2 9.2 %weight_grads.1 = (f32[4,1024,512]{2,1,0:T(8,128)}, f32[4,1024,512]{2,1,0:T(8,128)}, f32[4,512,1024]{2,1,0:T(8,128)}, bf16[64,1024]{1,0:T(8,128)(2,1)}, f32[8,64]{1,0:T(8,128)}) custom-call(bf16[1024,512]{1,0:T(8,128)(2,1)S(1)} %get-tuple-element.26.xt_ref, bf16[512,1024]{1,0:T(8,128)(2,1)S(1)} %get-tuple-element.27.dy_ref, ...), custom_call_target="tpu_custom_call" | custom-call | flops 6442450944 | bytes 35651584 | tf_op jit(solution)/shard_map/weight_grads/pallas_call | solution.py:505
  47.3 0.0 collective-permute-done.x_ref
  47.3 0.8 %collective-permute-done.1.y_ref = f32[64,1536]{1,0:T(8,128)S(1)} collective-permute-done((f32[64,1536]{1,0:T(8,128)S(1)}, f32[64,1536]{1,0:T(8,128)S(1)}, u32[]{:S(2)}, u32[]{:S(2)}) %collective-permute-start.1) | collective-permute-done | bytes 393248 | tf_op jit(solution)/shard_map/ppermute | solution.py:540
  48.1 0.8 %combine.1 = (bf16[64,1024]{1,0:T(8,128)(2,1)}, bf16[64,1024]{1,0:T(8,128)(2,1)}) custom-call(f32[64,1024]{1,0:T(8,128)S(1)} %get-tuple-element.35.dx_ref, f32[64,1024]{1,0:T(8,128)S(1)} %get-tuple-element.36.at_ref, f32[64,1536]{1,0:T(8,128)S(1)} %collective-permute-done.x_ref, f32[64,1536]{1,0:T(8,128)S(1)} %collective-permute-done.1.y_ref), custom_call_target="tpu_custom_call" | custom-call | tf_op jit(solution)/shard_map/combine/pallas_call | solution.py:529
Async XLA Ops:
  36.1 11.2 %collective-permute-start = (f32[64,1536]{1,0:T(8,128)S(1)}, f32[64,1536]{1,0:T(8,128)S(1)}, u32[]{:S(2)}, u32[]{:S(2)}) collective-permute-start(f32[64,1536]{1,0:T(8,128)S(1)} %get-tuple-element.37), channel_id=1, source_target_pairs={{0,2},{1,3},{2,0},{3,1},{4,6},{5,7},{6,4},{7,5}} | collective-permute-start | bytes 1179656 | tf_op jit(solution)/shard_map/ppermute | solution.py:539
  37.3 10.8 %collective-permute-start.1 = (f32[64,1536]{1,0:T(8,128)S(1)}, f32[64,1536]{1,0:T(8,128)S(1)}, u32[]{:S(2)}, u32[]{:S(2)}) collective-permute-start(f32[64,1536]{1,0:T(8,128)S(1)} %get-tuple-element.38), channel_id=1, source_target_pairs={{0,4},{1,5},{2,6},{3,7},{4,0},{5,1},{6,2},{7,3}} | collective-permute-start | bytes 1179656 | tf_op jit(solution)/shard_map/ppermute | solution.py:540

commit v11 on v10

--- a/solution.py
+++ b/solution.py
@@ -516,18 +516,25 @@
     )(*args)
 
 
-def combine_kernel(dx_ref, at_ref, x_ref, y_ref, dx_out, at_out):
-    dx_out[...] = (dx_ref[...] + x_ref[:, 0:D] + y_ref[:, 0:D]).astype(BF)
-    at_out[:, 0:HALF] = (at_ref[:, 0:HALF] + y_ref[:, D:D + HALF]).astype(BF)
-    at_out[:, HALF:D] = (at_ref[:, HALF:D] + x_ref[:, D:D + HALF]).astype(BF)
+def combine_kernel(dx_ref, at_ref, x_ref, y_ref, dx_out, at_out, dx_buf, at_buf, sem):
+    dx_cp = pltpu.make_async_copy(dx_buf, dx_out, sem.at[0])
+    at_cp = pltpu.make_async_copy(at_buf, at_out, sem.at[1])
+    dx_buf[...] = (dx_ref[...] + x_ref[:, 0:D] + y_ref[:, 0:D]).astype(BF)
+    dx_cp.start()
+    at_buf[:, 0:HALF] = (at_ref[:, 0:HALF] + y_ref[:, D:D + HALF]).astype(BF)
+    at_buf[:, HALF:D] = (at_ref[:, HALF:D] + x_ref[:, D:D + HALF]).astype(BF)
+    at_cp.start()
+    dx_cp.wait()
+    at_cp.wait()
 
 
 def combine(*args):
     sds = jax.ShapeDtypeStruct
     args = [pltpu.with_memory_space_constraint(v, pltpu.VMEM) for v in args]
-    vmem = pl.BlockSpec(memory_space=pltpu.VMEM)
     return pl.pallas_call(combine_kernel, name='combine', out_shape=[sds((ROWS, D), BF)] * 2,
-                          in_specs=[vmem] * 4, out_specs=[vmem] * 2)(*args)
+                          in_specs=[pl.BlockSpec(memory_space=pltpu.VMEM)] * 4,
+                          out_specs=[pl.BlockSpec(memory_space=pl.ANY)] * 2,
+                          scratch_shapes=[pltpu.VMEM((ROWS, D), BF), pltpu.VMEM((ROWS, D), BF), pltpu.SemaphoreType.DMA((2,))])(*args)
 
 
 def solution(mesh):

time: 49 us -> 49 us (level)
  no operation moved by 1% of the time
where the time goes in v11:
time: 49 us; the launch traced here: 48.9 us
  Pallas kernels  45.4 us (93%)
  starting transfers between devices  2.05 us (4%)
  waiting for transfers between devices  0.79 us (2%)
  between operations  0.66 us (1%)
    pallas_call x1, Pallas kernels, exchange(): pl.pallas_call(exchange_kernel, name='exchange', out_shape=[pltpu.VMEM((R...  35.5 us
    pallas_call x1, Pallas kernels, weight_grads(): pl.pallas_call(grads_kernel, name='weight_grads', out_shape=[sds((EXP, D,...  9.15 us
    ppermute x1, starting transfers between devices, local_step(): from_x = lax.ppermute(to_x, GROUP_AXES, [(g, g ^ 2) for g in range(8)])  1.16 us
  transfers between devices with their start and end apart: 2, of which 1 were waited for; matrix products, arithmetic and copies ran while one was open for 0% of the time, Pallas kernels for 19%

profile of v11, /device:TPU:0, one launch (start us, length us, event | category | flops | bytes accessed | tf_op | source)
XLA Modules:
  0.0 48.9 jit_solution(3211744539898386029)
XLA Ops:
  0.6 35.5 %exchange.1 = (bf16[64,1024]{1,0:T(8,128)(2,1)S(1)}, f32[8,64]{1,0:T(8,128)S(1)}, f32[64,1536]{1,0:T(8,128)S(1)}, f32[64,1536]{1,0:T(8,128)S(1)}, f32[64,1024]{1...) custom-call(bf16[64,1024]{1,0:T(8,128)(2,1)} %x_hbm.1, ...), custom_call_target="tpu_custom_call" | custom-call | tf_op jit(solution)/shard_map/exchange/pallas_call | solution.py:439
  36.1 1.2 %collective-permute-start = (f32[64,1536]{1,0:T(8,128)S(1)}, f32[64,1536]{1,0:T(8,128)S(1)}, u32[]{:S(2)}, u32[]{:S(2)}) collective-permute-start(f32[64,1536]{1,0:T(8,128)S(1)} %get-tuple-element.37), channel_id=1, source_target_pairs={{0,2},{1,3},{2,0},{3,1},{4,6},{5,7},{6,4},{7,5}} | collective-permute-start | bytes 1179656 | tf_op jit(solution)/shard_map/ppermute | solution.py:546
  37.3 0.9 %collective-permute-start.1 = (f32[64,1536]{1,0:T(8,128)S(1)}, f32[64,1536]{1,0:T(8,128)S(1)}, u32[]{:S(2)}, u32[]{:S(2)}) collective-permute-start(f32[64,1536]{1,0:T(8,128)S(1)} %get-tuple-element.38), channel_id=1, source_target_pairs={{0,4},{1,5},{2,6},{3,7},{4,0},{5,1},{6,2},{7,3}} | collective-permute-start | bytes 1179656 | tf_op jit(solution)/shard_map/ppermute | solution.py:547
  38.2 9.2 %weight_grads.1 = (f32[4,1024,512]{2,1,0:T(8,128)}, f32[4,1024,512]{2,1,0:T(8,128)}, f32[4,512,1024]{2,1,0:T(8,128)}, bf16[64,1024]{1,0:T(8,128)(2,1)}, f32[8,64]{1,0:T(8,128)}) custom-call(bf16[1024,512]{1,0:T(8,128)(2,1)S(1)} %get-tuple-element.26.xt_ref, bf16[512,1024]{1,0:T(8,128)(2,1)S(1)} %get-tuple-element.27.dy_ref, ...), custom_call_target="tpu_custom_call" | custom-call | flops 6442450944 | bytes 35651584 | tf_op jit(solution)/shard_map/weight_grads/pallas_call | solution.py:505
  47.3 0.0 collective-permute-done.x_ref
  47.3 0.8 %collective-permute-done.1.y_ref = f32[64,1536]{1,0:T(8,128)S(1)} collective-permute-done((f32[64,1536]{1,0:T(8,128)S(1)}, f32[64,1536]{1,0:T(8,128)S(1)}, u32[]{:S(2)}, u32[]{:S(2)}) %collective-permute-start.1) | collective-permute-done | bytes 393248 | tf_op jit(solution)/shard_map/ppermute | solution.py:547
  48.1 0.8 %combine.1 = (bf16[64,1024]{1,0:T(8,128)(2,1)}, bf16[64,1024]{1,0:T(8,128)(2,1)}) custom-call(f32[64,1024]{1,0:T(8,128)S(1)} %get-tuple-element.35.dx_ref, f32[64,1024]{1,0:T(8,128)S(1)} %get-tuple-element.36.at_ref, f32[64,1536]{1,0:T(8,128)S(1)} %collective-permute-done.x_ref, f32[64,1536]{1,0:T(8,128)S(1)} %collective-permute-done.1.y_ref), custom_call_target="tpu_custom_call" | custom-call | tf_op jit(solution)/shard_map/combine/pallas_call | solution.py:534
Async XLA Ops:
  36.1 11.2 %collective-permute-start = (f32[64,1536]{1,0:T(8,128)S(1)}, f32[64,1536]{1,0:T(8,128)S(1)}, u32[]{:S(2)}, u32[]{:S(2)}) collective-permute-start(f32[64,1536]{1,0:T(8,128)S(1)} %get-tuple-element.37), channel_id=1, source_target_pairs={{0,2},{1,3},{2,0},{3,1},{4,6},{5,7},{6,4},{7,5}} | collective-permute-start | bytes 1179656 | tf_op jit(solution)/shard_map/ppermute | solution.py:546
  37.3 10.8 %collective-permute-start.1 = (f32[64,1536]{1,0:T(8,128)S(1)}, f32[64,1536]{1,0:T(8,128)S(1)}, u32[]{:S(2)}, u32[]{:S(2)}) collective-permute-start(f32[64,1536]{1,0:T(8,128)S(1)} %get-tuple-element.38), channel_id=1, source_target_pairs={{0,4},{1,5},{2,6},{3,7},{4,0},{5,1},{6,2},{7,3}} | collective-permute-start | bytes 1179656 | tf_op jit(solution)/shard_map/ppermute | solution.py:547

commit v12 on v11

--- a/solution.py
+++ b/solution.py
@@ -386,11 +386,10 @@
     ag_own_a(DY)
     ag[XT][7].wait_recv()
     ag[XT][8].wait_recv()
-    experts(forward([X, Y]), {0: lambda: (ag_forward(XA), ag_own_b(DY)), 1: lambda: ag_pair(XA), 2: lambda: ag_last(XT)})
+    experts(forward([X, Y]), {0: lambda: (ag_forward(XA), ag_own_b(DY)), 1: lambda: ag_pair(XA), 2: lambda: (ag_last(XT), ag_forward(DY))})
     rs_pair(1, X)
     rs_pair(1, Y)
     gate_table(DI)
-    ag_forward(DY)
     pltpu.make_async_copy(wg_hbm.at[0, 0:768], wg.at[0, 0:768], w_sem.at[0]).wait()
     for cp in wo_cps[:2]:
         cp.start()

time: 49 us -> 48.4 us (0.988)
  no operation moved by 1% of the time
where the time goes in v12:
time: 48.4 us; the launch traced here: 48.3 us
  Pallas kernels  45.2 us (93%)
  starting transfers between devices  2.05 us (4%)
  between operations  0.66 us (1%)
    pallas_call x1, Pallas kernels, exchange(): pl.pallas_call(exchange_kernel, name='exchange', out_shape=[pltpu.VMEM((R...  35.3 us
    pallas_call x1, Pallas kernels, weight_grads(): pl.pallas_call(grads_kernel, name='weight_grads', out_shape=[sds((EXP, D,...  9.15 us
    ppermute x1, starting transfers between devices, local_step(): from_x = lax.ppermute(to_x, GROUP_AXES, [(g, g ^ 2) for g in range(8)])  1.03 us
    ppermute x1, starting transfers between devices, local_step(): from_y = lax.ppermute(to_y, GROUP_AXES, [(g, g ^ 4) for g in range(8)])  1.01 us
  transfers between devices with their start and end apart: 2, of which 1 were waited for; matrix products, arithmetic and copies ran while one was open for 0% of the time, Pallas kernels for 19%

profile of v12, /device:TPU:0, one launch (start us, length us, event | category | flops | bytes accessed | tf_op | source)
XLA Modules:
  0.0 48.3 jit_solution(2274239661862470121)
XLA Ops:
  0.6 35.3 %exchange.1 = (bf16[64,1024]{1,0:T(8,128)(2,1)S(1)}, f32[8,64]{1,0:T(8,128)S(1)}, f32[64,1536]{1,0:T(8,128)S(1)}, f32[64,1536]{1,0:T(8,128)S(1)}, f32[64,1024]{1...) custom-call(bf16[64,1024]{1,0:T(8,128)(2,1)} %x_hbm.1, ...), custom_call_target="tpu_custom_call" | custom-call | tf_op jit(solution)/shard_map/exchange/pallas_call | solution.py:438
  35.9 1.0 %collective-permute-start = (f32[64,1536]{1,0:T(8,128)S(1)}, f32[64,1536]{1,0:T(8,128)S(1)}, u32[]{:S(2)}, u32[]{:S(2)}) collective-permute-start(f32[64,1536]{1,0:T(8,128)S(1)} %get-tuple-element.37), channel_id=1, source_target_pairs={{0,2},{1,3},{2,0},{3,1},{4,6},{5,7},{6,4},{7,5}} | collective-permute-start | bytes 1179656 | tf_op jit(solution)/shard_map/ppermute | solution.py:545
  37.0 1.0 %collective-permute-start.1 = (f32[64,1536]{1,0:T(8,128)S(1)}, f32[64,1536]{1,0:T(8,128)S(1)}, u32[]{:S(2)}, u32[]{:S(2)}) collective-permute-start(f32[64,1536]{1,0:T(8,128)S(1)} %get-tuple-element.38), channel_id=1, source_target_pairs={{0,4},{1,5},{2,6},{3,7},{4,0},{5,1},{6,2},{7,3}} | collective-permute-start | bytes 1179656 | tf_op jit(solution)/shard_map/ppermute | solution.py:546
  38.0 9.2 %weight_grads.1 = (f32[4,1024,512]{2,1,0:T(8,128)}, f32[4,1024,512]{2,1,0:T(8,128)}, f32[4,512,1024]{2,1,0:T(8,128)}, bf16[64,1024]{1,0:T(8,128)(2,1)}, f32[8,64]{1,0:T(8,128)}) custom-call(bf16[1024,512]{1,0:T(8,128)(2,1)S(1)} %get-tuple-element.26.xt_ref, bf16[512,1024]{1,0:T(8,128)(2,1)S(1)} %get-tuple-element.27.dy_ref, ...), custom_call_target="tpu_custom_call" | custom-call | flops 6442450944 | bytes 35651584 | tf_op jit(solution)/shard_map/weight_grads/pallas_call | solution.py:504
  47.1 0.0 collective-permute-done.x_ref
  47.2 0.3 collective-permute-done.1.y_ref
  47.5 0.8 %combine.1 = (bf16[64,1024]{1,0:T(8,128)(2,1)}, bf16[64,1024]{1,0:T(8,128)(2,1)}) custom-call(f32[64,1024]{1,0:T(8,128)S(1)} %get-tuple-element.35.dx_ref, f32[64,1024]{1,0:T(8,128)S(1)} %get-tuple-element.36.at_ref, f32[64,1536]{1,0:T(8,128)S(1)} %collective-permute-done.x_ref, f32[64,1536]{1,0:T(8,128)S(1)} %collective-permute-done.1.y_ref), custom_call_target="tpu_custom_call" | custom-call | tf_op jit(solution)/shard_map/combine/pallas_call | solution.py:533
Async XLA Ops:
  35.9 11.2 %collective-permute-start = (f32[64,1536]{1,0:T(8,128)S(1)}, f32[64,1536]{1,0:T(8,128)S(1)}, u32[]{:S(2)}, u32[]{:S(2)}) collective-permute-start(f32[64,1536]{1,0:T(8,128)S(1)} %get-tuple-element.37), channel_id=1, source_target_pairs={{0,2},{1,3},{2,0},{3,1},{4,6},{5,7},{6,4},{7,5}} | collective-permute-start | bytes 1179656 | tf_op jit(solution)/shard_map/ppermute | solution.py:545
  37.0 10.5 %collective-permute-start.1 = (f32[64,1536]{1,0:T(8,128)S(1)}, f32[64,1536]{1,0:T(8,128)S(1)}, u32[]{:S(2)}, u32[]{:S(2)}) collective-permute-start(f32[64,1536]{1,0:T(8,128)S(1)} %get-tuple-element.38), channel_id=1, source_target_pairs={{0,4},{1,5},{2,6},{3,7},{4,0},{5,1},{6,2},{7,3}} | collective-permute-start | bytes 1179656 | tf_op jit(solution)/shard_map/ppermute | solution.py:546
